TPU v7x, 32 devices: a whole 2x2x4 slice. The times are simulated.
32 devices in a mesh: gz: 2 (over x), row: 4 (over y, core), col: 4 (over z).
Axes of the slice: x: 2, y: 2, z: 4, core: 2. Of those that a mesh axis runs over, the one named last changes fastest.
Arguments:
- sections: bfloat16 [4, 2048, 2048], P('gz', 'row', 'col'), may hold values from -6 to 6
- priors: int32 [2, 4, 8, 8], P(None, 'gz', 'row', 'col'), may hold values from -64 to 64
- row_order: int32 [8], replicated, may hold values from 0 to 7, each once
Outputs:
- mesh_flows: float32 [8, 64], P('row')
Inputs may be any that keep to these rules, and one draw needn't show every extreme that they name: A permutation of the patch rows: mesh row m holds patch row row_order[m].
All inputs are finite; a program needn't handle non-finite values.
Results may differ from a plain program's by a relative error of at most 0.0003.
Values may be sent and summed in bfloat16 or wider, within the bound.
No kernel may reach another device: no remote copies, remote signals or barrier semaphores. Data moves between devices by JAX's collectives and lax.ppermute only.
A program may use at most 64 MiB of HBM per device.

v0:
```python
import math

import jax
import jax.numpy as jnp
from jax import lax
from jax.sharding import PartitionSpec as P

PATCH = 512
STRIDE = 256
LAGS = 128
HALO = 256


def with_halo(shard, sides, width):
    for axis, dim in sides:
        devices, length = (lax.axis_size(axis), shard.shape[dim])
        up = [(i, (i + 1) % devices) for i in range(devices - 1)]
        down = [(j, i) for i, j in up]
        last = lax.slice_in_dim(shard, length - width, length, axis=dim)
        first = lax.slice_in_dim(shard, 0, width, axis=dim)
        before = lax.ppermute(last, axis, up)
        after = lax.ppermute(first, axis, down)
        shard = jnp.concatenate([before, shard, after], axis=dim)
    return shard


def shifted(value, axis, steps):
    count = lax.axis_size(axis)
    pairs = [(source, (source + steps) % count) for source in range(count)]
    return lax.ppermute(value, axis, pairs)


def dft_tables(length):
    frequencies = jnp.arange(length, dtype=jnp.int32)
    angles = jnp.mod(frequencies[:, None] * frequencies[None, :], length).astype(jnp.float32) * (
        2.0 * math.pi / length
    )
    cosine = jnp.cos(angles)
    sine_part = jnp.sin(angles)
    minus_table = jnp.concatenate([cosine, -sine_part], axis=1).astype(jnp.bfloat16)
    plus_table = jnp.concatenate([cosine, sine_part], axis=1).astype(jnp.bfloat16)
    return (minus_table, plus_table)


def spectra_of(patches, minus_table, plus_table):
    length = patches.shape[-1]
    row_pass = jnp.einsum(
        "nxy,yk->nxk", patches, minus_table, preferred_element_type=jnp.float32
    ).astype(jnp.bfloat16)
    real_rows = row_pass[:, :, :length]
    imag_rows = row_pass[:, :, length:]
    upper_stack = jnp.concatenate([real_rows, imag_rows], axis=1)
    lower_stack = jnp.concatenate([imag_rows, real_rows], axis=1)
    spec_real = (
        jnp.einsum("kx,nxm->nkm", plus_table, upper_stack, preferred_element_type=jnp.float32)
        / length
    )
    spec_imag = (
        jnp.einsum("kx,nxm->nkm", minus_table, lower_stack, preferred_element_type=jnp.float32)
        / length
    )
    return jnp.stack([spec_real, spec_imag], axis=1).astype(jnp.bfloat16)


def lag_angles(offsets, length):
    frequencies = jnp.arange(length, dtype=jnp.int32)
    shifts = offsets[:, None] + jnp.arange(LAGS, dtype=jnp.int32)[None, :] - LAGS // 2
    angles = jnp.mod(shifts[:, :, None] * frequencies[None, None, :], length).astype(
        jnp.float32
    ) * (2.0 * math.pi / length)
    return (jnp.cos(angles), jnp.sin(angles))


def flows_of(first_spec, second_spec, offsets):
    length = first_spec.shape[-1]
    first_real = first_spec[:, 0].astype(jnp.float32)
    first_imag = first_spec[:, 1].astype(jnp.float32)
    second_real = second_spec[:, 0].astype(jnp.float32)
    second_imag = second_spec[:, 1].astype(jnp.float32)
    prod_real = (first_real * second_real + first_imag * second_imag).astype(jnp.bfloat16)
    prod_imag = (first_real * second_imag - first_imag * second_real).astype(jnp.bfloat16)
    row_cosine, row_sine = lag_angles(offsets[0], length)
    column_cosine, column_sine = lag_angles(offsets[1], length)
    products = jnp.concatenate([prod_real, prod_imag], axis=2)
    column_real = jnp.concatenate([column_cosine, -column_sine], axis=2).astype(jnp.bfloat16)
    column_imag = jnp.concatenate([column_sine, column_cosine], axis=2).astype(jnp.bfloat16)
    half_real = jnp.einsum(
        "nkl,nul->nku", products, column_real, preferred_element_type=jnp.float32
    ).astype(jnp.bfloat16)
    half_imag = jnp.einsum(
        "nkl,nul->nku", products, column_imag, preferred_element_type=jnp.float32
    ).astype(jnp.bfloat16)
    row_table = jnp.concatenate([row_cosine, -row_sine], axis=2).astype(jnp.bfloat16)
    stacked = jnp.concatenate([half_real, half_imag], axis=1)
    surface = (
        jnp.einsum("ntk,nku->ntu", row_table, stacked, preferred_element_type=jnp.float32) / length
    )
    weights = surface * surface
    displacement = (jnp.arange(LAGS, dtype=jnp.int32) - LAGS // 2).astype(jnp.float32)
    weight_sum = 1.0 + jnp.sum(weights, axis=(1, 2))
    row_shift = jnp.sum(weights * displacement[None, :, None], axis=(1, 2)) / weight_sum
    column_shift = jnp.sum(weights * displacement[None, None, :], axis=(1, 2)) / weight_sum
    return jnp.stack(
        [offsets[0].astype(jnp.float32) + row_shift, offsets[1].astype(jnp.float32) + column_shift],
        axis=0,
    )


def body(sections, priors, row_order):
    sec_count = sections.shape[0]
    block_side = sections.shape[1]
    per_side = block_side // STRIDE
    place_count = per_side * per_side
    margin = HALO // 2
    minus_table, plus_table = dft_tables(PATCH)
    offsets_all = jnp.transpose(priors, (2, 3, 0, 1)).reshape(place_count, 2, sec_count)
    positions = jnp.arange(place_count, dtype=jnp.int32)

    def cut_window(extended, position):
        top_edge = position // per_side * STRIDE
        left_edge = position % per_side * STRIDE
        return lax.dynamic_slice(
            extended, (jnp.int32(0), top_edge, left_edge), (extended.shape[0], PATCH, PATCH)
        )

    arrived = shifted(sections[:1], "gz", -1)
    extended = with_halo(
        jnp.concatenate([sections, arrived], axis=0), (("row", 1), ("col", 2)), margin
    )

    def place_flows(inputs):
        position, offsets = inputs
        section_spectra = spectra_of(cut_window(extended, position), minus_table, plus_table)
        return flows_of(section_spectra[:-1], section_spectra[1:], offsets)

    all_flows = lax.map(place_flows, (positions, offsets_all))
    local_table = jnp.transpose(all_flows.reshape(per_side, per_side, 2, sec_count), (2, 3, 0, 1))
    flat_flows = local_table.reshape(1, 2 * sec_count * place_count)
    gathered = lax.all_gather(flat_flows, ("gz", "row", "col"), axis=0, tiled=True)
    size_gz = lax.axis_size("gz")
    size_row = lax.axis_size("row")
    size_col = lax.axis_size("col")
    whole_grid = gathered.reshape(size_gz, size_row, size_col, 2, sec_count, per_side, per_side)
    whole_grid = jnp.transpose(whole_grid, (3, 0, 4, 1, 5, 2, 6)).reshape(
        2, size_gz * sec_count, size_row * per_side, size_col * per_side
    )
    rows_each = row_order.shape[0] // size_row
    owned = lax.dynamic_slice_in_dim(row_order, lax.axis_index("row") * rows_each, rows_each)
    selector = (owned[:, None] == jnp.arange(row_order.shape[0], dtype=jnp.int32)[None, :]).astype(
        jnp.float32
    )
    picked = jnp.einsum("jr,csrk->jcsk", selector, whole_grid, precision=lax.Precision.HIGHEST)
    return picked.reshape(rows_each, 2 * size_gz * sec_count * size_col * per_side)


def solution(mesh):
    placed = (P("gz", "row", "col"), P(None, "gz", "row", "col"), P())
    return jax.shard_map(
        body, mesh=mesh, in_specs=placed, out_specs=P("row", None), check_vma=False
    )
```

profile of v0, /device:TPU:0, one launch (start us, length us, event | category | flops | bytes accessed | tf_op | source)
XLA Modules:
  0.0 189.6 jit_solution(16648246001251315316)
XLA Ops:
  1.1 3.0 %collective-permute-start = (bf16[1,512,512]{2,1,0:T(8,128)(2,1)S(1)}, bf16[1,512,512]{2,1,0:T(8,128)(2,1)S(1)}, u32[]{:S(2)}, u32[]{:S(2)}) collective-permute-start(bf16[1,512,512]{2,1,0:T(8,128)(2,1)S(1)} %slice.97), channel_id=1, source_target_pairs={{0,16},{16,0},{1,17},{17,1},{2,18},{18,2},{3,19},{19,3},{4,20},{20... | collective-permute-start | bytes 1572872 | tf_op jit(solution)/shard_map/ppermute | solution.py:30
  4.1 1.3 constant_dynamic-update-slice_fusion.1
  5.4 10.6 %collective-permute-done = bf16[1,512,512]{2,1,0:T(8,128)(2,1)S(1)} collective-permute-done((bf16[1,512,512]{2,1,0:T(8,128)(2,1)S(1)}, bf16[1,512,512]{2,1,0:T(8,128)(2,1)S(1)}, u32[]{:S(2)}, u32[]{:S(2)}) %collective-permute-start) | collective-permute-done | bytes 524320 | tf_op jit(solution)/shard_map/ppermute | solution.py:30
  16.2 1.3 collective-permute-start.1
  18.8 4.3 %collective-permute-done.2 = bf16[3,128,512]{2,1,0:T(8,128)(2,1)S(1)} collective-permute-done((bf16[3,128,512]{2,1,0:T(8,128)(2,1)S(1)}, bf16[3,128,512]{2,1,0:T(8,128)(2,1)S(1)}, u32[]{:S(2)}, u32[]{:S(2)}) %collective-permute-start.2) | collective-permute-done | bytes 393248 | tf_op jit(solution)/shard_map/ppermute | solution.py:22
  24.3 4.3 %collective-permute-start.3 = (bf16[3,768,128]{2,1,0:T(8,128)(2,1)}, bf16[3,768,128]{2,1,0:T(8,128)(2,1)}, u32[]{:S(2)}, u32[]{:S(2)}) collective-permute-start(bf16[3,768,128]{2,1,0:T(8,128)(2,1)} %get-tuple-element.187), channel_id=1, source_target_pairs={{0,1},{1,2},{2,3},{4,5},{5,6},{6,7},{8,9},{9,10},{10,11},{12,13},{... | collective-permute-start | bytes 1769480 | tf_op jit(solution)/shard_map/ppermute | solution.py:21
  30.2 4.0 %fusion.71 = bf16[512,512]{1,0:T(8,128)(2,1)S(1)} fusion(), kind=kLoop, calls=%fused_computation.104 | loop fusion | flops 3932160 | bytes 524288 | tf_op jit(solution)/shard_map/convert.13
  34.1 4.3 %negate_convert_fusion.2 = (bf16[512,512]{1,0:T(8,128)(2,1)S(1)}, bf16[512,512]{1,0:T(8,128)(2,1)S(1)}) fusion(), kind=kLoop, calls=%fused_computation.95 | loop fusion | flops 4456448 | bytes 1048576 | tf_op jit(solution)/shard_map/convert.15
  39.7 2.6 %collective-permute-done.4 = bf16[3,768,128]{2,1,0:T(8,128)(2,1)} collective-permute-done((bf16[3,768,128]{2,1,0:T(8,128)(2,1)}, bf16[3,768,128]{2,1,0:T(8,128)(2,1)}, u32[]{:S(2)}, u32[]{:S(2)}) %collective-permute-start.4) | collective-permute-done | bytes 589856 | tf_op jit(solution)/shard_map/ppermute | solution.py:22
  42.3 4.3 %pad_maximum_fusion.7 = bf16[3,768,768]{2,1,0:T(8,128)(2,1)} fusion(bf16[3,768,128]{2,1,0:T(8,128)(2,1)} %collective-permute-done.4, bf16[3,128,512]{2,1,0:T(8,128)(2,1)S(1)} %collective-permute-done.2, bf16[3,512,512]{2,1,0:T(8,128)(2,1)S(1)} %constant_dynamic-update-slice_fusion, bf16[3,128,512]{2,1,0:T(8,128)(2,1)S(1)} %collective-permute-done.1, ...), kind=kLoop, calls=%fused_computation.86 | loop fusion | flops 17694720 | bytes 7077888 | tf_op jit(solution)/shard_map/concatenate | solution.py:23
  46.7 75.7 %while.13 = (s32[]{:T(128)}, f32[4,2,2]{2,1,0:T(2,128)S(1)}, s32[4,2,2]{2,1,0:T(2,128)S(1)}, s32[4]{0:T(128)S(1)}, bf16[3,768,768]{2,1,0:T(8,128)(2,1)}, /*index...) while((s32[]{:T(128)}, f32[4,2,2]{2,1,0:T(2,128)S(1)}, ...), condition=%wide.region_4.5_spmd, body=%wide.region_0.4_spmd.sunk | while | flops 5477073920 | bytes 42212972 | solution.py:136
  49.8 3.5 %convolution_convert_fusion.2 = bf16[3,512,1024]{2,1,0:T(8,128)(2,1)S(1)} fusion(bf16[3,768,768]{2,1,0:T(8,128)(2,1)} %get-tuple-element.304, s32[]{:T(128)S(6)} %select_n.116, s32[]{:T(128)S(6)} %select_n.118, bf16[512,1024]{1,0:T(8,128)(2,1)} %get-tuple-element.305), kind=kOutput, calls=%fused_computation.14.clone.1 | convolution fusion | flops 1612185600 | bytes 5767176 | tf_op jit(solution)/shard_map/while/body/eval_jaxpr/nxy,yk->nxk/dot_general | solution.py:47
  53.6 1.9 fusion.104
  55.5 1.9 fusion.103
  58.3 2.5 %negate_convert_fusion.4 = (bf16[2,128,512]{2,1,0:T(8,128)(2,1)S(1)}, bf16[2,128,512]{2,1,0:T(8,128)(2,1)S(1)}, bf16[2,128,512]{2,1,0:T(8,128)(2,1)S(1)}) fusion(s32[2,128]{1,0:T(2,128)S(1)} %get-tuple-element.262), kind=kLoop, calls=%fused_computation.56.clone.1 | loop fusion | flops 2359296 | bytes 787456 | tf_op jit(solution)/shard_map/convert.3
  62.7 2.5 %cosine_convert_fusion.4 = (bf16[2,128,512]{2,1,0:T(8,128)(2,1)S(1)}, bf16[2,128,512]{2,1,0:T(8,128)(2,1)S(1)}) fusion(s32[2,128]{1,0:T(2,128)S(1)} %get-tuple-element.266), kind=kLoop, calls=%fused_computation.61.clone.1 | loop fusion | flops 2228224 | bytes 525312 | tf_op jit(solution)/shard_map/convert.10
  68.7 3.5 %convolution_convert_fusion.2 = bf16[3,512,1024]{2,1,0:T(8,128)(2,1)S(1)} fusion(bf16[3,768,768]{2,1,0:T(8,128)(2,1)} %get-tuple-element.304, s32[]{:T(128)S(6)} %select_n.116, s32[]{:T(128)S(6)} %select_n.118, bf16[512,1024]{1,0:T(8,128)(2,1)} %get-tuple-element.305), kind=kOutput, calls=%fused_computation.14.clone.1 | convolution fusion | flops 1612185600 | bytes 5767176 | tf_op jit(solution)/shard_map/while/body/eval_jaxpr/nxy,yk->nxk/dot_general | solution.py:47
  72.6 1.9 fusion.104
  74.5 1.9 fusion.103
  77.2 2.5 %negate_convert_fusion.4 = (bf16[2,128,512]{2,1,0:T(8,128)(2,1)S(1)}, bf16[2,128,512]{2,1,0:T(8,128)(2,1)S(1)}, bf16[2,128,512]{2,1,0:T(8,128)(2,1)S(1)}) fusion(s32[2,128]{1,0:T(2,128)S(1)} %get-tuple-element.262), kind=kLoop, calls=%fused_computation.56.clone.1 | loop fusion | flops 2359296 | bytes 787456 | tf_op jit(solution)/shard_map/convert.3
  81.6 2.5 %cosine_convert_fusion.4 = (bf16[2,128,512]{2,1,0:T(8,128)(2,1)S(1)}, bf16[2,128,512]{2,1,0:T(8,128)(2,1)S(1)}) fusion(s32[2,128]{1,0:T(2,128)S(1)} %get-tuple-element.266), kind=kLoop, calls=%fused_computation.61.clone.1 | loop fusion | flops 2228224 | bytes 525312 | tf_op jit(solution)/shard_map/convert.10
  87.7 3.5 %convolution_convert_fusion.2 = bf16[3,512,1024]{2,1,0:T(8,128)(2,1)S(1)} fusion(bf16[3,768,768]{2,1,0:T(8,128)(2,1)} %get-tuple-element.304, s32[]{:T(128)S(6)} %select_n.116, s32[]{:T(128)S(6)} %select_n.118, bf16[512,1024]{1,0:T(8,128)(2,1)} %get-tuple-element.305), kind=kOutput, calls=%fused_computation.14.clone.1 | convolution fusion | flops 1612185600 | bytes 5767176 | tf_op jit(solution)/shard_map/while/body/eval_jaxpr/nxy,yk->nxk/dot_general | solution.py:47
  91.5 1.9 fusion.104
  93.4 1.9 fusion.103
  96.2 2.5 %negate_convert_fusion.4 = (bf16[2,128,512]{2,1,0:T(8,128)(2,1)S(1)}, bf16[2,128,512]{2,1,0:T(8,128)(2,1)S(1)}, bf16[2,128,512]{2,1,0:T(8,128)(2,1)S(1)}) fusion(s32[2,128]{1,0:T(2,128)S(1)} %get-tuple-element.262), kind=kLoop, calls=%fused_computation.56.clone.1 | loop fusion | flops 2359296 | bytes 787456 | tf_op jit(solution)/shard_map/convert.3
  100.5 2.5 %cosine_convert_fusion.4 = (bf16[2,128,512]{2,1,0:T(8,128)(2,1)S(1)}, bf16[2,128,512]{2,1,0:T(8,128)(2,1)S(1)}) fusion(s32[2,128]{1,0:T(2,128)S(1)} %get-tuple-element.266), kind=kLoop, calls=%fused_computation.61.clone.1 | loop fusion | flops 2228224 | bytes 525312 | tf_op jit(solution)/shard_map/convert.10
  106.6 3.5 %convolution_convert_fusion.2 = bf16[3,512,1024]{2,1,0:T(8,128)(2,1)S(1)} fusion(bf16[3,768,768]{2,1,0:T(8,128)(2,1)} %get-tuple-element.304, s32[]{:T(128)S(6)} %select_n.116, s32[]{:T(128)S(6)} %select_n.118, bf16[512,1024]{1,0:T(8,128)(2,1)} %get-tuple-element.305), kind=kOutput, calls=%fused_computation.14.clone.1 | convolution fusion | flops 1612185600 | bytes 5767176 | tf_op jit(solution)/shard_map/while/body/eval_jaxpr/nxy,yk->nxk/dot_general | solution.py:47
  110.4 1.9 fusion.104
  112.3 1.9 fusion.103
  115.1 2.5 %negate_convert_fusion.4 = (bf16[2,128,512]{2,1,0:T(8,128)(2,1)S(1)}, bf16[2,128,512]{2,1,0:T(8,128)(2,1)S(1)}, bf16[2,128,512]{2,1,0:T(8,128)(2,1)S(1)}) fusion(s32[2,128]{1,0:T(2,128)S(1)} %get-tuple-element.262), kind=kLoop, calls=%fused_computation.56.clone.1 | loop fusion | flops 2359296 | bytes 787456 | tf_op jit(solution)/shard_map/convert.3
  119.5 2.5 %cosine_convert_fusion.4 = (bf16[2,128,512]{2,1,0:T(8,128)(2,1)S(1)}, bf16[2,128,512]{2,1,0:T(8,128)(2,1)S(1)}) fusion(s32[2,128]{1,0:T(2,128)S(1)} %get-tuple-element.266), kind=kLoop, calls=%fused_computation.61.clone.1 | loop fusion | flops 2228224 | bytes 525312 | tf_op jit(solution)/shard_map/convert.10
  122.6 65.3 %all-gather = f32[32,1,16]{2,1,0:T(1,128)S(1)} all-gather(f32[1,1,16]{2,1,0:T(1,128)S(1)} %reshape.208), channel_id=1, replica_groups=mesh['gz'=2,'row'=4,'col'=4] {'gz','row','col'}, dimensions={0}, use_global_device_ids=true | all-gather | bytes 2112 | tf_op jit(solution)/shard_map/all_gather | solution.py:139
  (82 shorter events, 24.6 us)
Async XLA Ops:
  1.1 15.0 %collective-permute-start = (bf16[1,512,512]{2,1,0:T(8,128)(2,1)S(1)}, bf16[1,512,512]{2,1,0:T(8,128)(2,1)S(1)}, u32[]{:S(2)}, u32[]{:S(2)}) collective-permute-start(bf16[1,512,512]{2,1,0:T(8,128)(2,1)S(1)} %slice.97), channel_id=1, source_target_pairs={{0,16},{16,0},{1,17},{17,1},{2,18},{18,2},{3,19},{19,3},{4,20},{20... | collective-permute-start | bytes 1572872 | tf_op jit(solution)/shard_map/ppermute | solution.py:30
  16.1 13.8 %copy-start.1 = (s32[2,2,2,2]{3,2,1,0:T(2,128)S(1)}, s32[2,2,2,2]{3,2,1,0:T(2,128)}, u32[]{:S(2)}) copy-start(s32[2,2,2,2]{3,2,1,0:T(2,128)} %param.6) | copy-start | bytes 196
  16.1 13.9 %copy-start.2 = (s32[8]{0:T(128)S(1)}, s32[8]{0:T(128)}, u32[]{:S(2)}) copy-start(s32[8]{0:T(128)} %param.7) | copy-start | bytes 100
  16.2 2.6 %collective-permute-start.1 = (bf16[3,128,512]{2,1,0:T(8,128)(2,1)S(1)}, bf16[3,128,512]{2,1,0:T(8,128)(2,1)S(1)}, u32[]{:S(2)}, u32[]{:S(2)}) collective-permute-start(bf16[3,128,512]{2,1,0:T(8,128)(2,1)S(1)} %get-tuple-element.189), channel_id=1, source_target_pairs={{0,4},{4,8},{8,12},{1,5},{5,9},{9,13},{2,6},{6,10},{10,14},{3,7},{... | collective-permute-start | bytes 1179656 | tf_op jit(solution)/shard_map/ppermute | solution.py:21
  17.5 5.6 %collective-permute-start.2 = (bf16[3,128,512]{2,1,0:T(8,128)(2,1)S(1)}, bf16[3,128,512]{2,1,0:T(8,128)(2,1)S(1)}, u32[]{:S(2)}, u32[]{:S(2)}) collective-permute-start(bf16[3,128,512]{2,1,0:T(8,128)(2,1)S(1)} %get-tuple-element.190), channel_id=1, source_target_pairs={{4,0},{8,4},{12,8},{5,1},{9,5},{13,9},{6,2},{10,6},{14,10},{7,3},{... | collective-permute-start | bytes 1179656 | tf_op jit(solution)/shard_map/ppermute | solution.py:22
  24.3 15.4 %collective-permute-start.3 = (bf16[3,768,128]{2,1,0:T(8,128)(2,1)}, bf16[3,768,128]{2,1,0:T(8,128)(2,1)}, u32[]{:S(2)}, u32[]{:S(2)}) collective-permute-start(bf16[3,768,128]{2,1,0:T(8,128)(2,1)} %get-tuple-element.187), channel_id=1, source_target_pairs={{0,1},{1,2},{2,3},{4,5},{5,6},{6,7},{8,9},{9,10},{10,11},{12,13},{... | collective-permute-start | bytes 1769480 | tf_op jit(solution)/shard_map/ppermute | solution.py:21
  28.7 13.7 %collective-permute-start.4 = (bf16[3,768,128]{2,1,0:T(8,128)(2,1)}, bf16[3,768,128]{2,1,0:T(8,128)(2,1)}, u32[]{:S(2)}, u32[]{:S(2)}) collective-permute-start(bf16[3,768,128]{2,1,0:T(8,128)(2,1)} %get-tuple-element.188), channel_id=1, source_target_pairs={{1,0},{2,1},{3,2},{5,4},{6,5},{7,6},{9,8},{10,9},{11,10},{13,12},{... | collective-permute-start | bytes 1769480 | tf_op jit(solution)/shard_map/ppermute | solution.py:22
  53.6 1.9 %copy-start = (bf16[512,1024]{1,0:T(8,128)(2,1)S(1)}, bf16[512,1024]{1,0:T(8,128)(2,1)}, u32[]{:S(2)}) copy-start(bf16[512,1024]{1,0:T(8,128)(2,1)} %get-tuple-element.305) | copy-start | bytes 3145732 | tf_op jit(solution)/shard_map/while
  72.6 1.9 %copy-start = (bf16[512,1024]{1,0:T(8,128)(2,1)S(1)}, bf16[512,1024]{1,0:T(8,128)(2,1)}, u32[]{:S(2)}) copy-start(bf16[512,1024]{1,0:T(8,128)(2,1)} %get-tuple-element.305) | copy-start | bytes 3145732 | tf_op jit(solution)/shard_map/while
  91.5 1.9 %copy-start = (bf16[512,1024]{1,0:T(8,128)(2,1)S(1)}, bf16[512,1024]{1,0:T(8,128)(2,1)}, u32[]{:S(2)}) copy-start(bf16[512,1024]{1,0:T(8,128)(2,1)} %get-tuple-element.305) | copy-start | bytes 3145732 | tf_op jit(solution)/shard_map/while
  110.4 1.9 %copy-start = (bf16[512,1024]{1,0:T(8,128)(2,1)S(1)}, bf16[512,1024]{1,0:T(8,128)(2,1)}, u32[]{:S(2)}) copy-start(bf16[512,1024]{1,0:T(8,128)(2,1)} %get-tuple-element.305) | copy-start | bytes 3145732 | tf_op jit(solution)/shard_map/while
where the time goes:
time: 190 us
  blocking collectives  65.3 us (34%)
  matrix products  39 us (21%)
  other arithmetic  38.4 us (20%)
  waiting for transfers between devices  17.5 us (9%)
  starting transfers between devices  11.3 us (6%)
  loops' own time  10.6 us (6%)
  local copies, waits for them, and re-layouts  7.37 us (4%)
    all_gather x1, blocking collectives, body(): lax.all_gather(flat_flows, ('gz', 'row', 'col'), axis=0, tiled=True)  65.3 us
    another operation x11, other arithmetic  28 us
    dot_general x4, matrix products, spectra_of(): jnp.einsum('nxy,yk->nxk', patches, minus_table, preferred_element_type=jn...  14.1 us
    ppermute x1, waiting for transfers between devices, shifted(): return lax.ppermute(value, axis, pairs)  10.6 us
    another operation x1, loops' own time, body(): all_flows = lax.map(place_flows, (positions, offsets_all))  10.6 us
    dot_general x4, matrix products, spectra_of(): jnp.einsum('kx,nxm->nkm', minus_table, lower_stack, preferred_element_typ...  7.51 us
    dot_general x4, matrix products, spectra_of(): jnp.einsum('kx,nxm->nkm', plus_table, upper_stack, preferred_element_type...  7.51 us
    ppermute x2, waiting for transfers between devices, with_halo(): after = lax.ppermute(first, axis, down)  6.89 us
  transfers between devices with their start and end apart: 5, of which 3 were waited for; matrix products, arithmetic and copies ran while one was open for 6% of the time, Pallas kernels for 0%

commit v1 on v0

v1 whole, which is shorter than its diff:
```python
import functools
import math

import jax
import jax.numpy as jnp
import numpy as np
from jax import lax
from jax.experimental import pallas as pl
from jax.experimental.pallas import tpu as pltpu
from jax.sharding import PartitionSpec as P

PATCH = 512
STRIDE = 256
LAGS = 128
MAXOFF = 64
HALO = 256
HALF = PATCH // 2
MARGIN = HALO // 2
AXES = ("gz", "row", "col")


def frequency_tables():
    frequencies = np.arange(HALF)[:, None]
    places = np.arange(PATCH)[None, :]
    step = 2.0 * math.pi / PATCH
    cosine = np.cos(np.mod(frequencies * places, PATCH) * step)
    sine_part = np.sin(np.mod(frequencies * places, PATCH) * step)
    sine_part[0] = np.cos(np.mod(HALF * places[0], PATCH) * step)
    table = np.concatenate([cosine, sine_part], axis=0)
    lags = np.arange(-MAXOFF - LAGS // 2, MAXOFF + LAGS // 2) % PATCH
    return table.astype(np.float32), table.T[lags].astype(np.float32)


def neighbours(value, axis, dim, width):
    devices, length = (lax.axis_size(axis), value.shape[dim])
    up = [(i, i + 1) for i in range(devices - 1)]
    down = [(j, i) for i, j in up]
    last = lax.slice_in_dim(value, length - width, length, axis=dim)
    first = lax.slice_in_dim(value, 0, width, axis=dim)
    return lax.ppermute(last, axis, up), lax.ppermute(first, axis, down)


def split_parts(spec_ref, out_ref):
    for rows, cols in ((slice(0, 16), slice(0, HALF)), (slice(16, HALF), slice(0, 128)), (slice(16, HALF), slice(128, HALF))):
        low_r = slice(rows.start + HALF, rows.stop + HALF)
        low_c = slice(cols.start + HALF, cols.stop + HALF)
        cc = spec_ref[rows, cols]
        cs = spec_ref[rows, low_c]
        sc = spec_ref[low_r, cols]
        ss = spec_ref[low_r, low_c]
        a, b, c, d = cc - ss, sc + cs, cc + ss, sc - cs
        if cols.start == 0:
            edge = lax.broadcasted_iota(jnp.int32, cc.shape, 1) == 0
            a, b, c, d = jnp.where(edge, cc, a), jnp.where(edge, sc, b), jnp.where(edge, cs, c), jnp.where(edge, ss, d)
        if rows.start == 0:
            edge = lax.broadcasted_iota(jnp.int32, cc.shape, 0) == 0
            a, b, c, d = jnp.where(edge, cc, a), jnp.where(edge, cs, b), jnp.where(edge, sc, c), jnp.where(edge, ss, d)
        out_ref[0, rows, cols] = a.astype(out_ref.dtype)
        out_ref[1, rows, cols] = b.astype(out_ref.dtype)
        out_ref[2, rows, cols] = c.astype(out_ref.dtype)
        out_ref[3, rows, cols] = d.astype(out_ref.dtype)


def cross_parts(first_ref, second_ref, out_ref):
    for rows, cols in ((slice(0, 16), slice(0, HALF)), (slice(16, HALF), slice(0, 128)), (slice(16, HALF), slice(128, HALF))):
        low_r = slice(rows.start + HALF, rows.stop + HALF)
        low_c = slice(cols.start + HALF, cols.stop + HALF)
        a, b, c, d = (first_ref[n, rows, cols].astype(jnp.float32) for n in range(4))
        e, f, g, h = (second_ref[n, rows, cols].astype(jnp.float32) for n in range(4))
        p, u = a * e + b * f, a * f - b * e
        q, v = c * g + d * h, c * h - d * g
        cc, cs, sc, ss = p + q, u - v, u + v, q - p
        if cols.start == 0:
            edge = lax.broadcasted_iota(jnp.int32, cc.shape, 1) == 0
            cc, cs, sc, ss = jnp.where(edge, p, cc), jnp.where(edge, q, cs), jnp.where(edge, u, sc), jnp.where(edge, v, ss)
        if rows.start == 0:
            row = lax.broadcasted_iota(jnp.int32, cc.shape, 0) == 0
            cc, cs, sc, ss = jnp.where(row, p, cc), jnp.where(row, u, cs), jnp.where(row, q, sc), jnp.where(row, v, ss)
            corner = jnp.logical_and(row, lax.broadcasted_iota(jnp.int32, cc.shape, 1) == 0)
            cc, cs = jnp.where(corner, 0.5 * (a * e), cc), jnp.where(corner, 0.5 * (b * f), cs)
            sc, ss = jnp.where(corner, 0.5 * (c * g), sc), jnp.where(corner, 0.5 * (d * h), ss)
        out_ref[rows, cols] = cc.astype(jnp.bfloat16)
        out_ref[rows, low_c] = cs.astype(jnp.bfloat16)
        out_ref[low_r, cols] = sc.astype(jnp.bfloat16)
        out_ref[low_r, low_c] = ss.astype(jnp.bfloat16)


def lag_rows(lag_ref, offset):
    pieces = [lag_ref[n, pl.ds(offset + MAXOFF, LAGS), :] for n in range(lag_ref.shape[0])]
    return jnp.concatenate(pieces, axis=1).astype(jnp.bfloat16)


def match_kernel(
    meta_ref, table_ref, turned_ref, lag_ref, own_ref, arrived_ref, left_ref, right_ref, above_ref, below_ref,
    out_ref, ext_ref, rows_ref, spec_ref, part_ref, cross_ref, *, sizes,
):
    size_gz, size_row, size_col, sec_count, per_side = sizes
    side = per_side * STRIDE
    top, wide = side + MARGIN, side + HALO
    place_count = per_side * per_side
    for s in range(sec_count + 1):
        center = own_ref[s] if s < sec_count else arrived_ref[0]
        ext_ref[0:MARGIN, :] = above_ref[s]
        ext_ref[MARGIN:top, 0:MARGIN] = left_ref[s]
        ext_ref[MARGIN:top, MARGIN:top] = center
        ext_ref[MARGIN:top, top:wide] = right_ref[s]
        ext_ref[top:wide, :] = below_ref[s]
        for pj in range(per_side):
            rows_ref[...] = jnp.dot(
                ext_ref[:, pj * STRIDE : pj * STRIDE + PATCH], turned_ref[...], preferred_element_type=jnp.float32
            ).astype(jnp.bfloat16)
            for pi in range(per_side):
                spec_ref[...] = jnp.dot(
                    table_ref[...], rows_ref[pi * STRIDE : pi * STRIDE + PATCH, :], preferred_element_type=jnp.float32
                )
                split_parts(spec_ref, part_ref.at[s, pi * per_side + pj])

    lanes_each = 2 * size_gz * sec_count * size_col * per_side
    row_count = size_row * per_side
    rows_each = row_count // size_row
    shape = (size_row, rows_each * lanes_each)
    holder = lax.broadcasted_iota(jnp.int32, shape, 0)
    lane = lax.broadcasted_iota(jnp.int32, shape, 1)
    slot = jnp.zeros(shape, jnp.int32)
    head = 3 + 2 * sec_count * place_count
    for m in range(row_count):
        here = jnp.logical_and(holder == m // rows_each, lane // lanes_each == m % rows_each)
        slot = jnp.where(here, meta_ref[head + m], slot)
    lane = lane % lanes_each
    my_gz, my_row, my_col = meta_ref[0], meta_ref[1], meta_ref[2]
    total_out = jnp.zeros(shape, jnp.float32)
    scale = 2.0 / float(PATCH) ** 3
    down = (lax.broadcasted_iota(jnp.int32, (LAGS, LAGS), 0) - LAGS // 2).astype(jnp.float32)
    across = (lax.broadcasted_iota(jnp.int32, (LAGS, LAGS), 1) - LAGS // 2).astype(jnp.float32)
    for s in range(sec_count):
        for n in range(place_count):
            pi, pj = n // per_side, n % per_side
            cross_parts(part_ref.at[s, n], part_ref.at[s + 1, n], cross_ref)
            p = meta_ref[3 + s * place_count + n]
            q = meta_ref[3 + (sec_count + s) * place_count + n]
            row_lags = lag_rows(lag_ref, p)
            col_lags = lag_rows(lag_ref, q)
            half = lax.dot_general(
                cross_ref[...], col_lags, (((1,), (1,)), ((), ())), preferred_element_type=jnp.float32
            ).astype(jnp.bfloat16)
            surface = jnp.dot(row_lags, half, preferred_element_type=jnp.float32) * scale
            weights = surface * surface
            total = 1.0 + jnp.sum(weights, keepdims=True)
            shift_r = jnp.sum(weights * down, keepdims=True) / total
            shift_c = jnp.sum(weights * across, keepdims=True) / total
            mine = slot == my_row * per_side + pi
            place = (my_gz * sec_count + s) * (size_col * per_side) + my_col * per_side + pj
            half_lanes = lanes_each // 2
            total_out += jnp.where(jnp.logical_and(mine, lane == place), p.astype(jnp.float32) + shift_r, 0.0)
            total_out += jnp.where(jnp.logical_and(mine, lane == place + half_lanes), q.astype(jnp.float32) + shift_c, 0.0)
    for g in range(size_gz):
        for r in range(size_row):
            out_ref[(g * size_row + r) * size_col : (g * size_row + r + 1) * size_col, :] = jnp.broadcast_to(
                total_out[r : r + 1, :], (size_col, shape[1])
            )


def body(sections, priors, row_order):
    sec_count, side = sections.shape[:2]
    per_side = side // STRIDE
    size_gz, size_row, size_col = (lax.axis_size(a) for a in AXES)
    table, lag_table = frequency_tables()
    table = jnp.asarray(table).astype(jnp.bfloat16)
    turned = jnp.asarray(frequency_tables()[0].T).astype(jnp.bfloat16)
    lag_table = jnp.asarray(np.stack(np.split(lag_table, PATCH // 128, axis=1))).astype(jnp.bfloat16).astype(jnp.float32)
    arrived = lax.ppermute(sections[:1], "gz", [(i, (i - 1) % size_gz) for i in range(size_gz)])
    all_sections = jnp.concatenate([sections, arrived], axis=0)
    left, right = neighbours(all_sections, "col", 2, MARGIN)
    def edge_rows(a, b):
        return jnp.concatenate([left[:, a:b], all_sections[:, a:b], right[:, a:b]], axis=2)
    up = [(i, i + 1) for i in range(size_row - 1)]
    above = lax.ppermute(edge_rows(side - MARGIN, side), "row", up)
    below = lax.ppermute(edge_rows(0, MARGIN), "row", [(j, i) for i, j in up])
    meta = jnp.concatenate(
        [jnp.stack([lax.axis_index(a) for a in AXES]).astype(jnp.int32), priors.reshape(-1), row_order]
    )
    lanes = (row_order.shape[0] // size_row) * 2 * size_gz * sec_count * size_col * per_side
    devices = size_gz * size_row * size_col
    wide = side + HALO
    sizes = (size_gz, size_row, size_col, sec_count, per_side)
    vmem = pl.BlockSpec(memory_space=pltpu.VMEM)
    sent = pl.pallas_call(
        functools.partial(match_kernel, sizes=sizes),
        out_shape=jax.ShapeDtypeStruct((devices, lanes), jnp.float32),
        in_specs=[pl.BlockSpec(memory_space=pltpu.SMEM)] + [vmem] * 9,
        out_specs=vmem,
        scratch_shapes=[
            pltpu.VMEM((wide, wide), jnp.bfloat16),
            pltpu.VMEM((wide, PATCH), jnp.bfloat16),
            pltpu.VMEM((PATCH, PATCH), jnp.float32),
            pltpu.VMEM((sec_count + 1, per_side * per_side, 4, HALF, HALF), jnp.float32),
            pltpu.VMEM((PATCH, PATCH), jnp.bfloat16),
        ],
        name="match",
    )(meta, table, turned, lag_table, sections, arrived, left, right, above, below)
    received = lax.all_to_all(sent, AXES, 0, 0, tiled=True)
    return jnp.sum(received, axis=0).reshape(row_order.shape[0] // size_row, -1)


def solution(mesh):
    placed = (P("gz", "row", "col"), P(None, "gz", "row", "col"), P())
    return jax.shard_map(body, mesh=mesh, in_specs=placed, out_specs=P("row", None), check_vma=False)
```

time: 190 us -> 73.5 us (0.39)
  blocking collectives: 65.3 us -> 20.4 us
  matrix products: 39 us -> 0 us
  other arithmetic: 38.4 us -> 0.17 us
  Pallas kernels: 0 us -> 13.8 us
  loops' own time: 10.6 us -> 0 us
  waiting for transfers between devices: 17.5 us -> 22.8 us
  local copies, waits for them, and re-layouts: 7.37 us -> 4.35 us
    all_gather x1 -> x0, blocking collectives: 65.3 us -> none  [body(): lax.all_gather(flat_flows, ('gz', 'row', 'col'), axis=0, tiled=True)]
    dot_general x25 -> x0, matrix products: 39 us -> none  [the longest x4 14.1 us: spectra_of(): jnp.einsum('nxy,yk->nxk', patches, minus_table, preferred_element_type=jn...]
    another operation x11 -> x0, other arithmetic: 28 us -> none
    all_to_all x0 -> x1, blocking collectives: none -> 20.4 us  [body(): received = lax.all_to_all(sent, AXES, 0, 0, tiled=True)]
    pallas_call x0 -> x1, Pallas kernels: none -> 13.8 us  [body(): pl.pallas_call(functools.partial(match_kernel, sizes=sizes), out_shape=ja...]
    another operation x1 -> x0, loops' own time: 10.6 us -> none  [body(): all_flows = lax.map(place_flows, (positions, offsets_all))]
    concatenate x2, other arithmetic: 5.6 us -> 0.12 us  [edge_rows(): jnp.concatenate([left[:, a:b], all_sections[:, a:b], right[:, a:b]], axis=2)]
    ppermute x5, waiting for transfers between devices: 17.5 us -> 22.8 us  [the longest x1 11.8 us: body(): lax.ppermute(sections[:1], 'gz', [(i, (i - 1) % size_gz) for i in range(s...]
  transfers between devices with their start and end apart: 5 -> 5, of which waited for: 3 -> 4; matrix products, arithmetic and copies ran while one was open for 6% -> 1% of each run, Pallas kernels for 0% -> 0%
where the time goes in v1:
time: 73.5 us; the launch traced here: 73.2 us
  waiting for transfers between devices  22.8 us (31%)
  blocking collectives  20.4 us (28%)
  Pallas kernels  13.8 us (19%)
  starting transfers between devices  11.6 us (16%)
  local copies, waits for them, and re-layouts  4.35 us (6%)
    all_to_all x1, blocking collectives, body(): received = lax.all_to_all(sent, AXES, 0, 0, tiled=True)  20.4 us
    pallas_call x1, Pallas kernels, body(): pl.pallas_call(functools.partial(match_kernel, sizes=sizes), out_shape=ja...  13.8 us
    ppermute x1, waiting for transfers between devices, body(): lax.ppermute(sections[:1], 'gz', [(i, (i - 1) % size_gz) for i in range(s...  11.8 us
    ppermute x2, waiting for transfers between devices, neighbours(): return (lax.ppermute(last, axis, up), lax.ppermute(first, axis, down))  7.39 us
    ppermute x2, starting transfers between devices, neighbours(): return (lax.ppermute(last, axis, up), lax.ppermute(first, axis, down))  5.85 us
    ppermute x1, waiting for transfers between devices, body(): below = lax.ppermute(edge_rows(0, MARGIN), 'row', [(j, i) for i, j in up])  3.51 us
    ppermute x1, starting transfers between devices, body(): lax.ppermute(sections[:1], 'gz', [(i, (i - 1) % size_gz) for i in range(s...  3.03 us
    unnamed x17, local copies, waits for them, and re-layouts  1.53 us
  transfers between devices with their start and end apart: 5, of which 4 were waited for; matrix products, arithmetic and copies ran while one was open for 1% of the time, Pallas kernels for 0%

profile of v1, /device:TPU:0, one launch (start us, length us, event | category | flops | bytes accessed | tf_op | source)
XLA Modules:
  0.0 73.2 jit_solution(1775775646783621430)
XLA Ops:
  0.0 1.2 %slice.27 = bf16[1,512,512]{2,1,0:T(8,128)(2,1)S(1)} slice(bf16[2,512,512]{2,1,0:T(8,128)(2,1)} %own_ref.1), slice={[0:1], [0:512], [0:512]} | slice | bytes 1048576 | tf_op jit(solution)/shard_map/slice | solution.py:171
  1.2 3.0 %collective-permute-start = (bf16[1,512,512]{2,1,0:T(8,128)(2,1)S(1)}, bf16[1,512,512]{2,1,0:T(8,128)(2,1)S(1)}, u32[]{:S(2)}, u32[]{:S(2)}) collective-permute-start(bf16[1,512,512]{2,1,0:T(8,128)(2,1)S(1)} %slice.27), channel_id=1, source_target_pairs={{0,16},{16,0},{1,17},{17,1},{2,18},{18,2},{3,19},{19,3},{4,20},{20... | collective-permute-start | bytes 1572872 | tf_op jit(solution)/shard_map/ppermute | solution.py:171
  4.2 0.0 copy-done
  4.2 0.1 constant_dynamic-update-slice_fusion.1
  4.3 11.8 %collective-permute-done.arrived_ref = bf16[1,512,512]{2,1,0:T(8,128)(2,1)S(1)} collective-permute-done((bf16[1,512,512]{2,1,0:T(8,128)(2,1)S(1)}, bf16[1,512,512]{2,1,0:T(8,128)(2,1)S(1)}, u32[]{:S(2)}, u32[]{:S(2)}) %collective-permute-start) | collective-permute-done | bytes 524320 | tf_op jit(solution)/shard_map/ppermute | solution.py:171
  16.2 0.1 fusion.1
  16.3 0.6 copy-done.1
  16.9 1.3 %collective-permute-start.2 = (bf16[3,512,128]{2,1,0:T(8,128)(2,1)S(1)}, bf16[3,512,128]{2,1,0:T(8,128)(2,1)S(1)}, u32[]{:S(2)}, u32[]{:S(2)}) collective-permute-start(bf16[3,512,128]{2,1,0:T(8,128)(2,1)S(1)} %get-tuple-element.7), channel_id=1, source_target_pairs={{1,0},{2,1},{3,2},{5,4},{6,5},{7,6},{9,8},{10,9},{11,10},{13,12},{... | collective-permute-start | bytes 1179656 | tf_op jit(solution)/shard_map/ppermute | solution.py:40
  18.2 4.6 %collective-permute-start.1 = (bf16[3,512,128]{2,1,0:T(8,128)(2,1)S(1)}, bf16[3,512,128]{2,1,0:T(8,128)(2,1)S(1)}, u32[]{:S(2)}, u32[]{:S(2)}) collective-permute-start(bf16[3,512,128]{2,1,0:T(8,128)(2,1)S(1)} %get-tuple-element.8), channel_id=1, source_target_pairs={{0,1},{1,2},{2,3},{4,5},{5,6},{6,7},{8,9},{9,10},{10,11},{12,13},{... | collective-permute-start | bytes 1179656 | tf_op jit(solution)/shard_map/ppermute | solution.py:40
  22.8 0.1 fusion
  22.8 6.2 %collective-permute-done.2.right_ref = bf16[3,512,128]{2,1,0:T(8,128)(2,1)S(1)} collective-permute-done((bf16[3,512,128]{2,1,0:T(8,128)(2,1)S(1)}, bf16[3,512,128]{2,1,0:T(8,128)(2,1)S(1)}, u32[]{:S(2)}, u32[]{:S(2)}) %collective-permute-start.2) | collective-permute-done | bytes 393248 | tf_op jit(solution)/shard_map/ppermute | solution.py:40
  29.1 1.2 %collective-permute-done.1.left_ref = bf16[3,512,128]{2,1,0:T(8,128)(2,1)S(1)} collective-permute-done((bf16[3,512,128]{2,1,0:T(8,128)(2,1)S(1)}, bf16[3,512,128]{2,1,0:T(8,128)(2,1)S(1)}, u32[]{:S(2)}, u32[]{:S(2)}) %collective-permute-start.1) | collective-permute-done | bytes 393248 | tf_op jit(solution)/shard_map/ppermute | solution.py:40
  30.3 0.0 copy-start.6
  30.3 0.0 copy-start.7
  30.3 0.1 pad_maximum_fusion
  30.4 1.5 %collective-permute-start.3 = (bf16[3,128,768]{2,1,0:T(8,128)(2,1)S(1)}, bf16[3,128,768]{2,1,0:T(8,128)(2,1)S(1)}, u32[]{:S(2)}, u32[]{:S(2)}) collective-permute-start(bf16[3,128,768]{2,1,0:T(8,128)(2,1)S(1)} %pad_maximum_fusion), channel_id=1, source_target_pairs={{0,4},{4,8},{8,12},{1,5},{5,9},{9,13},{2,6},{6,10},{10,14},{3,7},{... | collective-permute-start | bytes 1769480 | tf_op jit(solution)/shard_map/ppermute | solution.py:177
  31.8 0.1 pad_maximum_fusion.1
  31.9 0.0 copy-done.2
  31.9 0.0 copy-done.3
  31.9 1.3 %collective-permute-start.4 = (bf16[3,128,768]{2,1,0:T(8,128)(2,1)S(1)}, bf16[3,128,768]{2,1,0:T(8,128)(2,1)S(1)}, u32[]{:S(2)}, u32[]{:S(2)}) collective-permute-start(bf16[3,128,768]{2,1,0:T(8,128)(2,1)S(1)} %pad_maximum_fusion.1), channel_id=1, source_target_pairs={{4,0},{8,4},{12,8},{5,1},{9,5},{13,9},{6,2},{10,6},{14,10},{7,3},{... | collective-permute-start | bytes 1769480 | tf_op jit(solution)/shard_map/ppermute | solution.py:178
  33.2 0.0 copy-done.6
  33.2 0.1 reshape.8
  33.3 0.0 copy-done.7
  33.3 0.7 concatenate.12.meta_ref
  34.0 0.0 collective-permute-done.3.above_ref
  34.0 3.5 %collective-permute-done.4.below_ref = bf16[3,128,768]{2,1,0:T(8,128)(2,1)S(1)} collective-permute-done((bf16[3,128,768]{2,1,0:T(8,128)(2,1)S(1)}, bf16[3,128,768]{2,1,0:T(8,128)(2,1)S(1)}, u32[]{:S(2)}, u32[]{:S(2)}) %collective-permute-start.4) | collective-permute-done | bytes 589856 | tf_op jit(solution)/shard_map/ppermute | solution.py:178
  37.5 0.0 copy-done.4
  37.5 0.8 %copy-done.5 = bf16[3,128,768]{2,1,0:T(8,128)(2,1)} copy-done((bf16[3,128,768]{2,1,0:T(8,128)(2,1)}, bf16[3,128,768]{2,1,0:T(8,128)(2,1)S(1)}, u32[]{:S(2)}) %copy-start.5) | copy-done | bytes 589848
  38.3 13.8 %match.1 = f32[32,128]{1,0:T(8,128)} custom-call(s32[27]{0:T(128)} %concatenate.12.meta_ref, bf16[512,512]{1,0:T(8,128)(2,1)} %constant.25.table_ref, bf16[512,512]{1,0:T(8,128)(2,1)} %constant.26.turned_ref, f32[4,256,128]{2,1,0:T(8,128)} %constant.28.lag_ref, bf16[2,512,512]{2,1,0:T(8,128)(2,1)} %own_ref.1, bf16[1,512,512]{2,1,0:T(8,128)(2,1)} %copy-done.1, ...), custom_call_target="tpu_custom_call" | custom-call | tf_op jit(solution)/shard_map/match/pallas_call | solution.py:187
  52.1 20.4 %all_to_all.9 = f32[32,1,128]{2,1,0:T(1,128)S(1)} all-to-all(f32[32,1,128]{2,1,0:T(1,128)} %bitcast.6), channel_id=1, replica_groups=mesh['gz'=2,'row'=4,'col'=4] {'gz','row','col'}, dimensions={0} | all-to-all | bytes 32768 | tf_op jit(solution)/shard_map/all_to_all | solution.py:201
  72.5 0.1 reduce_sum.9
  72.6 0.6 reshape.9
  (9 shorter events, 0.1 us)
Async XLA Ops:
  0.0 4.2 %copy-start = (bf16[2,512,512]{2,1,0:T(8,128)(2,1)S(1)}, bf16[2,512,512]{2,1,0:T(8,128)(2,1)}, u32[]{:S(2)}) copy-start(bf16[2,512,512]{2,1,0:T(8,128)(2,1)} %own_ref.1) | copy-start | bytes 3145732
  1.2 15.0 %collective-permute-start = (bf16[1,512,512]{2,1,0:T(8,128)(2,1)S(1)}, bf16[1,512,512]{2,1,0:T(8,128)(2,1)S(1)}, u32[]{:S(2)}, u32[]{:S(2)}) collective-permute-start(bf16[1,512,512]{2,1,0:T(8,128)(2,1)S(1)} %slice.27), channel_id=1, source_target_pairs={{0,16},{16,0},{1,17},{17,1},{2,18},{18,2},{3,19},{19,3},{4,20},{20... | collective-permute-start | bytes 1572872 | tf_op jit(solution)/shard_map/ppermute | solution.py:171
  16.1 0.8 %copy-start.1 = (bf16[1,512,512]{2,1,0:T(8,128)(2,1)}, bf16[1,512,512]{2,1,0:T(8,128)(2,1)S(1)}, u32[]{:S(2)}) copy-start(bf16[1,512,512]{2,1,0:T(8,128)(2,1)S(1)} %collective-permute-done.arrived_ref) | copy-start | bytes 1572868
  16.9 12.2 %collective-permute-start.2 = (bf16[3,512,128]{2,1,0:T(8,128)(2,1)S(1)}, bf16[3,512,128]{2,1,0:T(8,128)(2,1)S(1)}, u32[]{:S(2)}, u32[]{:S(2)}) collective-permute-start(bf16[3,512,128]{2,1,0:T(8,128)(2,1)S(1)} %get-tuple-element.7), channel_id=1, source_target_pairs={{1,0},{2,1},{3,2},{5,4},{6,5},{7,6},{9,8},{10,9},{11,10},{13,12},{... | collective-permute-start | bytes 1179656 | tf_op jit(solution)/shard_map/ppermute | solution.py:40
  18.2 12.1 %collective-permute-start.1 = (bf16[3,512,128]{2,1,0:T(8,128)(2,1)S(1)}, bf16[3,512,128]{2,1,0:T(8,128)(2,1)S(1)}, u32[]{:S(2)}, u32[]{:S(2)}) collective-permute-start(bf16[3,512,128]{2,1,0:T(8,128)(2,1)S(1)} %get-tuple-element.8), channel_id=1, source_target_pairs={{0,1},{1,2},{2,3},{4,5},{5,6},{6,7},{8,9},{9,10},{10,11},{12,13},{... | collective-permute-start | bytes 1179656 | tf_op jit(solution)/shard_map/ppermute | solution.py:40
  29.1 2.8 %copy-start.2 = (bf16[3,512,128]{2,1,0:T(8,128)(2,1)}, bf16[3,512,128]{2,1,0:T(8,128)(2,1)S(1)}, u32[]{:S(2)}) copy-start(bf16[3,512,128]{2,1,0:T(8,128)(2,1)S(1)} %collective-permute-done.2.right_ref) | copy-start | bytes 1179652
  30.3 1.7 %copy-start.3 = (bf16[3,512,128]{2,1,0:T(8,128)(2,1)}, bf16[3,512,128]{2,1,0:T(8,128)(2,1)S(1)}, u32[]{:S(2)}) copy-start(bf16[3,512,128]{2,1,0:T(8,128)(2,1)S(1)} %collective-permute-done.1.left_ref) | copy-start | bytes 1179652
  30.3 3.0 %copy-start.6 = (s32[2,2,2,2]{3,2,1,0:T(2,128)S(1)}, s32[2,2,2,2]{3,2,1,0:T(2,128)}, u32[]{:S(2)}) copy-start(s32[2,2,2,2]{3,2,1,0:T(2,128)} %param.7) | copy-start | bytes 196
  30.3 3.0 %copy-start.7 = (s32[8]{0:T(128)S(1)}, s32[8]{0:T(128)}, u32[]{:S(2)}) copy-start(s32[8]{0:T(128)} %param.8) | copy-start | bytes 100
  30.4 3.6 %collective-permute-start.3 = (bf16[3,128,768]{2,1,0:T(8,128)(2,1)S(1)}, bf16[3,128,768]{2,1,0:T(8,128)(2,1)S(1)}, u32[]{:S(2)}, u32[]{:S(2)}) collective-permute-start(bf16[3,128,768]{2,1,0:T(8,128)(2,1)S(1)} %pad_maximum_fusion), channel_id=1, source_target_pairs={{0,4},{4,8},{8,12},{1,5},{5,9},{9,13},{2,6},{6,10},{10,14},{3,7},{... | collective-permute-start | bytes 1769480 | tf_op jit(solution)/shard_map/ppermute | solution.py:177
  31.9 5.6 %collective-permute-start.4 = (bf16[3,128,768]{2,1,0:T(8,128)(2,1)S(1)}, bf16[3,128,768]{2,1,0:T(8,128)(2,1)S(1)}, u32[]{:S(2)}, u32[]{:S(2)}) collective-permute-start(bf16[3,128,768]{2,1,0:T(8,128)(2,1)S(1)} %pad_maximum_fusion.1), channel_id=1, source_target_pairs={{4,0},{8,4},{12,8},{5,1},{9,5},{13,9},{6,2},{10,6},{14,10},{7,3},{... | collective-permute-start | bytes 1769480 | tf_op jit(solution)/shard_map/ppermute | solution.py:178
  34.0 3.5 %copy-start.4 = (bf16[3,128,768]{2,1,0:T(8,128)(2,1)}, bf16[3,128,768]{2,1,0:T(8,128)(2,1)S(1)}, u32[]{:S(2)}) copy-start(bf16[3,128,768]{2,1,0:T(8,128)(2,1)S(1)} %collective-permute-done.3.above_ref) | copy-start | bytes 1769476
  37.5 0.8 %copy-start.5 = (bf16[3,128,768]{2,1,0:T(8,128)(2,1)}, bf16[3,128,768]{2,1,0:T(8,128)(2,1)S(1)}, u32[]{:S(2)}) copy-start(bf16[3,128,768]{2,1,0:T(8,128)(2,1)S(1)} %collective-permute-done.4.below_ref) | copy-start | bytes 1769476

commit v2 on v1

v2 whole, which is shorter than its diff:
```python
import functools
import math

import jax
import jax.numpy as jnp
import numpy as np
from jax import lax
from jax.experimental import pallas as pl
from jax.experimental.pallas import tpu as pltpu
from jax.sharding import PartitionSpec as P


PATCH = 512
STRIDE = 256
LAGS = 128
MAXOFF = 64
HALO = 256
HALF = PATCH // 2
MARGIN = HALO // 2
AXES = ("gz", "row", "col")
VMEM_LIMIT = 16 * 1024 * 1024
GLUE_FLOPS = 4 * 10**9


def frequency_tables():
    frequencies = np.arange(HALF)[:, None]
    places = np.arange(PATCH)[None, :]
    step = 2.0 * math.pi / PATCH
    cosine = np.cos(np.mod(frequencies * places, PATCH) * step)
    sine_part = np.sin(np.mod(frequencies * places, PATCH) * step)
    sine_part[0] = np.cos(np.mod(HALF * places[0], PATCH) * step)
    table = np.concatenate([cosine, sine_part], axis=0)
    lags = np.arange(-MAXOFF - LAGS // 2, MAXOFF + LAGS // 2) % PATCH
    return table.astype(np.float32), table.T[lags].astype(np.float32)


def split_parts(spec_ref, out_ref):
    for rows, cols in ((slice(0, 16), slice(0, HALF)), (slice(16, HALF), slice(0, 128)), (slice(16, HALF), slice(128, HALF))):
        low_r = slice(rows.start + HALF, rows.stop + HALF)
        low_c = slice(cols.start + HALF, cols.stop + HALF)
        cc = spec_ref[rows, cols]
        cs = spec_ref[rows, low_c]
        sc = spec_ref[low_r, cols]
        ss = spec_ref[low_r, low_c]
        a, b, c, d = cc - ss, sc + cs, cc + ss, sc - cs
        if cols.start == 0:
            edge = lax.broadcasted_iota(jnp.int32, cc.shape, 1) == 0
            a, b, c, d = jnp.where(edge, cc, a), jnp.where(edge, sc, b), jnp.where(edge, cs, c), jnp.where(edge, ss, d)
        if rows.start == 0:
            edge = lax.broadcasted_iota(jnp.int32, cc.shape, 0) == 0
            a, b, c, d = jnp.where(edge, cc, a), jnp.where(edge, cs, b), jnp.where(edge, sc, c), jnp.where(edge, ss, d)
        out_ref[0, rows, cols] = a.astype(out_ref.dtype)
        out_ref[1, rows, cols] = b.astype(out_ref.dtype)
        out_ref[2, rows, cols] = c.astype(out_ref.dtype)
        out_ref[3, rows, cols] = d.astype(out_ref.dtype)


def cross_parts(first_ref, second_ref, out_ref):
    for rows, cols in ((slice(0, 16), slice(0, HALF)), (slice(16, HALF), slice(0, 128)), (slice(16, HALF), slice(128, HALF))):
        low_r = slice(rows.start + HALF, rows.stop + HALF)
        low_c = slice(cols.start + HALF, cols.stop + HALF)
        a, b, c, d = (first_ref[n, rows, cols].astype(jnp.float32) for n in range(4))
        e, f, g, h = (second_ref[n, rows, cols].astype(jnp.float32) for n in range(4))
        p, u = a * e + b * f, a * f - b * e
        q, v = c * g + d * h, c * h - d * g
        cc, cs, sc, ss = p + q, u - v, u + v, q - p
        if cols.start == 0:
            edge = lax.broadcasted_iota(jnp.int32, cc.shape, 1) == 0
            cc, cs, sc, ss = jnp.where(edge, p, cc), jnp.where(edge, q, cs), jnp.where(edge, u, sc), jnp.where(edge, v, ss)
        if rows.start == 0:
            row = lax.broadcasted_iota(jnp.int32, cc.shape, 0) == 0
            cc, cs, sc, ss = jnp.where(row, p, cc), jnp.where(row, u, cs), jnp.where(row, q, sc), jnp.where(row, v, ss)
            corner = jnp.logical_and(row, lax.broadcasted_iota(jnp.int32, cc.shape, 1) == 0)
            cc, cs = jnp.where(corner, 0.5 * (a * e), cc), jnp.where(corner, 0.5 * (b * f), cs)
            sc, ss = jnp.where(corner, 0.5 * (c * g), sc), jnp.where(corner, 0.5 * (d * h), ss)
        out_ref[rows, cols] = cc.astype(jnp.bfloat16)
        out_ref[rows, low_c] = cs.astype(jnp.bfloat16)
        out_ref[low_r, cols] = sc.astype(jnp.bfloat16)
        out_ref[low_r, low_c] = ss.astype(jnp.bfloat16)


def lag_rows(lag_ref, offset):
    pieces = [lag_ref[n, pl.ds(offset + MAXOFF, LAGS), :] for n in range(lag_ref.shape[0])]
    return jnp.concatenate(pieces, axis=1).astype(jnp.bfloat16)


def fill_parts(table_ref, turned_ref, meta_ref, pieces, s, out_ref, ext_ref, rows_ref, spec_ref):
    center_refs, col_refs, row_refs = pieces
    top = ext_ref.shape[0] - MARGIN
    row_even, col_even = meta_ref[1] % 2 == 0, meta_ref[2] % 2 == 0
    inner, outer = row_refs[0][s], row_refs[1][s]
    ext_ref[0:MARGIN, :] = lax.select(row_even, outer, inner)
    ext_ref[top:, :] = lax.select(row_even, inner, outer)
    inner, outer = col_refs[0][s], col_refs[1][s]
    ext_ref[MARGIN:top, 0:MARGIN] = lax.select(col_even, outer, inner)
    ext_ref[MARGIN:top, top:] = lax.select(col_even, inner, outer)
    center_rows(ext_ref.at[MARGIN:top, MARGIN:top], col_even, center_refs, s, slice(0, top - MARGIN))
    per_side = (top - MARGIN) // STRIDE
    for pj in range(per_side):
        rows_ref[...] = jnp.dot(
            ext_ref[:, pj * STRIDE : pj * STRIDE + PATCH], turned_ref[...], preferred_element_type=jnp.float32
        ).astype(jnp.bfloat16)
        for pi in range(per_side):
            spec_ref[...] = jnp.dot(
                table_ref[...], rows_ref[pi * STRIDE : pi * STRIDE + PATCH, :], preferred_element_type=jnp.float32
            )
            split_parts(spec_ref, out_ref.at[pi * per_side + pj])


def center_rows(out_ref, col_even, center_refs, s, rows):
    if len(center_refs) == 1:
        out_ref[...] = center_refs[0][s, rows]
        return
    middle_ref, inner_ref, outer_ref = center_refs
    side = out_ref.shape[1]
    inner, outer = inner_ref[s, rows], outer_ref[s, rows]
    out_ref[:, 0:MARGIN] = lax.select(col_even, outer, inner)
    out_ref[:, MARGIN : side - MARGIN] = middle_ref[s, rows]
    out_ref[:, side - MARGIN :] = lax.select(col_even, inner, outer)


def cut_kernel(meta_ref, far_ref, inner_ref, outer_ref, first_inner_ref, first_outer_ref, middle_ref, own_ref):
    own_ref[...] = far_ref[...]
    side = own_ref.shape[2]
    col_even = meta_ref[2] % 2 == 0
    for s in range(own_ref.shape[0]):
        low, high = own_ref[s, :, 0:MARGIN], own_ref[s, :, side - MARGIN :]
        inner_ref[s] = lax.select(col_even, high, low)
        outer_ref[s] = lax.select(col_even, low, high)
    low, high = own_ref[0, :, 0:MARGIN], own_ref[0, :, side - MARGIN :]
    first_inner_ref[0] = lax.select(col_even, high, low)
    first_outer_ref[0] = lax.select(col_even, low, high)
    middle_ref[0] = own_ref[0, :, MARGIN : side - MARGIN]


def edge_kernel(meta_ref, *refs):
    *center_refs, col_inner_ref, col_outer_ref, inner_ref, outer_ref = refs
    side = col_inner_ref.shape[1]
    row_even, col_even = meta_ref[1] % 2 == 0, meta_ref[2] % 2 == 0
    low, high = slice(0, MARGIN), slice(side - MARGIN, side)
    for s in range(inner_ref.shape[0]):
        for ref, even_rows, odd_rows in ((inner_ref, high, low), (outer_ref, low, high)):
            def pick(source, start, stop):
                return lax.select(row_even, source[s, even_rows, start:stop], source[s, odd_rows, start:stop])

            inner, outer = pick(col_inner_ref, 0, MARGIN), pick(col_outer_ref, 0, MARGIN)
            ref[s, :, 0:MARGIN] = lax.select(col_even, outer, inner)
            ref[s, :, side + MARGIN :] = lax.select(col_even, inner, outer)
            if len(center_refs) == 1:
                ref[s, :, MARGIN : side + MARGIN] = pick(center_refs[0], 0, side)
            else:
                middle_ref, first_inner_ref, first_outer_ref = center_refs
                inner, outer = pick(first_inner_ref, 0, MARGIN), pick(first_outer_ref, 0, MARGIN)
                ref[s, :, MARGIN : 2 * MARGIN] = lax.select(col_even, outer, inner)
                ref[s, :, 2 * MARGIN : side] = pick(middle_ref, 0, side - 2 * MARGIN)
                ref[s, :, side : side + MARGIN] = lax.select(col_even, inner, outer)


def placed_flows(meta_ref, prior_ref, order_ref, lag_ref, cross_ref, first_ref, second_ref, s, shape, sizes):
    size_gz, size_row, size_col, sec_count, per_side = sizes
    place_count = per_side * per_side
    lanes_each = 2 * size_gz * sec_count * size_col * per_side
    row_count = size_row * per_side
    rows_each = row_count // size_row
    holder = lax.broadcasted_iota(jnp.int32, shape, 0)
    lane = lax.broadcasted_iota(jnp.int32, shape, 1)
    slot = jnp.zeros(shape, jnp.int32)
    for m in range(row_count):
        here = jnp.logical_and(holder == m // rows_each, lane // lanes_each == m % rows_each)
        slot = jnp.where(here, order_ref[m], slot)
    lane = lane % lanes_each
    my_gz, my_row, my_col = meta_ref[0], meta_ref[1], meta_ref[2]
    total_out = jnp.zeros(shape, jnp.float32)
    scale = 2.0 / float(PATCH) ** 3
    down = (lax.broadcasted_iota(jnp.int32, (LAGS, LAGS), 0) - LAGS // 2).astype(jnp.float32)
    across = (lax.broadcasted_iota(jnp.int32, (LAGS, LAGS), 1) - LAGS // 2).astype(jnp.float32)
    for n in range(place_count):
        pi, pj = n // per_side, n % per_side
        cross_parts(first_ref.at[n], second_ref.at[n], cross_ref)
        p = prior_ref[0, s, pi, pj]
        q = prior_ref[1, s, pi, pj]
        row_lags = lag_rows(lag_ref, p)
        col_lags = lag_rows(lag_ref, q)
        half = lax.dot_general(
            cross_ref[...], col_lags, (((1,), (1,)), ((), ())), preferred_element_type=jnp.float32
        ).astype(jnp.bfloat16)
        surface = jnp.dot(row_lags, half, preferred_element_type=jnp.float32) * scale
        weights = surface * surface
        total = 1.0 + jnp.sum(weights, keepdims=True)
        shift_r = jnp.sum(weights * down, keepdims=True) / total
        shift_c = jnp.sum(weights * across, keepdims=True) / total
        mine = slot == my_row * per_side + pi
        place = (my_gz * sec_count + s) * (size_col * per_side) + my_col * per_side + pj
        half_lanes = lanes_each // 2
        total_out += jnp.where(jnp.logical_and(mine, lane == place), p.astype(jnp.float32) + shift_r, 0.0)
        total_out += jnp.where(jnp.logical_and(mine, lane == place + half_lanes), q.astype(jnp.float32) + shift_c, 0.0)
    return total_out


def first_kernel(
    meta_ref, table_ref, turned_ref, own_ref, col_inner_ref, col_outer_ref, row_inner_ref, row_outer_ref,
    part_ref, ext_ref, rows_ref, spec_ref, *, section,
):
    pieces = ((own_ref,), (col_inner_ref, col_outer_ref), (row_inner_ref, row_outer_ref))
    fill_parts(table_ref, turned_ref, meta_ref, pieces, section, part_ref, ext_ref, rows_ref, spec_ref)


def next_kernel(
    meta_ref, prior_ref, order_ref, table_ref, turned_ref, own_ref, col_inner_ref, col_outer_ref, row_inner_ref, row_outer_ref,
    lag_ref, flow_in_ref, before_ref, part_ref, flow_ref, ext_ref, rows_ref, spec_ref, cross_ref, *, section, sizes,
):
    pieces = ((own_ref,), (col_inner_ref, col_outer_ref), (row_inner_ref, row_outer_ref))
    fill_parts(table_ref, turned_ref, meta_ref, pieces, section, part_ref, ext_ref, rows_ref, spec_ref)
    flow_ref[...] = flow_in_ref[...] + placed_flows(
        meta_ref, prior_ref, order_ref, lag_ref, cross_ref, before_ref, part_ref, section - 1, flow_ref.shape, sizes
    )


def last_kernel(
    meta_ref, prior_ref, order_ref, table_ref, turned_ref, lag_ref, middle_ref, first_inner_ref, first_outer_ref, col_inner_ref, col_outer_ref,
    row_inner_ref, row_outer_ref, flow_ref, first_ref, out_ref, ext_ref, rows_ref, spec_ref, part_ref, cross_ref, *, sizes,
):
    size_gz, size_row, size_col, sec_count, _ = sizes
    center = (middle_ref, first_inner_ref, first_outer_ref)
    pieces = (center, (col_inner_ref, col_outer_ref), (row_inner_ref, row_outer_ref))
    fill_parts(table_ref, turned_ref, meta_ref, pieces, 0, part_ref, ext_ref, rows_ref, spec_ref)
    flow = flow_ref[...] + placed_flows(
        meta_ref, prior_ref, order_ref, lag_ref, cross_ref, first_ref, part_ref, sec_count - 1, flow_ref.shape, sizes
    )
    for g in range(size_gz):
        for r in range(size_row):
            out_ref[(g * size_row + r) * size_col : (g * size_row + r + 1) * size_col, :] = jnp.broadcast_to(
                flow[r : r + 1, :], (size_col, flow.shape[1])
            )


def exchanges(size):
    inner = [(i, i + 1) for i in range(0, size - 1, 2)]
    outer = [(i, i + 1) for i in range(1, size - 1, 2)]
    return [pairs + [(j, i) for i, j in pairs] for pairs in (inner, outer)]


def match(sections, priors, row_order):
    sec_count, side = sections.shape[:2]
    per_side = side // STRIDE
    place_count = per_side * per_side
    size_gz, size_row, size_col = (lax.axis_size(a) for a in AXES)
    table, lag_table = frequency_tables()
    turned = jnp.asarray(table.T).astype(jnp.bfloat16)
    table = jnp.asarray(table).astype(jnp.bfloat16)
    lag_table = jnp.asarray(np.stack(np.split(lag_table, PATCH // 128, axis=1))).astype(jnp.bfloat16).astype(jnp.float32)
    meta = jnp.stack([lax.axis_index(a) for a in AXES]).astype(jnp.int32)
    wide = side + HALO
    vmem = pl.BlockSpec(memory_space=pltpu.VMEM)
    smem = pl.BlockSpec(memory_space=pltpu.SMEM)
    params = pltpu.CompilerParams(vmem_limit_bytes=VMEM_LIMIT)
    small = pltpu.CompilerParams(vmem_limit_bytes=VMEM_LIMIT // 4)

    def pixels(*shape):
        return jax.ShapeDtypeStruct(shape, jnp.bfloat16)

    gz_pairs = [(i, (i - 1) % size_gz) for i in range(size_gz)]
    col_inner, col_outer = exchanges(size_col)
    row_inner, row_outer = exchanges(size_row)
    glue_cost = pl.CostEstimate(flops=GLUE_FLOPS, bytes_accessed=0, transcendentals=0)
    cuts = pl.pallas_call(
        cut_kernel,
        out_shape=[pixels(sec_count, side, MARGIN)] * 2 + [pixels(1, side, MARGIN)] * 2 + [pixels(1, side, side - HALO), pixels(*sections.shape)],
        in_specs=[smem, vmem],
        out_specs=[vmem] * 6,
        compiler_params=small,
        cost_estimate=glue_cost,
        name="cut",
    )(meta, sections)
    own = cuts[5]
    own_cols = (lax.ppermute(cuts[0], "col", col_inner), lax.ppermute(cuts[1], "col", col_outer))
    first_inner = lax.ppermute(cuts[2], "gz", gz_pairs)
    first_outer = lax.ppermute(cuts[3], "gz", gz_pairs)
    middle = lax.ppermute(cuts[4], "gz", gz_pairs)
    last_cols = (lax.ppermute(first_inner, "col", col_inner), lax.ppermute(first_outer, "col", col_outer))

    def edges(count, center, cols):
        call = pl.pallas_call(
            edge_kernel,
            out_shape=[pixels(count, MARGIN, wide)] * 2,
            in_specs=[smem] + [vmem] * (len(center) + 2),
            out_specs=[vmem] * 2,
            compiler_params=small,
            cost_estimate=glue_cost,
        )
        inner, outer = call(meta, *center, *cols)
        return lax.ppermute(inner, "row", row_inner), lax.ppermute(outer, "row", row_outer)

    last_center = (middle, first_inner, first_outer)
    own_rows = edges(sec_count, (own,), own_cols)
    last_rows = edges(1, last_center, last_cols)
    lanes = (row_order.shape[0] // size_row) * 2 * size_gz * sec_count * size_col * per_side
    devices = size_gz * size_row * size_col
    sizes = (size_gz, size_row, size_col, sec_count, per_side)
    parts = (place_count, 4, HALF, HALF)

    part_shape = jax.ShapeDtypeStruct(parts, jnp.float32)
    flow_shape = jax.ShapeDtypeStruct((size_row, lanes), jnp.float32)
    ext_scratch = pltpu.VMEM((wide, wide), jnp.bfloat16)
    rows_scratch = pltpu.VMEM((wide, PATCH), jnp.bfloat16)
    spec_scratch = pltpu.VMEM((PATCH, PATCH), jnp.float32)
    part_scratch = pltpu.VMEM(parts, jnp.float32)
    cross_scratch = pltpu.VMEM((PATCH, PATCH), jnp.bfloat16)
    spectra_cost = 2 * per_side * wide * PATCH * PATCH + 2 * place_count * PATCH**3
    pair_cost = 2 * place_count * PATCH * LAGS * (PATCH + LAGS)

    def cost(flops):
        return pl.CostEstimate(flops=flops, bytes_accessed=place_count * PATCH * PATCH * 4, transcendentals=0)

    flow = jnp.zeros((size_row, lanes), jnp.float32)
    pieces = (own, *own_cols, *own_rows)
    first_call = pl.pallas_call(
        functools.partial(first_kernel, section=0),
        out_shape=part_shape,
        in_specs=[smem] + [vmem] * 7,
        out_specs=vmem,
        scratch_shapes=[ext_scratch, rows_scratch, spec_scratch],
        compiler_params=params,
        cost_estimate=cost(spectra_cost),
        name="first",
    )
    part = first_call(meta, table, turned, *pieces)
    for section in range(1, sec_count):
        next_call = pl.pallas_call(
            functools.partial(next_kernel, section=section, sizes=sizes),
            out_shape=(part_shape, flow_shape),
            in_specs=[smem] * 3 + [vmem] * 10,
            out_specs=(vmem, vmem),
            scratch_shapes=[ext_scratch, rows_scratch, spec_scratch, cross_scratch],
            compiler_params=params,
            cost_estimate=cost(spectra_cost + pair_cost),
            name="next",
        )
        part, flow = next_call(meta, priors, row_order, table, turned, *pieces, lag_table, flow, part)
    sent = pl.pallas_call(
        functools.partial(last_kernel, sizes=sizes),
        out_shape=jax.ShapeDtypeStruct((devices, lanes), jnp.float32),
        in_specs=[smem] * 3 + [vmem] * 12,
        out_specs=vmem,
        scratch_shapes=[ext_scratch, rows_scratch, spec_scratch, part_scratch, cross_scratch],
        compiler_params=params,
        cost_estimate=cost(spectra_cost + pair_cost),
        name="last",
    )(meta, priors, row_order, table, turned, lag_table, *last_center, *last_cols, *last_rows, flow, part)
    received = lax.all_to_all(sent, AXES, 0, 0, tiled=True)
    return jnp.sum(received, axis=0).reshape(row_order.shape[0] // size_row, -1)


def solution(mesh):
    placed = (P("gz", "row", "col"), P(None, "gz", "row", "col"), P())
    return jax.shard_map(match, mesh=mesh, in_specs=placed, out_specs=P("row", None), check_vma=False)
```

time: 73.5 us -> 56.6 us (0.77)
  waiting for transfers between devices: 22.8 us -> 2.87 us
  starting transfers between devices: 11.6 us -> 16.9 us
  local copies, waits for them, and re-layouts: 4.35 us -> 1.91 us
  Pallas kernels: 13.8 us -> 15.7 us
  blocking collectives: 20.4 us -> 18.6 us
    ppermute x5 -> x11, waiting for transfers between devices: 22.8 us -> 2.87 us  [the longest x1 2.85 us: match(): first_inner = lax.ppermute(cuts[2], 'gz', gz_pairs)]
    ppermute x5 -> x11, starting transfers between devices: 11.6 us -> 16.9 us  [the longest x1 4.39 us: match(): lax.ppermute(first_inner, 'col', col_inner)]
    pallas_call x1 -> x6, Pallas kernels: 13.8 us -> 15.7 us  [the longest x1 5.52 us: match(): next_call(meta, priors, row_order, table, turned, *pieces, lag_table, flo...]
    all_to_all x1, blocking collectives: 20.4 us -> 18.6 us  [match(): received = lax.all_to_all(sent, AXES, 0, 0, tiled=True)]
    slice x5 -> x0, local copies, waits for them, and re-layouts: 1.38 us -> none  [the longest x1 1.16 us: body(): sections[:1]]
    unnamed x17 -> x12, local copies, waits for them, and re-layouts: 1.53 us -> 1.26 us
  transfers between devices with their start and end apart: 5 -> 11, of which waited for: 4 -> 1; matrix products, arithmetic and copies ran while one was open for 1% -> 0% of each run, Pallas kernels for 0% -> 17%
where the time goes in v2:
time: 56.6 us; the launch traced here: 56.3 us
  blocking collectives  18.6 us (33%)
  starting transfers between devices  16.9 us (30%)
  Pallas kernels  15.7 us (28%)
  waiting for transfers between devices  2.87 us (5%)
  local copies, waits for them, and re-layouts  1.91 us (3%)
    all_to_all x1, blocking collectives, match(): received = lax.all_to_all(sent, AXES, 0, 0, tiled=True)  18.6 us
    pallas_call x1, Pallas kernels, match(): next_call(meta, priors, row_order, table, turned, *pieces, lag_table, flo...  5.52 us
    pallas_call x1, Pallas kernels, match(): pl.pallas_call(functools.partial(last_kernel, sizes=sizes), out_shape=jax...  5.36 us
    ppermute x1, starting transfers between devices, match(): lax.ppermute(first_inner, 'col', col_inner)  4.39 us
    ppermute x1, starting transfers between devices, match(): lax.ppermute(cuts[0], 'col', col_inner)  3.12 us
    ppermute x2, starting transfers between devices, edges(): lax.ppermute(inner, 'row', row_inner)  3.02 us
    ppermute x1, waiting for transfers between devices, match(): first_inner = lax.ppermute(cuts[2], 'gz', gz_pairs)  2.85 us
    pallas_call x1, Pallas kernels, match(): part = first_call(meta, table, turned, *pieces)  2.68 us
  transfers between devices with their start and end apart: 11, of which 1 were waited for; matrix products, arithmetic and copies ran while one was open for 0% of the time, Pallas kernels for 17%

profile of v2, /device:TPU:0, one launch (start us, length us, event | category | flops | bytes accessed | tf_op | source)
XLA Modules:
  0.0 56.3 jit_solution(11895032884889311432)
XLA Ops:
  0.0 0.1 pad_add_fusion.meta_ref
  0.1 1.2 %copy-done.2 = bf16[2,512,512]{2,1,0:T(8,128)(2,1)S(1)} copy-done((bf16[2,512,512]{2,1,0:T(8,128)(2,1)S(1)}, bf16[2,512,512]{2,1,0:T(8,128)(2,1)}, u32[]{:S(2)}) %copy-start.2) | copy-done | bytes 1048600
  1.3 0.8 %cut.1 = (bf16[2,512,128]{2,1,0:T(8,128)(2,1)S(1)}, bf16[2,512,128]{2,1,0:T(8,128)(2,1)S(1)}, bf16[1,512,128]{2,1,0:T(8,128)(2,1)S(1)}, bf16[1,512,128]{2,1,0:T(...) custom-call(s32[3]{0:T(128)S(1)} %pad_add_fusion.meta_ref, ...), custom_call_target="tpu_custom_call" | custom-call | flops 4000000000 | tf_op jit(solution)/shard_map/cut/pallas_call | solution.py:266
  2.1 3.1 %collective-permute-start.7 = (bf16[2,512,128]{2,1,0:T(8,128)(2,1)S(1)}, bf16[2,512,128]{2,1,0:T(8,128)(2,1)S(1)}, u32[]{:S(2)}, u32[]{:S(2)}) collective-permute-start(bf16[2,512,128]{2,1,0:T(8,128)(2,1)S(1)} %get-tuple-element.23), channel_id=1, source_target_pairs={{0,1},{2,3},{1,0},{3,2},{4,5},{6,7},{5,4},{7,6},{8,9},{10,11},{9,8... | collective-permute-start | bytes 786440 | tf_op jit(solution)/shard_map/ppermute | solution.py:276
  5.2 0.7 %collective-permute-start.8 = (bf16[2,512,128]{2,1,0:T(8,128)(2,1)S(1)}, bf16[2,512,128]{2,1,0:T(8,128)(2,1)S(1)}, u32[]{:S(2)}, u32[]{:S(2)}) collective-permute-start(bf16[2,512,128]{2,1,0:T(8,128)(2,1)S(1)} %get-tuple-element.24), channel_id=1, source_target_pairs={{1,2},{2,1},{5,6},{6,5},{9,10},{10,9},{13,14},{14,13},{17,18},{18,... | collective-permute-start | bytes 786440 | tf_op jit(solution)/shard_map/ppermute | solution.py:276
  5.9 1.6 %collective-permute-start.1 = (bf16[1,512,128]{2,1,0:T(8,128)(2,1)S(1)}, bf16[1,512,128]{2,1,0:T(8,128)(2,1)S(1)}, u32[]{:S(2)}, u32[]{:S(2)}) collective-permute-start(bf16[1,512,128]{2,1,0:T(8,128)(2,1)S(1)} %get-tuple-element.18), channel_id=1, source_target_pairs={{0,16},{16,0},{1,17},{17,1},{2,18},{18,2},{3,19},{19,3},{4,20},{20... | collective-permute-start | bytes 393224 | tf_op jit(solution)/shard_map/ppermute | solution.py:277
  7.4 0.5 collective-permute-start.2
  8.0 1.5 %collective-permute-start = (bf16[1,512,256]{2,1,0:T(8,128)(2,1)S(1)}, bf16[1,512,256]{2,1,0:T(8,128)(2,1)S(1)}, u32[]{:S(2)}, u32[]{:S(2)}) collective-permute-start(bf16[1,512,256]{2,1,0:T(8,128)(2,1)S(1)} %get-tuple-element.17), channel_id=1, source_target_pairs={{0,16},{16,0},{1,17},{17,1},{2,18},{18,2},{3,19},{19,3},{4,20},{20... | collective-permute-start | bytes 786440 | tf_op jit(solution)/shard_map/ppermute | solution.py:279
  9.5 2.8 %collective-permute-done.1.refs_1_.first_inner_ref = bf16[1,512,128]{2,1,0:T(8,128)(2,1)S(1)} collective-permute-done((bf16[1,512,128]{2,1,0:T(8,128)(2,1)S(1)}, bf16[1,512,128]{2,1,0:T(8,128)(2,1)S(1)}, u32[]{:S(2)}, u32[]{:S(2)}) %collective-permute-start.1) | collective-permute-done | bytes 131104 | tf_op jit(solution)/shard_map/ppermute | solution.py:277
  12.3 4.4 %collective-permute-start.3 = (bf16[1,512,128]{2,1,0:T(8,128)(2,1)S(1)}, bf16[1,512,128]{2,1,0:T(8,128)(2,1)S(1)}, u32[]{:S(2)}, u32[]{:S(2)}) collective-permute-start(bf16[1,512,128]{2,1,0:T(8,128)(2,1)S(1)} %collective-permute-done.1.refs_1_.first_inner_ref), channel_id=1, source_target_pairs={{0,1},{2,3},{1,0},{3,2},{4,5},{6,7},{5,4},{7,6},{8,9},{10,11},{9,8... | collective-permute-start | bytes 393224 | tf_op jit(solution)/shard_map/ppermute | solution.py:280
  16.7 0.0 collective-permute-done.2.refs_2_.first_outer_ref
  16.7 0.7 %collective-permute-start.4 = (bf16[1,512,128]{2,1,0:T(8,128)(2,1)S(1)}, bf16[1,512,128]{2,1,0:T(8,128)(2,1)S(1)}, u32[]{:S(2)}, u32[]{:S(2)}) collective-permute-start(bf16[1,512,128]{2,1,0:T(8,128)(2,1)S(1)} %collective-permute-done.2.refs_2_.first_outer_ref), channel_id=1, source_target_pairs={{1,2},{2,1},{5,6},{6,5},{9,10},{10,9},{13,14},{14,13},{17,18},{18,... | collective-permute-start | bytes 393224 | tf_op jit(solution)/shard_map/ppermute | solution.py:280
  17.4 0.0 collective-permute-done.8.refs_2_.col_outer_ref
  17.4 0.7 %shard_map.65 = (bf16[2,128,768]{2,1,0:T(8,128)(2,1)S(1)}, bf16[2,128,768]{2,1,0:T(8,128)(2,1)S(1)}) custom-call(s32[3]{0:T(128)S(1)} %pad_add_fusion.meta_ref, bf16[2,512,512]{2,1,0:T(8,128)(2,1)S(1)} %get-tuple-element.22.refs_0_.own_ref, bf16[2,512,128]{2,1,0:T(8,128)(2,1)S(1)} %collective-permute-done.7.refs_1_.col_inner_ref, ...), custom_call_target="tpu_custom_call" | custom-call | flops 4000000000 | tf_op jit(solution)/shard_map/pallas_call | solution.py:291
  18.1 0.7 %collective-permute-start.10 = (bf16[2,128,768]{2,1,0:T(8,128)(2,1)S(1)}, bf16[2,128,768]{2,1,0:T(8,128)(2,1)S(1)}, u32[]{:S(2)}, u32[]{:S(2)}) collective-permute-start(bf16[2,128,768]{2,1,0:T(8,128)(2,1)S(1)} %get-tuple-element.26), channel_id=1, source_target_pairs={{4,8},{8,4},{5,9},{9,5},{6,10},{10,6},{7,11},{11,7},{20,24},{24,20... | collective-permute-start | bytes 1179656 | tf_op jit(solution)/shard_map/ppermute | solution.py:292
  18.8 0.0 copy-start
  18.8 0.0 copy-start.1
  18.8 2.9 %collective-permute-start.9 = (bf16[2,128,768]{2,1,0:T(8,128)(2,1)S(1)}, bf16[2,128,768]{2,1,0:T(8,128)(2,1)S(1)}, u32[]{:S(2)}, u32[]{:S(2)}) collective-permute-start(bf16[2,128,768]{2,1,0:T(8,128)(2,1)S(1)} %get-tuple-element.25), channel_id=1, source_target_pairs={{0,4},{8,12},{4,0},{12,8},{1,5},{9,13},{5,1},{13,9},{2,6},{10,14},... | collective-permute-start | bytes 1179656 | tf_op jit(solution)/shard_map/ppermute | solution.py:292
  21.7 0.6 %shard_map.64 = (bf16[1,128,768]{2,1,0:T(8,128)(2,1)S(1)}, bf16[1,128,768]{2,1,0:T(8,128)(2,1)S(1)}) custom-call(s32[3]{0:T(128)S(1)} %pad_add_fusion.meta_ref, bf16[1,512,256]{2,1,0:T(8,128)(2,1)S(1)} %collective-permute-done.refs_0_.middle_ref, bf16[1,512,128]{2,1,0:T(8,128)(2,1)S(1)} %collective-permute-done.1.refs_1_.first_inner_ref, ...), custom_call_target="tpu_custom_call" | custom-call | flops 4000000000 | tf_op jit(solution)/shard_map/pallas_call | solution.py:291
  22.4 0.0 copy-start.3
  22.4 0.0 copy-start.4
  22.4 0.0 copy-start.5
  22.4 0.1 collective-permute-start.5
  22.5 0.8 %collective-permute-start.6 = (bf16[1,128,768]{2,1,0:T(8,128)(2,1)S(1)}, bf16[1,128,768]{2,1,0:T(8,128)(2,1)S(1)}, u32[]{:S(2)}, u32[]{:S(2)}) collective-permute-start(bf16[1,128,768]{2,1,0:T(8,128)(2,1)S(1)} %get-tuple-element.21), channel_id=1, source_target_pairs={{4,8},{8,4},{5,9},{9,5},{6,10},{10,6},{7,11},{11,7},{20,24},{24,20... | collective-permute-start | bytes 589832 | tf_op jit(solution)/shard_map/ppermute | solution.py:292
  23.3 0.0 collective-permute-done.10.row_outer_ref
  23.3 2.7 %first.1.before_ref = f32[4,4,256,256]{3,2,1,0:T(8,128)S(1)} custom-call(s32[3]{0:T(128)S(1)} %pad_add_fusion.meta_ref, bf16[512,512]{1,0:T(8,128)(2,1)S(1)} %copy-done, bf16[512,512]{1,0:T(8,128)(2,1)S(1)} %copy-done.1, bf16[2,512,512]{2,1,0:T(8,128)(2,1)S(1)} %get-tuple-element.22.refs_0_.own_ref, ...), custom_call_target="tpu_custom_call" | custom-call | flops 1879048192 | bytes 4194304 | tf_op jit(solution)/shard_map/first/pallas_call | solution.py:327
  26.1 5.5 %next.1 = (f32[4,4,256,256]{3,2,1,0:T(8,128)S(1)}, f32[4,128]{1,0:T(4,128)S(1)}) custom-call(s32[3]{0:T(128)S(1)} %pad_add_fusion.meta_ref, s32[2,2,2,2]{3,2,1,0:T(2,128)S(1)} %copy-done.3, s32[8]{0:T(128)S(1)} %copy-done.4, bf16[512,512]{1,0:T(8,128)(2,1)S(1)} %copy-done, bf16[512,512]{1,0:T(8,128)(2,1)S(1)} %copy-done.1, ...), custom_call_target="tpu_custom_call" | custom-call | flops 2214592512 | bytes 4194304 | tf_op jit(solution)/shard_map/next/pallas_call | solution.py:339
  31.6 0.0 collective-permute-done.6.row_outer_ref
  31.6 5.4 %last.1 = f32[32,128]{1,0:T(8,128)S(1)} custom-call(s32[3]{0:T(128)S(1)} %pad_add_fusion.meta_ref, s32[2,2,2,2]{3,2,1,0:T(2,128)S(1)} %copy-done.3, s32[8]{0:T(128)S(1)} %copy-done.4, bf16[512,512]{1,0:T(8,128)(2,1)S(1)} %copy-done, bf16[512,512]{1,0:T(8,128)(2,1)S(1)} %copy-done.1, f32[4,256,128]{2,1,0:T(8,128)S(1)} %copy-done.5, ...), custom_call_target="tpu_custom_call" | custom-call | flops 2214592512 | bytes 4194304 | tf_op jit(solution)/shard_map/last/pallas_call | solution.py:340
  37.0 18.6 %all_to_all.9 = f32[32,1,128]{2,1,0:T(1,128)S(1)} all-to-all(f32[32,1,128]{2,1,0:T(1,128)S(1)} %bitcast.6), channel_id=1, replica_groups=mesh['gz'=2,'row'=4,'col'=4] {'gz','row','col'}, dimensions={0} | all-to-all | bytes 32768 | tf_op jit(solution)/shard_map/all_to_all | solution.py:350
  55.6 0.1 reduce_sum.9
  55.7 0.6 %reshape.5 = f32[2,64]{1,0:T(2,128)} reshape(f32[128]{0:T(128)S(1)} %reduce_sum.9) | data formatting | bytes 1024 | tf_op jit(solution)/shard_map/reshape | solution.py:351
  (13 shorter events, 0.0 us)
Async XLA Ops:
  0.1 1.2 %copy-start.2 = (bf16[2,512,512]{2,1,0:T(8,128)(2,1)S(1)}, bf16[2,512,512]{2,1,0:T(8,128)(2,1)}, u32[]{:S(2)}) copy-start(bf16[2,512,512]{2,1,0:T(8,128)(2,1)} %far_ref.1) | copy-start | bytes 3145732
  2.1 15.3 %collective-permute-start.7 = (bf16[2,512,128]{2,1,0:T(8,128)(2,1)S(1)}, bf16[2,512,128]{2,1,0:T(8,128)(2,1)S(1)}, u32[]{:S(2)}, u32[]{:S(2)}) collective-permute-start(bf16[2,512,128]{2,1,0:T(8,128)(2,1)S(1)} %get-tuple-element.23), channel_id=1, source_target_pairs={{0,1},{2,3},{1,0},{3,2},{4,5},{6,7},{5,4},{7,6},{8,9},{10,11},{9,8... | collective-permute-start | bytes 786440 | tf_op jit(solution)/shard_map/ppermute | solution.py:276
  5.2 12.2 %collective-permute-start.8 = (bf16[2,512,128]{2,1,0:T(8,128)(2,1)S(1)}, bf16[2,512,128]{2,1,0:T(8,128)(2,1)S(1)}, u32[]{:S(2)}, u32[]{:S(2)}) collective-permute-start(bf16[2,512,128]{2,1,0:T(8,128)(2,1)S(1)} %get-tuple-element.24), channel_id=1, source_target_pairs={{1,2},{2,1},{5,6},{6,5},{9,10},{10,9},{13,14},{14,13},{17,18},{18,... | collective-permute-start | bytes 786440 | tf_op jit(solution)/shard_map/ppermute | solution.py:276
  5.9 6.4 %collective-permute-start.1 = (bf16[1,512,128]{2,1,0:T(8,128)(2,1)S(1)}, bf16[1,512,128]{2,1,0:T(8,128)(2,1)S(1)}, u32[]{:S(2)}, u32[]{:S(2)}) collective-permute-start(bf16[1,512,128]{2,1,0:T(8,128)(2,1)S(1)} %get-tuple-element.18), channel_id=1, source_target_pairs={{0,16},{16,0},{1,17},{17,1},{2,18},{18,2},{3,19},{19,3},{4,20},{20... | collective-permute-start | bytes 393224 | tf_op jit(solution)/shard_map/ppermute | solution.py:277
  7.4 9.3 %collective-permute-start.2 = (bf16[1,512,128]{2,1,0:T(8,128)(2,1)S(1)}, bf16[1,512,128]{2,1,0:T(8,128)(2,1)S(1)}, u32[]{:S(2)}, u32[]{:S(2)}) collective-permute-start(bf16[1,512,128]{2,1,0:T(8,128)(2,1)S(1)} %get-tuple-element.19), channel_id=1, source_target_pairs={{0,16},{16,0},{1,17},{17,1},{2,18},{18,2},{3,19},{19,3},{4,20},{20... | collective-permute-start | bytes 393224 | tf_op jit(solution)/shard_map/ppermute | solution.py:278
  8.0 13.8 %collective-permute-start = (bf16[1,512,256]{2,1,0:T(8,128)(2,1)S(1)}, bf16[1,512,256]{2,1,0:T(8,128)(2,1)S(1)}, u32[]{:S(2)}, u32[]{:S(2)}) collective-permute-start(bf16[1,512,256]{2,1,0:T(8,128)(2,1)S(1)} %get-tuple-element.17), channel_id=1, source_target_pairs={{0,16},{16,0},{1,17},{17,1},{2,18},{18,2},{3,19},{19,3},{4,20},{20... | collective-permute-start | bytes 786440 | tf_op jit(solution)/shard_map/ppermute | solution.py:279
  12.3 9.4 %collective-permute-start.3 = (bf16[1,512,128]{2,1,0:T(8,128)(2,1)S(1)}, bf16[1,512,128]{2,1,0:T(8,128)(2,1)S(1)}, u32[]{:S(2)}, u32[]{:S(2)}) collective-permute-start(bf16[1,512,128]{2,1,0:T(8,128)(2,1)S(1)} %collective-permute-done.1.refs_1_.first_inner_ref), channel_id=1, source_target_pairs={{0,1},{2,3},{1,0},{3,2},{4,5},{6,7},{5,4},{7,6},{8,9},{10,11},{9,8... | collective-permute-start | bytes 393224 | tf_op jit(solution)/shard_map/ppermute | solution.py:280
  16.7 5.0 %collective-permute-start.4 = (bf16[1,512,128]{2,1,0:T(8,128)(2,1)S(1)}, bf16[1,512,128]{2,1,0:T(8,128)(2,1)S(1)}, u32[]{:S(2)}, u32[]{:S(2)}) collective-permute-start(bf16[1,512,128]{2,1,0:T(8,128)(2,1)S(1)} %collective-permute-done.2.refs_2_.first_outer_ref), channel_id=1, source_target_pairs={{1,2},{2,1},{5,6},{6,5},{9,10},{10,9},{13,14},{14,13},{17,18},{18,... | collective-permute-start | bytes 393224 | tf_op jit(solution)/shard_map/ppermute | solution.py:280
  18.1 5.2 %collective-permute-start.10 = (bf16[2,128,768]{2,1,0:T(8,128)(2,1)S(1)}, bf16[2,128,768]{2,1,0:T(8,128)(2,1)S(1)}, u32[]{:S(2)}, u32[]{:S(2)}) collective-permute-start(bf16[2,128,768]{2,1,0:T(8,128)(2,1)S(1)} %get-tuple-element.26), channel_id=1, source_target_pairs={{4,8},{8,4},{5,9},{9,5},{6,10},{10,6},{7,11},{11,7},{20,24},{24,20... | collective-permute-start | bytes 1179656 | tf_op jit(solution)/shard_map/ppermute | solution.py:292
  18.8 4.6 %copy-start = (bf16[512,512]{1,0:T(8,128)(2,1)S(1)}, bf16[512,512]{1,0:T(8,128)(2,1)}, u32[]{:S(2)}) copy-start(bf16[512,512]{1,0:T(8,128)(2,1)} %constant.26.table_ref) | copy-start | bytes 1572868
  18.8 4.6 %copy-start.1 = (bf16[512,512]{1,0:T(8,128)(2,1)S(1)}, bf16[512,512]{1,0:T(8,128)(2,1)}, u32[]{:S(2)}) copy-start(bf16[512,512]{1,0:T(8,128)(2,1)} %constant.27.turned_ref) | copy-start | bytes 1572868
  18.8 4.5 %collective-permute-start.9 = (bf16[2,128,768]{2,1,0:T(8,128)(2,1)S(1)}, bf16[2,128,768]{2,1,0:T(8,128)(2,1)S(1)}, u32[]{:S(2)}, u32[]{:S(2)}) collective-permute-start(bf16[2,128,768]{2,1,0:T(8,128)(2,1)S(1)} %get-tuple-element.25), channel_id=1, source_target_pairs={{0,4},{8,12},{4,0},{12,8},{1,5},{9,13},{5,1},{13,9},{2,6},{10,14},... | collective-permute-start | bytes 1179656 | tf_op jit(solution)/shard_map/ppermute | solution.py:292
  22.4 3.7 %copy-start.3 = (s32[2,2,2,2]{3,2,1,0:T(2,128)S(1)}, s32[2,2,2,2]{3,2,1,0:T(2,128)}, u32[]{:S(2)}) copy-start(s32[2,2,2,2]{3,2,1,0:T(2,128)} %prior_ref.3) | copy-start | bytes 196
  22.4 3.7 %copy-start.4 = (s32[8]{0:T(128)S(1)}, s32[8]{0:T(128)}, u32[]{:S(2)}) copy-start(s32[8]{0:T(128)} %order_ref.3) | copy-start | bytes 100
  22.4 3.7 %copy-start.5 = (f32[4,256,128]{2,1,0:T(8,128)S(1)}, f32[4,256,128]{2,1,0:T(8,128)}, u32[]{:S(2)}) copy-start(f32[4,256,128]{2,1,0:T(8,128)} %constant.29.lag_ref) | copy-start | bytes 1572868
  22.4 9.2 %collective-permute-start.5 = (bf16[1,128,768]{2,1,0:T(8,128)(2,1)S(1)}, bf16[1,128,768]{2,1,0:T(8,128)(2,1)S(1)}, u32[]{:S(2)}, u32[]{:S(2)}) collective-permute-start(bf16[1,128,768]{2,1,0:T(8,128)(2,1)S(1)} %get-tuple-element.20), channel_id=1, source_target_pairs={{0,4},{8,12},{4,0},{12,8},{1,5},{9,13},{5,1},{13,9},{2,6},{10,14},... | collective-permute-start | bytes 589832 | tf_op jit(solution)/shard_map/ppermute | solution.py:292
  22.5 9.1 %collective-permute-start.6 = (bf16[1,128,768]{2,1,0:T(8,128)(2,1)S(1)}, bf16[1,128,768]{2,1,0:T(8,128)(2,1)S(1)}, u32[]{:S(2)}, u32[]{:S(2)}) collective-permute-start(bf16[1,128,768]{2,1,0:T(8,128)(2,1)S(1)} %get-tuple-element.21), channel_id=1, source_target_pairs={{4,8},{8,4},{5,9},{9,5},{6,10},{10,6},{7,11},{11,7},{20,24},{24,20... | collective-permute-start | bytes 589832 | tf_op jit(solution)/shard_map/ppermute | solution.py:292

commit v3 on v2

--- a/solution.py
+++ b/solution.py
@@ -23,25 +23,40 @@
 
 
 def frequency_tables():
-    frequencies = np.arange(HALF)[:, None]
+    frequencies = np.concatenate([np.arange(0, HALF, 2), np.arange(1, HALF, 2)])[:, None]
     places = np.arange(PATCH)[None, :]
     step = 2.0 * math.pi / PATCH
     cosine = np.cos(np.mod(frequencies * places, PATCH) * step)
     sine_part = np.sin(np.mod(frequencies * places, PATCH) * step)
     sine_part[0] = np.cos(np.mod(HALF * places[0], PATCH) * step)
-    table = np.concatenate([cosine, sine_part], axis=0)
+    quarter = HALF // 2
+    table = np.concatenate([cosine[:quarter], sine_part[:quarter], cosine[quarter:], sine_part[quarter:]], axis=0)
     lags = np.arange(-MAXOFF - LAGS // 2, MAXOFF + LAGS // 2) % PATCH
-    return table.astype(np.float32), table.T[lags].astype(np.float32)
+    return table[:, :HALF].astype(np.float32), table.T[lags].astype(np.float32)
+
+
+def blocks():
+    quarter = HALF // 2
+    for k_odd in range(2):
+        for l_odd in range(2):
+            cols = slice(l_odd * HALF, l_odd * HALF + quarter)
+            if k_odd == 0:
+                yield slice(0, 16), cols
+                yield slice(16, quarter), cols
+            else:
+                yield slice(HALF, HALF + quarter), cols
+
+
+def sines(part):
+    return slice(part.start + HALF // 2, part.stop + HALF // 2)
 
 
 def split_parts(spec_ref, out_ref):
-    for rows, cols in ((slice(0, 16), slice(0, HALF)), (slice(16, HALF), slice(0, 128)), (slice(16, HALF), slice(128, HALF))):
-        low_r = slice(rows.start + HALF, rows.stop + HALF)
-        low_c = slice(cols.start + HALF, cols.stop + HALF)
+    for rows, cols in blocks():
         cc = spec_ref[rows, cols]
-        cs = spec_ref[rows, low_c]
-        sc = spec_ref[low_r, cols]
-        ss = spec_ref[low_r, low_c]
+        cs = spec_ref[rows, sines(cols)]
+        sc = spec_ref[sines(rows), cols]
+        ss = spec_ref[sines(rows), sines(cols)]
         a, b, c, d = cc - ss, sc + cs, cc + ss, sc - cs
         if cols.start == 0:
             edge = lax.broadcasted_iota(jnp.int32, cc.shape, 1) == 0
@@ -49,18 +64,17 @@
         if rows.start == 0:
             edge = lax.broadcasted_iota(jnp.int32, cc.shape, 0) == 0
             a, b, c, d = jnp.where(edge, cc, a), jnp.where(edge, cs, b), jnp.where(edge, sc, c), jnp.where(edge, ss, d)
-        out_ref[0, rows, cols] = a.astype(out_ref.dtype)
-        out_ref[1, rows, cols] = b.astype(out_ref.dtype)
-        out_ref[2, rows, cols] = c.astype(out_ref.dtype)
-        out_ref[3, rows, cols] = d.astype(out_ref.dtype)
+        out_ref[rows, cols] = a
+        out_ref[rows, sines(cols)] = b
+        out_ref[sines(rows), cols] = c
+        out_ref[sines(rows), sines(cols)] = d
 
 
 def cross_parts(first_ref, second_ref, out_ref):
-    for rows, cols in ((slice(0, 16), slice(0, HALF)), (slice(16, HALF), slice(0, 128)), (slice(16, HALF), slice(128, HALF))):
-        low_r = slice(rows.start + HALF, rows.stop + HALF)
-        low_c = slice(cols.start + HALF, cols.stop + HALF)
-        a, b, c, d = (first_ref[n, rows, cols].astype(jnp.float32) for n in range(4))
-        e, f, g, h = (second_ref[n, rows, cols].astype(jnp.float32) for n in range(4))
+    for rows, cols in blocks():
+        places = ((rows, cols), (rows, sines(cols)), (sines(rows), cols), (sines(rows), sines(cols)))
+        a, b, c, d = (first_ref[place] for place in places)
+        e, f, g, h = (second_ref[place] for place in places)
         p, u = a * e + b * f, a * f - b * e
         q, v = c * g + d * h, c * h - d * g
         cc, cs, sc, ss = p + q, u - v, u + v, q - p
@@ -70,13 +84,12 @@
         if rows.start == 0:
             row = lax.broadcasted_iota(jnp.int32, cc.shape, 0) == 0
             cc, cs, sc, ss = jnp.where(row, p, cc), jnp.where(row, u, cs), jnp.where(row, q, sc), jnp.where(row, v, ss)
-            corner = jnp.logical_and(row, lax.broadcasted_iota(jnp.int32, cc.shape, 1) == 0)
-            cc, cs = jnp.where(corner, 0.5 * (a * e), cc), jnp.where(corner, 0.5 * (b * f), cs)
-            sc, ss = jnp.where(corner, 0.5 * (c * g), sc), jnp.where(corner, 0.5 * (d * h), ss)
-        out_ref[rows, cols] = cc.astype(jnp.bfloat16)
-        out_ref[rows, low_c] = cs.astype(jnp.bfloat16)
-        out_ref[low_r, cols] = sc.astype(jnp.bfloat16)
-        out_ref[low_r, low_c] = ss.astype(jnp.bfloat16)
+            if cols.start == 0:
+                corner = jnp.logical_and(row, edge)
+                cc, cs = jnp.where(corner, 0.5 * (a * e), cc), jnp.where(corner, 0.5 * (b * f), cs)
+                sc, ss = jnp.where(corner, 0.5 * (c * g), sc), jnp.where(corner, 0.5 * (d * h), ss)
+        for place, value in zip(places, (cc, cs, sc, ss)):
+            out_ref[place] = value.astype(jnp.bfloat16)
 
 
 def lag_rows(lag_ref, offset):
@@ -96,15 +109,19 @@
     ext_ref[MARGIN:top, top:] = lax.select(col_even, inner, outer)
     center_rows(ext_ref.at[MARGIN:top, MARGIN:top], col_even, center_refs, s, slice(0, top - MARGIN))
     per_side = (top - MARGIN) // STRIDE
+    parities = (slice(0, HALF), slice(HALF, PATCH))
     for pj in range(per_side):
-        rows_ref[...] = jnp.dot(
-            ext_ref[:, pj * STRIDE : pj * STRIDE + PATCH], turned_ref[...], preferred_element_type=jnp.float32
-        ).astype(jnp.bfloat16)
+        near = ext_ref[:, pj * STRIDE : pj * STRIDE + HALF]
+        away = ext_ref[:, pj * STRIDE + HALF : pj * STRIDE + PATCH]
+        for part, folded in zip(parities, (near + away, near - away)):
+            rows_ref[pj, :, part] = jnp.dot(folded, turned_ref[:, part], preferred_element_type=jnp.float32).astype(jnp.bfloat16)
         for pi in range(per_side):
-            spec_ref[...] = jnp.dot(
-                table_ref[...], rows_ref[pi * STRIDE : pi * STRIDE + PATCH, :], preferred_element_type=jnp.float32
-            )
-            split_parts(spec_ref, out_ref.at[pi * per_side + pj])
+            n = pi * per_side + pj
+            near = rows_ref[pj, pi * STRIDE : pi * STRIDE + HALF, :]
+            away = rows_ref[pj, pi * STRIDE + HALF : pi * STRIDE + PATCH, :]
+            for part, folded in zip(parities, (near + away, near - away)):
+                spec_ref[n % 2, part] = jnp.dot(table_ref[part], folded, preferred_element_type=jnp.float32)
+            split_parts(spec_ref.at[n % 2], out_ref.at[n])
 
 
 def center_rows(out_ref, col_even, center_refs, s, rows):
@@ -173,27 +190,29 @@
     total_out = jnp.zeros(shape, jnp.float32)
     scale = 2.0 / float(PATCH) ** 3
     down = (lax.broadcasted_iota(jnp.int32, (LAGS, LAGS), 0) - LAGS // 2).astype(jnp.float32)
-    across = (lax.broadcasted_iota(jnp.int32, (LAGS, LAGS), 1) - LAGS // 2).astype(jnp.float32)
+    across = (lax.broadcasted_iota(jnp.int32, (1, LAGS), 1) - LAGS // 2).astype(jnp.float32)
+    sums = []
     for n in range(place_count):
         pi, pj = n // per_side, n % per_side
-        cross_parts(first_ref.at[n], second_ref.at[n], cross_ref)
-        p = prior_ref[0, s, pi, pj]
-        q = prior_ref[1, s, pi, pj]
-        row_lags = lag_rows(lag_ref, p)
-        col_lags = lag_rows(lag_ref, q)
-        half = lax.dot_general(
-            cross_ref[...], col_lags, (((1,), (1,)), ((), ())), preferred_element_type=jnp.float32
-        ).astype(jnp.bfloat16)
-        surface = jnp.dot(row_lags, half, preferred_element_type=jnp.float32) * scale
+        cross_parts(first_ref.at[n], second_ref.at[n], cross_ref.at[n])
+        row_lags = lag_rows(lag_ref, prior_ref[0, s, pi, pj])
+        col_lags = lag_rows(lag_ref, prior_ref[1, s, pi, pj])
+        half = jnp.dot(row_lags, cross_ref[n], preferred_element_type=jnp.float32).astype(jnp.bfloat16)
+        surface = scale * lax.dot_general(
+            half, col_lags, (((1,), (1,)), ((), ())), preferred_element_type=jnp.float32
+        )
         weights = surface * surface
-        total = 1.0 + jnp.sum(weights, keepdims=True)
-        shift_r = jnp.sum(weights * down, keepdims=True) / total
-        shift_c = jnp.sum(weights * across, keepdims=True) / total
-        mine = slot == my_row * per_side + pi
+        plain = jnp.sum(weights, axis=0, keepdims=True)
+        sums += [plain, jnp.sum(weights * down, axis=0, keepdims=True), plain * across]
+    sums = jnp.sum(jnp.concatenate(sums, axis=0), axis=1, keepdims=True)
+    for n in range(place_count):
+        pi, pj = n // per_side, n % per_side
+        total = 1.0 + sums[3 * n : 3 * n + 1]
         place = (my_gz * sec_count + s) * (size_col * per_side) + my_col * per_side + pj
-        half_lanes = lanes_each // 2
-        total_out += jnp.where(jnp.logical_and(mine, lane == place), p.astype(jnp.float32) + shift_r, 0.0)
-        total_out += jnp.where(jnp.logical_and(mine, lane == place + half_lanes), q.astype(jnp.float32) + shift_c, 0.0)
+        for c in range(2):
+            value = prior_ref[c, s, pi, pj].astype(jnp.float32) + sums[3 * n + 1 + c : 3 * n + 2 + c] / total
+            here = jnp.logical_and(slot == my_row * per_side + pi, lane == place + c * (lanes_each // 2))
+            total_out += jnp.where(here, value, 0.0)
     return total_out
 
 
@@ -297,15 +316,15 @@
     lanes = (row_order.shape[0] // size_row) * 2 * size_gz * sec_count * size_col * per_side
     devices = size_gz * size_row * size_col
     sizes = (size_gz, size_row, size_col, sec_count, per_side)
-    parts = (place_count, 4, HALF, HALF)
+    parts = (place_count, PATCH, PATCH)
 
     part_shape = jax.ShapeDtypeStruct(parts, jnp.float32)
     flow_shape = jax.ShapeDtypeStruct((size_row, lanes), jnp.float32)
     ext_scratch = pltpu.VMEM((wide, wide), jnp.bfloat16)
-    rows_scratch = pltpu.VMEM((wide, PATCH), jnp.bfloat16)
-    spec_scratch = pltpu.VMEM((PATCH, PATCH), jnp.float32)
+    rows_scratch = pltpu.VMEM((per_side, wide, PATCH), jnp.bfloat16)
+    spec_scratch = pltpu.VMEM((2, PATCH, PATCH), jnp.float32)
     part_scratch = pltpu.VMEM(parts, jnp.float32)
-    cross_scratch = pltpu.VMEM((PATCH, PATCH), jnp.bfloat16)
+    cross_scratch = pltpu.VMEM((place_count, PATCH, PATCH), jnp.bfloat16)
     spectra_cost = 2 * per_side * wide * PATCH * PATCH + 2 * place_count * PATCH**3
     pair_cost = 2 * place_count * PATCH * LAGS * (PATCH + LAGS)
 

time: 56.6 us -> 52.3 us (0.924)
  Pallas kernels: 15.7 us -> 11.4 us
    pallas_call x1, Pallas kernels: 5.52 us -> 3.71 us  [match(): next_call(meta, priors, row_order, table, turned, *pieces, lag_table, flo...]
    pallas_call x1, Pallas kernels: 5.36 us -> 3.73 us  [match(): pl.pallas_call(functools.partial(last_kernel, sizes=sizes), out_shape=jax...]
    pallas_call x1, Pallas kernels: 2.68 us -> 1.91 us  [match(): part = first_call(meta, table, turned, *pieces)]
  transfers between devices with their start and end apart: 11 -> 11, of which waited for: 1 -> 1; matrix products, arithmetic and copies ran while one was open for 0% -> 0% of each run, Pallas kernels for 17% -> 13%
where the time goes in v3:
time: 52.3 us; the launch traced here: 52.1 us
  blocking collectives  18.6 us (36%)
  starting transfers between devices  16.9 us (32%)
  Pallas kernels  11.4 us (22%)
  waiting for transfers between devices  2.87 us (5%)
  local copies, waits for them, and re-layouts  1.91 us (4%)
    all_to_all x1, blocking collectives, match(): received = lax.all_to_all(sent, AXES, 0, 0, tiled=True)  18.6 us
    ppermute x1, starting transfers between devices, match(): lax.ppermute(first_inner, 'col', col_inner)  4.39 us
    pallas_call x1, Pallas kernels, match(): pl.pallas_call(functools.partial(last_kernel, sizes=sizes), out_shape=jax...  3.73 us
    pallas_call x1, Pallas kernels, match(): next_call(meta, priors, row_order, table, turned, *pieces, lag_table, flo...  3.71 us
    ppermute x1, starting transfers between devices, match(): lax.ppermute(cuts[0], 'col', col_inner)  3.12 us
    ppermute x2, starting transfers between devices, edges(): lax.ppermute(inner, 'row', row_inner)  3.02 us
    ppermute x1, waiting for transfers between devices, match(): first_inner = lax.ppermute(cuts[2], 'gz', gz_pairs)  2.85 us
    pallas_call x1, Pallas kernels, match(): part = first_call(meta, table, turned, *pieces)  1.91 us
  transfers between devices with their start and end apart: 11, of which 1 were waited for; matrix products, arithmetic and copies ran while one was open for 0% of the time, Pallas kernels for 13%

profile of v3, /device:TPU:0, one launch (start us, length us, event | category | flops | bytes accessed | tf_op | source)
XLA Modules:
  0.0 52.1 jit_solution(9411762372012494746)
XLA Ops:
  0.0 0.1 pad_add_fusion.meta_ref
  0.1 1.2 %copy-done.2 = bf16[2,512,512]{2,1,0:T(8,128)(2,1)S(1)} copy-done((bf16[2,512,512]{2,1,0:T(8,128)(2,1)S(1)}, bf16[2,512,512]{2,1,0:T(8,128)(2,1)}, u32[]{:S(2)}) %copy-start.2) | copy-done | bytes 1048600
  1.3 0.8 %cut.1 = (bf16[2,512,128]{2,1,0:T(8,128)(2,1)S(1)}, bf16[2,512,128]{2,1,0:T(8,128)(2,1)S(1)}, bf16[1,512,128]{2,1,0:T(8,128)(2,1)S(1)}, bf16[1,512,128]{2,1,0:T(...) custom-call(s32[3]{0:T(128)S(1)} %pad_add_fusion.meta_ref, ...), custom_call_target="tpu_custom_call" | custom-call | flops 4000000000 | tf_op jit(solution)/shard_map/cut/pallas_call | solution.py:285
  2.1 3.1 %collective-permute-start.7 = (bf16[2,512,128]{2,1,0:T(8,128)(2,1)S(1)}, bf16[2,512,128]{2,1,0:T(8,128)(2,1)S(1)}, u32[]{:S(2)}, u32[]{:S(2)}) collective-permute-start(bf16[2,512,128]{2,1,0:T(8,128)(2,1)S(1)} %get-tuple-element.23), channel_id=1, source_target_pairs={{0,1},{2,3},{1,0},{3,2},{4,5},{6,7},{5,4},{7,6},{8,9},{10,11},{9,8... | collective-permute-start | bytes 786440 | tf_op jit(solution)/shard_map/ppermute | solution.py:295
  5.2 0.7 %collective-permute-start.8 = (bf16[2,512,128]{2,1,0:T(8,128)(2,1)S(1)}, bf16[2,512,128]{2,1,0:T(8,128)(2,1)S(1)}, u32[]{:S(2)}, u32[]{:S(2)}) collective-permute-start(bf16[2,512,128]{2,1,0:T(8,128)(2,1)S(1)} %get-tuple-element.24), channel_id=1, source_target_pairs={{1,2},{2,1},{5,6},{6,5},{9,10},{10,9},{13,14},{14,13},{17,18},{18,... | collective-permute-start | bytes 786440 | tf_op jit(solution)/shard_map/ppermute | solution.py:295
  5.9 1.6 %collective-permute-start.1 = (bf16[1,512,128]{2,1,0:T(8,128)(2,1)S(1)}, bf16[1,512,128]{2,1,0:T(8,128)(2,1)S(1)}, u32[]{:S(2)}, u32[]{:S(2)}) collective-permute-start(bf16[1,512,128]{2,1,0:T(8,128)(2,1)S(1)} %get-tuple-element.18), channel_id=1, source_target_pairs={{0,16},{16,0},{1,17},{17,1},{2,18},{18,2},{3,19},{19,3},{4,20},{20... | collective-permute-start | bytes 393224 | tf_op jit(solution)/shard_map/ppermute | solution.py:296
  7.4 0.5 %collective-permute-start.2 = (bf16[1,512,128]{2,1,0:T(8,128)(2,1)S(1)}, bf16[1,512,128]{2,1,0:T(8,128)(2,1)S(1)}, u32[]{:S(2)}, u32[]{:S(2)}) collective-permute-start(bf16[1,512,128]{2,1,0:T(8,128)(2,1)S(1)} %get-tuple-element.19), channel_id=1, source_target_pairs={{0,16},{16,0},{1,17},{17,1},{2,18},{18,2},{3,19},{19,3},{4,20},{20... | collective-permute-start | bytes 393224 | tf_op jit(solution)/shard_map/ppermute | solution.py:297
  8.0 1.5 %collective-permute-start = (bf16[1,512,256]{2,1,0:T(8,128)(2,1)S(1)}, bf16[1,512,256]{2,1,0:T(8,128)(2,1)S(1)}, u32[]{:S(2)}, u32[]{:S(2)}) collective-permute-start(bf16[1,512,256]{2,1,0:T(8,128)(2,1)S(1)} %get-tuple-element.17), channel_id=1, source_target_pairs={{0,16},{16,0},{1,17},{17,1},{2,18},{18,2},{3,19},{19,3},{4,20},{20... | collective-permute-start | bytes 786440 | tf_op jit(solution)/shard_map/ppermute | solution.py:298
  9.5 2.8 %collective-permute-done.1.refs_1_.first_inner_ref = bf16[1,512,128]{2,1,0:T(8,128)(2,1)S(1)} collective-permute-done((bf16[1,512,128]{2,1,0:T(8,128)(2,1)S(1)}, bf16[1,512,128]{2,1,0:T(8,128)(2,1)S(1)}, u32[]{:S(2)}, u32[]{:S(2)}) %collective-permute-start.1) | collective-permute-done | bytes 131104 | tf_op jit(solution)/shard_map/ppermute | solution.py:296
  12.3 4.4 %collective-permute-start.3 = (bf16[1,512,128]{2,1,0:T(8,128)(2,1)S(1)}, bf16[1,512,128]{2,1,0:T(8,128)(2,1)S(1)}, u32[]{:S(2)}, u32[]{:S(2)}) collective-permute-start(bf16[1,512,128]{2,1,0:T(8,128)(2,1)S(1)} %collective-permute-done.1.refs_1_.first_inner_ref), channel_id=1, source_target_pairs={{0,1},{2,3},{1,0},{3,2},{4,5},{6,7},{5,4},{7,6},{8,9},{10,11},{9,8... | collective-permute-start | bytes 393224 | tf_op jit(solution)/shard_map/ppermute | solution.py:299
  16.7 0.0 collective-permute-done.2.refs_2_.first_outer_ref
  16.7 0.7 %collective-permute-start.4 = (bf16[1,512,128]{2,1,0:T(8,128)(2,1)S(1)}, bf16[1,512,128]{2,1,0:T(8,128)(2,1)S(1)}, u32[]{:S(2)}, u32[]{:S(2)}) collective-permute-start(bf16[1,512,128]{2,1,0:T(8,128)(2,1)S(1)} %collective-permute-done.2.refs_2_.first_outer_ref), channel_id=1, source_target_pairs={{1,2},{2,1},{5,6},{6,5},{9,10},{10,9},{13,14},{14,13},{17,18},{18,... | collective-permute-start | bytes 393224 | tf_op jit(solution)/shard_map/ppermute | solution.py:299
  17.4 0.0 collective-permute-done.7.refs_1_.col_inner_ref
  17.4 0.0 collective-permute-done.8.refs_2_.col_outer_ref
  17.4 0.7 %shard_map.65 = (bf16[2,128,768]{2,1,0:T(8,128)(2,1)S(1)}, bf16[2,128,768]{2,1,0:T(8,128)(2,1)S(1)}) custom-call(s32[3]{0:T(128)S(1)} %pad_add_fusion.meta_ref, bf16[2,512,512]{2,1,0:T(8,128)(2,1)S(1)} %get-tuple-element.22.refs_0_.own_ref, bf16[2,512,128]{2,1,0:T(8,128)(2,1)S(1)} %collective-permute-done.7.refs_1_.col_inner_ref, ...), custom_call_target="tpu_custom_call" | custom-call | flops 4000000000 | tf_op jit(solution)/shard_map/pallas_call | solution.py:310
  18.1 0.7 %collective-permute-start.10 = (bf16[2,128,768]{2,1,0:T(8,128)(2,1)S(1)}, bf16[2,128,768]{2,1,0:T(8,128)(2,1)S(1)}, u32[]{:S(2)}, u32[]{:S(2)}) collective-permute-start(bf16[2,128,768]{2,1,0:T(8,128)(2,1)S(1)} %get-tuple-element.26), channel_id=1, source_target_pairs={{4,8},{8,4},{5,9},{9,5},{6,10},{10,6},{7,11},{11,7},{20,24},{24,20... | collective-permute-start | bytes 1179656 | tf_op jit(solution)/shard_map/ppermute | solution.py:311
  18.8 0.0 copy-start
  18.8 0.0 copy-start.1
  18.8 2.9 %collective-permute-start.9 = (bf16[2,128,768]{2,1,0:T(8,128)(2,1)S(1)}, bf16[2,128,768]{2,1,0:T(8,128)(2,1)S(1)}, u32[]{:S(2)}, u32[]{:S(2)}) collective-permute-start(bf16[2,128,768]{2,1,0:T(8,128)(2,1)S(1)} %get-tuple-element.25), channel_id=1, source_target_pairs={{0,4},{8,12},{4,0},{12,8},{1,5},{9,13},{5,1},{13,9},{2,6},{10,14},... | collective-permute-start | bytes 1179656 | tf_op jit(solution)/shard_map/ppermute | solution.py:311
  21.7 0.6 %shard_map.64 = (bf16[1,128,768]{2,1,0:T(8,128)(2,1)S(1)}, bf16[1,128,768]{2,1,0:T(8,128)(2,1)S(1)}) custom-call(s32[3]{0:T(128)S(1)} %pad_add_fusion.meta_ref, bf16[1,512,256]{2,1,0:T(8,128)(2,1)S(1)} %collective-permute-done.refs_0_.middle_ref, bf16[1,512,128]{2,1,0:T(8,128)(2,1)S(1)} %collective-permute-done.1.refs_1_.first_inner_ref, ...), custom_call_target="tpu_custom_call" | custom-call | flops 4000000000 | tf_op jit(solution)/shard_map/pallas_call | solution.py:310
  22.4 0.0 copy-start.3
  22.4 0.0 copy-start.4
  22.4 0.0 copy-start.5
  22.4 0.1 collective-permute-start.5
  22.5 0.8 %collective-permute-start.6 = (bf16[1,128,768]{2,1,0:T(8,128)(2,1)S(1)}, bf16[1,128,768]{2,1,0:T(8,128)(2,1)S(1)}, u32[]{:S(2)}, u32[]{:S(2)}) collective-permute-start(bf16[1,128,768]{2,1,0:T(8,128)(2,1)S(1)} %get-tuple-element.21), channel_id=1, source_target_pairs={{4,8},{8,4},{5,9},{9,5},{6,10},{10,6},{7,11},{11,7},{20,24},{24,20... | collective-permute-start | bytes 589832 | tf_op jit(solution)/shard_map/ppermute | solution.py:311
  23.3 0.0 collective-permute-done.10.row_outer_ref
  23.3 1.9 %first.1.before_ref = f32[4,512,512]{2,1,0:T(8,128)S(1)} custom-call(s32[3]{0:T(128)S(1)} %pad_add_fusion.meta_ref, bf16[512,256]{1,0:T(8,128)(2,1)S(1)} %copy-done, bf16[256,512]{1,0:T(8,128)(2,1)S(1)} %copy-done.1, bf16[2,512,512]{2,1,0:T(8,128)(2,1)S(1)} %get-tuple-element.22.refs_0_.own_ref, ...), custom_call_target="tpu_custom_call" | custom-call | flops 1879048192 | bytes 4194304 | tf_op jit(solution)/shard_map/first/pallas_call | solution.py:346
  25.3 3.7 %next.1 = (f32[4,512,512]{2,1,0:T(8,128)S(1)}, f32[4,128]{1,0:T(4,128)S(1)}) custom-call(s32[3]{0:T(128)S(1)} %pad_add_fusion.meta_ref, s32[2,2,2,2]{3,2,1,0:T(2,128)S(1)} %copy-done.3, s32[8]{0:T(128)S(1)} %copy-done.4, bf16[512,256]{1,0:T(8,128)(2,1)S(1)} %copy-done, bf16[256,512]{1,0:T(8,128)(2,1)S(1)} %copy-done.1, ...), custom_call_target="tpu_custom_call" | custom-call | flops 2214592512 | bytes 4194304 | tf_op jit(solution)/shard_map/next/pallas_call | solution.py:358
  29.0 3.7 %last.1 = f32[32,128]{1,0:T(8,128)S(1)} custom-call(s32[3]{0:T(128)S(1)} %pad_add_fusion.meta_ref, s32[2,2,2,2]{3,2,1,0:T(2,128)S(1)} %copy-done.3, s32[8]{0:T(128)S(1)} %copy-done.4, bf16[512,256]{1,0:T(8,128)(2,1)S(1)} %copy-done, bf16[256,512]{1,0:T(8,128)(2,1)S(1)} %copy-done.1, f32[4,256,128]{2,1,0:T(8,128)S(1)} %copy-done.5, ...), custom_call_target="tpu_custom_call" | custom-call | flops 2214592512 | bytes 4194304 | tf_op jit(solution)/shard_map/last/pallas_call | solution.py:359
  32.8 18.6 %all_to_all.9 = f32[32,1,128]{2,1,0:T(1,128)S(1)} all-to-all(f32[32,1,128]{2,1,0:T(1,128)S(1)} %bitcast.6), channel_id=1, replica_groups=mesh['gz'=2,'row'=4,'col'=4] {'gz','row','col'}, dimensions={0} | all-to-all | bytes 32768 | tf_op jit(solution)/shard_map/all_to_all | solution.py:369
  51.4 0.1 reduce_sum.9
  51.4 0.6 %reshape.5 = f32[2,64]{1,0:T(2,128)} reshape(f32[128]{0:T(128)S(1)} %reduce_sum.9) | data formatting | bytes 1024 | tf_op jit(solution)/shard_map/reshape | solution.py:370
  (13 shorter events, 0.0 us)
Async XLA Ops:
  0.1 1.2 %copy-start.2 = (bf16[2,512,512]{2,1,0:T(8,128)(2,1)S(1)}, bf16[2,512,512]{2,1,0:T(8,128)(2,1)}, u32[]{:S(2)}) copy-start(bf16[2,512,512]{2,1,0:T(8,128)(2,1)} %far_ref.1) | copy-start | bytes 3145732
  2.1 15.3 %collective-permute-start.7 = (bf16[2,512,128]{2,1,0:T(8,128)(2,1)S(1)}, bf16[2,512,128]{2,1,0:T(8,128)(2,1)S(1)}, u32[]{:S(2)}, u32[]{:S(2)}) collective-permute-start(bf16[2,512,128]{2,1,0:T(8,128)(2,1)S(1)} %get-tuple-element.23), channel_id=1, source_target_pairs={{0,1},{2,3},{1,0},{3,2},{4,5},{6,7},{5,4},{7,6},{8,9},{10,11},{9,8... | collective-permute-start | bytes 786440 | tf_op jit(solution)/shard_map/ppermute | solution.py:295
  5.2 12.2 %collective-permute-start.8 = (bf16[2,512,128]{2,1,0:T(8,128)(2,1)S(1)}, bf16[2,512,128]{2,1,0:T(8,128)(2,1)S(1)}, u32[]{:S(2)}, u32[]{:S(2)}) collective-permute-start(bf16[2,512,128]{2,1,0:T(8,128)(2,1)S(1)} %get-tuple-element.24), channel_id=1, source_target_pairs={{1,2},{2,1},{5,6},{6,5},{9,10},{10,9},{13,14},{14,13},{17,18},{18,... | collective-permute-start | bytes 786440 | tf_op jit(solution)/shard_map/ppermute | solution.py:295
  5.9 6.4 %collective-permute-start.1 = (bf16[1,512,128]{2,1,0:T(8,128)(2,1)S(1)}, bf16[1,512,128]{2,1,0:T(8,128)(2,1)S(1)}, u32[]{:S(2)}, u32[]{:S(2)}) collective-permute-start(bf16[1,512,128]{2,1,0:T(8,128)(2,1)S(1)} %get-tuple-element.18), channel_id=1, source_target_pairs={{0,16},{16,0},{1,17},{17,1},{2,18},{18,2},{3,19},{19,3},{4,20},{20... | collective-permute-start | bytes 393224 | tf_op jit(solution)/shard_map/ppermute | solution.py:296
  7.4 9.3 %collective-permute-start.2 = (bf16[1,512,128]{2,1,0:T(8,128)(2,1)S(1)}, bf16[1,512,128]{2,1,0:T(8,128)(2,1)S(1)}, u32[]{:S(2)}, u32[]{:S(2)}) collective-permute-start(bf16[1,512,128]{2,1,0:T(8,128)(2,1)S(1)} %get-tuple-element.19), channel_id=1, source_target_pairs={{0,16},{16,0},{1,17},{17,1},{2,18},{18,2},{3,19},{19,3},{4,20},{20... | collective-permute-start | bytes 393224 | tf_op jit(solution)/shard_map/ppermute | solution.py:297
  8.0 13.8 %collective-permute-start = (bf16[1,512,256]{2,1,0:T(8,128)(2,1)S(1)}, bf16[1,512,256]{2,1,0:T(8,128)(2,1)S(1)}, u32[]{:S(2)}, u32[]{:S(2)}) collective-permute-start(bf16[1,512,256]{2,1,0:T(8,128)(2,1)S(1)} %get-tuple-element.17), channel_id=1, source_target_pairs={{0,16},{16,0},{1,17},{17,1},{2,18},{18,2},{3,19},{19,3},{4,20},{20... | collective-permute-start | bytes 786440 | tf_op jit(solution)/shard_map/ppermute | solution.py:298
  12.3 9.4 %collective-permute-start.3 = (bf16[1,512,128]{2,1,0:T(8,128)(2,1)S(1)}, bf16[1,512,128]{2,1,0:T(8,128)(2,1)S(1)}, u32[]{:S(2)}, u32[]{:S(2)}) collective-permute-start(bf16[1,512,128]{2,1,0:T(8,128)(2,1)S(1)} %collective-permute-done.1.refs_1_.first_inner_ref), channel_id=1, source_target_pairs={{0,1},{2,3},{1,0},{3,2},{4,5},{6,7},{5,4},{7,6},{8,9},{10,11},{9,8... | collective-permute-start | bytes 393224 | tf_op jit(solution)/shard_map/ppermute | solution.py:299
  16.7 5.0 %collective-permute-start.4 = (bf16[1,512,128]{2,1,0:T(8,128)(2,1)S(1)}, bf16[1,512,128]{2,1,0:T(8,128)(2,1)S(1)}, u32[]{:S(2)}, u32[]{:S(2)}) collective-permute-start(bf16[1,512,128]{2,1,0:T(8,128)(2,1)S(1)} %collective-permute-done.2.refs_2_.first_outer_ref), channel_id=1, source_target_pairs={{1,2},{2,1},{5,6},{6,5},{9,10},{10,9},{13,14},{14,13},{17,18},{18,... | collective-permute-start | bytes 393224 | tf_op jit(solution)/shard_map/ppermute | solution.py:299
  18.1 5.2 %collective-permute-start.10 = (bf16[2,128,768]{2,1,0:T(8,128)(2,1)S(1)}, bf16[2,128,768]{2,1,0:T(8,128)(2,1)S(1)}, u32[]{:S(2)}, u32[]{:S(2)}) collective-permute-start(bf16[2,128,768]{2,1,0:T(8,128)(2,1)S(1)} %get-tuple-element.26), channel_id=1, source_target_pairs={{4,8},{8,4},{5,9},{9,5},{6,10},{10,6},{7,11},{11,7},{20,24},{24,20... | collective-permute-start | bytes 1179656 | tf_op jit(solution)/shard_map/ppermute | solution.py:311
  18.8 4.6 %copy-start = (bf16[512,256]{1,0:T(8,128)(2,1)S(1)}, bf16[512,256]{1,0:T(8,128)(2,1)}, u32[]{:S(2)}) copy-start(bf16[512,256]{1,0:T(8,128)(2,1)} %constant.26.table_ref) | copy-start | bytes 786436
  18.8 4.6 %copy-start.1 = (bf16[256,512]{1,0:T(8,128)(2,1)S(1)}, bf16[256,512]{1,0:T(8,128)(2,1)}, u32[]{:S(2)}) copy-start(bf16[256,512]{1,0:T(8,128)(2,1)} %constant.27.turned_ref) | copy-start | bytes 786436
  18.8 4.5 %collective-permute-start.9 = (bf16[2,128,768]{2,1,0:T(8,128)(2,1)S(1)}, bf16[2,128,768]{2,1,0:T(8,128)(2,1)S(1)}, u32[]{:S(2)}, u32[]{:S(2)}) collective-permute-start(bf16[2,128,768]{2,1,0:T(8,128)(2,1)S(1)} %get-tuple-element.25), channel_id=1, source_target_pairs={{0,4},{8,12},{4,0},{12,8},{1,5},{9,13},{5,1},{13,9},{2,6},{10,14},... | collective-permute-start | bytes 1179656 | tf_op jit(solution)/shard_map/ppermute | solution.py:311
  22.4 2.9 %copy-start.3 = (s32[2,2,2,2]{3,2,1,0:T(2,128)S(1)}, s32[2,2,2,2]{3,2,1,0:T(2,128)}, u32[]{:S(2)}) copy-start(s32[2,2,2,2]{3,2,1,0:T(2,128)} %prior_ref.3) | copy-start | bytes 196
  22.4 2.9 %copy-start.4 = (s32[8]{0:T(128)S(1)}, s32[8]{0:T(128)}, u32[]{:S(2)}) copy-start(s32[8]{0:T(128)} %order_ref.3) | copy-start | bytes 100
  22.4 2.9 %copy-start.5 = (f32[4,256,128]{2,1,0:T(8,128)S(1)}, f32[4,256,128]{2,1,0:T(8,128)}, u32[]{:S(2)}) copy-start(f32[4,256,128]{2,1,0:T(8,128)} %constant.29.lag_ref) | copy-start | bytes 1572868
  22.4 6.6 %collective-permute-start.5 = (bf16[1,128,768]{2,1,0:T(8,128)(2,1)S(1)}, bf16[1,128,768]{2,1,0:T(8,128)(2,1)S(1)}, u32[]{:S(2)}, u32[]{:S(2)}) collective-permute-start(bf16[1,128,768]{2,1,0:T(8,128)(2,1)S(1)} %get-tuple-element.20), channel_id=1, source_target_pairs={{0,4},{8,12},{4,0},{12,8},{1,5},{9,13},{5,1},{13,9},{2,6},{10,14},... | collective-permute-start | bytes 589832 | tf_op jit(solution)/shard_map/ppermute | solution.py:311
  22.5 6.5 %collective-permute-start.6 = (bf16[1,128,768]{2,1,0:T(8,128)(2,1)S(1)}, bf16[1,128,768]{2,1,0:T(8,128)(2,1)S(1)}, u32[]{:S(2)}, u32[]{:S(2)}) collective-permute-start(bf16[1,128,768]{2,1,0:T(8,128)(2,1)S(1)} %get-tuple-element.21), channel_id=1, source_target_pairs={{4,8},{8,4},{5,9},{9,5},{6,10},{10,6},{7,11},{11,7},{20,24},{24,20... | collective-permute-start | bytes 589832 | tf_op jit(solution)/shard_map/ppermute | solution.py:311

commit v4 on v3

--- a/solution.py
+++ b/solution.py
@@ -101,9 +101,19 @@
     center_refs, col_refs, row_refs = pieces
     top = ext_ref.shape[0] - MARGIN
     row_even, col_even = meta_ref[1] % 2 == 0, meta_ref[2] % 2 == 0
-    inner, outer = row_refs[0][s], row_refs[1][s]
-    ext_ref[0:MARGIN, :] = lax.select(row_even, outer, inner)
-    ext_ref[top:, :] = lax.select(row_even, inner, outer)
+    if len(row_refs) == 2:
+        spans = ((row_refs, slice(None), slice(None)),)
+    else:
+        corners = row_refs[2:]
+        spans = (
+            (row_refs[:2], slice(None), slice(MARGIN, top)),
+            (corners, slice(0, MARGIN), slice(0, MARGIN)),
+            (corners, slice(MARGIN, 2 * MARGIN), slice(top, top + MARGIN)),
+        )
+    for refs, source, target in spans:
+        inner, outer = refs[0][s, :, source], refs[1][s, :, source]
+        ext_ref[0:MARGIN, target] = lax.select(row_even, outer, inner)
+        ext_ref[top:, target] = lax.select(row_even, inner, outer)
     inner, outer = col_refs[0][s], col_refs[1][s]
     ext_ref[MARGIN:top, 0:MARGIN] = lax.select(col_even, outer, inner)
     ext_ref[MARGIN:top, top:] = lax.select(col_even, inner, outer)
@@ -136,14 +146,19 @@
     out_ref[:, side - MARGIN :] = lax.select(col_even, inner, outer)
 
 
-def cut_kernel(meta_ref, far_ref, inner_ref, outer_ref, first_inner_ref, first_outer_ref, middle_ref, own_ref):
+def cut_kernel(
+    meta_ref, far_ref, inner_ref, outer_ref, row_inner_ref, row_outer_ref, first_inner_ref, first_outer_ref, middle_ref, own_ref,
+):
     own_ref[...] = far_ref[...]
     side = own_ref.shape[2]
-    col_even = meta_ref[2] % 2 == 0
+    row_even, col_even = meta_ref[1] % 2 == 0, meta_ref[2] % 2 == 0
     for s in range(own_ref.shape[0]):
         low, high = own_ref[s, :, 0:MARGIN], own_ref[s, :, side - MARGIN :]
         inner_ref[s] = lax.select(col_even, high, low)
         outer_ref[s] = lax.select(col_even, low, high)
+        low, high = own_ref[s, 0:MARGIN, :], own_ref[s, side - MARGIN :, :]
+        row_inner_ref[s] = lax.select(row_even, high, low)
+        row_outer_ref[s] = lax.select(row_even, low, high)
     low, high = own_ref[0, :, 0:MARGIN], own_ref[0, :, side - MARGIN :]
     first_inner_ref[0] = lax.select(col_even, high, low)
     first_outer_ref[0] = lax.select(col_even, low, high)
@@ -152,24 +167,22 @@
 
 def edge_kernel(meta_ref, *refs):
     *center_refs, col_inner_ref, col_outer_ref, inner_ref, outer_ref = refs
-    side = col_inner_ref.shape[1]
+    side, wide = col_inner_ref.shape[1], inner_ref.shape[2]
     row_even, col_even = meta_ref[1] % 2 == 0, meta_ref[2] % 2 == 0
     low, high = slice(0, MARGIN), slice(side - MARGIN, side)
     for s in range(inner_ref.shape[0]):
         for ref, even_rows, odd_rows in ((inner_ref, high, low), (outer_ref, low, high)):
-            def pick(source, start, stop):
-                return lax.select(row_even, source[s, even_rows, start:stop], source[s, odd_rows, start:stop])
-
-            inner, outer = pick(col_inner_ref, 0, MARGIN), pick(col_outer_ref, 0, MARGIN)
+            def pick(source):
+                return lax.select(row_even, source[s, even_rows, :], source[s, odd_rows, :])
+
+            inner, outer = pick(col_inner_ref), pick(col_outer_ref)
             ref[s, :, 0:MARGIN] = lax.select(col_even, outer, inner)
-            ref[s, :, side + MARGIN :] = lax.select(col_even, inner, outer)
-            if len(center_refs) == 1:
-                ref[s, :, MARGIN : side + MARGIN] = pick(center_refs[0], 0, side)
-            else:
+            ref[s, :, wide - MARGIN :] = lax.select(col_even, inner, outer)
+            if center_refs:
                 middle_ref, first_inner_ref, first_outer_ref = center_refs
-                inner, outer = pick(first_inner_ref, 0, MARGIN), pick(first_outer_ref, 0, MARGIN)
+                inner, outer = pick(first_inner_ref), pick(first_outer_ref)
                 ref[s, :, MARGIN : 2 * MARGIN] = lax.select(col_even, outer, inner)
-                ref[s, :, 2 * MARGIN : side] = pick(middle_ref, 0, side - 2 * MARGIN)
+                ref[s, :, 2 * MARGIN : side] = pick(middle_ref)
                 ref[s, :, side : side + MARGIN] = lax.select(col_even, inner, outer)
 
 
@@ -218,17 +231,17 @@
 
 def first_kernel(
     meta_ref, table_ref, turned_ref, own_ref, col_inner_ref, col_outer_ref, row_inner_ref, row_outer_ref,
-    part_ref, ext_ref, rows_ref, spec_ref, *, section,
+    corner_inner_ref, corner_outer_ref, part_ref, ext_ref, rows_ref, spec_ref, *, section,
 ):
-    pieces = ((own_ref,), (col_inner_ref, col_outer_ref), (row_inner_ref, row_outer_ref))
+    pieces = ((own_ref,), (col_inner_ref, col_outer_ref), (row_inner_ref, row_outer_ref, corner_inner_ref, corner_outer_ref))
     fill_parts(table_ref, turned_ref, meta_ref, pieces, section, part_ref, ext_ref, rows_ref, spec_ref)
 
 
 def next_kernel(
     meta_ref, prior_ref, order_ref, table_ref, turned_ref, own_ref, col_inner_ref, col_outer_ref, row_inner_ref, row_outer_ref,
-    lag_ref, flow_in_ref, before_ref, part_ref, flow_ref, ext_ref, rows_ref, spec_ref, cross_ref, *, section, sizes,
+    corner_inner_ref, corner_outer_ref, lag_ref, flow_in_ref, before_ref, part_ref, flow_ref, ext_ref, rows_ref, spec_ref, cross_ref, *, section, sizes,
 ):
-    pieces = ((own_ref,), (col_inner_ref, col_outer_ref), (row_inner_ref, row_outer_ref))
+    pieces = ((own_ref,), (col_inner_ref, col_outer_ref), (row_inner_ref, row_outer_ref, corner_inner_ref, corner_outer_ref))
     fill_parts(table_ref, turned_ref, meta_ref, pieces, section, part_ref, ext_ref, rows_ref, spec_ref)
     flow_ref[...] = flow_in_ref[...] + placed_flows(
         meta_ref, prior_ref, order_ref, lag_ref, cross_ref, before_ref, part_ref, section - 1, flow_ref.shape, sizes
@@ -284,24 +297,25 @@
     glue_cost = pl.CostEstimate(flops=GLUE_FLOPS, bytes_accessed=0, transcendentals=0)
     cuts = pl.pallas_call(
         cut_kernel,
-        out_shape=[pixels(sec_count, side, MARGIN)] * 2 + [pixels(1, side, MARGIN)] * 2 + [pixels(1, side, side - HALO), pixels(*sections.shape)],
+        out_shape=[pixels(sec_count, side, MARGIN)] * 2 + [pixels(sec_count, MARGIN, side)] * 2 + [pixels(1, side, MARGIN)] * 2 + [pixels(1, side, side - HALO), pixels(*sections.shape)],
         in_specs=[smem, vmem],
-        out_specs=[vmem] * 6,
+        out_specs=[vmem] * 8,
         compiler_params=small,
         cost_estimate=glue_cost,
         name="cut",
     )(meta, sections)
-    own = cuts[5]
+    own = cuts[7]
     own_cols = (lax.ppermute(cuts[0], "col", col_inner), lax.ppermute(cuts[1], "col", col_outer))
-    first_inner = lax.ppermute(cuts[2], "gz", gz_pairs)
-    first_outer = lax.ppermute(cuts[3], "gz", gz_pairs)
-    middle = lax.ppermute(cuts[4], "gz", gz_pairs)
+    own_rows = (lax.ppermute(cuts[2], "row", row_inner), lax.ppermute(cuts[3], "row", row_outer))
+    first_inner = lax.ppermute(cuts[4], "gz", gz_pairs)
+    first_outer = lax.ppermute(cuts[5], "gz", gz_pairs)
+    middle = lax.ppermute(cuts[6], "gz", gz_pairs)
     last_cols = (lax.ppermute(first_inner, "col", col_inner), lax.ppermute(first_outer, "col", col_outer))
 
-    def edges(count, center, cols):
+    def edges(count, center, cols, width):
         call = pl.pallas_call(
             edge_kernel,
-            out_shape=[pixels(count, MARGIN, wide)] * 2,
+            out_shape=[pixels(count, MARGIN, width)] * 2,
             in_specs=[smem] + [vmem] * (len(center) + 2),
             out_specs=[vmem] * 2,
             compiler_params=small,
@@ -311,8 +325,8 @@
         return lax.ppermute(inner, "row", row_inner), lax.ppermute(outer, "row", row_outer)
 
     last_center = (middle, first_inner, first_outer)
-    own_rows = edges(sec_count, (own,), own_cols)
-    last_rows = edges(1, last_center, last_cols)
+    own_corners = edges(sec_count, (), own_cols, HALO)
+    last_rows = edges(1, last_center, last_cols, wide)
     lanes = (row_order.shape[0] // size_row) * 2 * size_gz * sec_count * size_col * per_side
     devices = size_gz * size_row * size_col
     sizes = (size_gz, size_row, size_col, sec_count, per_side)
@@ -332,11 +346,11 @@
         return pl.CostEstimate(flops=flops, bytes_accessed=place_count * PATCH * PATCH * 4, transcendentals=0)
 
     flow = jnp.zeros((size_row, lanes), jnp.float32)
-    pieces = (own, *own_cols, *own_rows)
+    pieces = (own, *own_cols, *own_rows, *own_corners)
     first_call = pl.pallas_call(
         functools.partial(first_kernel, section=0),
         out_shape=part_shape,
-        in_specs=[smem] + [vmem] * 7,
+        in_specs=[smem] + [vmem] * 9,
         out_specs=vmem,
         scratch_shapes=[ext_scratch, rows_scratch, spec_scratch],
         compiler_params=params,
@@ -348,7 +362,7 @@
         next_call = pl.pallas_call(
             functools.partial(next_kernel, section=section, sizes=sizes),
             out_shape=(part_shape, flow_shape),
-            in_specs=[smem] * 3 + [vmem] * 10,
+            in_specs=[smem] * 3 + [vmem] * 12,
             out_specs=(vmem, vmem),
             scratch_shapes=[ext_scratch, rows_scratch, spec_scratch, cross_scratch],
             compiler_params=params,

time: 52.3 us -> 51.5 us (0.985)
  blocking collectives: 18.6 us -> 13.7 us
  waiting for transfers between devices: 2.87 us -> 6.75 us
    all_to_all x1, blocking collectives: 18.6 us -> 13.7 us  [match(): received = lax.all_to_all(sent, AXES, 0, 0, tiled=True)]
    ppermute x3 -> x5, waiting for transfers between devices: 2.85 us -> 5.07 us  [the longest x1 3.66 us: match(): first_inner = lax.ppermute(cuts[4], 'gz', gz_pairs)]
    ppermute x1, waiting for transfers between devices: 0.01 us -> 1.66 us  [match(): lax.ppermute(first_inner, 'col', col_inner)]
    ppermute x3 -> x5, starting transfers between devices: 3.58 us -> 4.25 us  [the longest x1 1.56 us: match(): first_inner = lax.ppermute(cuts[4], 'gz', gz_pairs)]
  transfers between devices with their start and end apart: 11 -> 13, of which waited for: 1 -> 3; matrix products, arithmetic and copies ran while one was open for 0% -> 0% of each run, Pallas kernels for 13% -> 13%
where the time goes in v4:
time: 51.5 us; the launch traced here: 51.3 us
  starting transfers between devices  17.2 us (33%)
  blocking collectives  13.7 us (27%)
  Pallas kernels  11.3 us (22%)
  waiting for transfers between devices  6.75 us (13%)
  local copies, waits for them, and re-layouts  1.9 us (4%)
    all_to_all x1, blocking collectives, match(): received = lax.all_to_all(sent, AXES, 0, 0, tiled=True)  13.7 us
    ppermute x1, starting transfers between devices, match(): lax.ppermute(first_inner, 'col', col_inner)  4.1 us
    pallas_call x1, Pallas kernels, match(): next_call(meta, priors, row_order, table, turned, *pieces, lag_table, flo...  3.72 us
    ppermute x1, waiting for transfers between devices, match(): first_inner = lax.ppermute(cuts[4], 'gz', gz_pairs)  3.66 us
    pallas_call x1, Pallas kernels, match(): pl.pallas_call(functools.partial(last_kernel, sizes=sizes), out_shape=jax...  3.66 us
    ppermute x1, starting transfers between devices, match(): lax.ppermute(cuts[0], 'col', col_inner)  3.12 us
    ppermute x2, starting transfers between devices, edges(): lax.ppermute(inner, 'row', row_inner)  2.94 us
    pallas_call x1, Pallas kernels, match(): part = first_call(meta, table, turned, *pieces)  1.89 us
  transfers between devices with their start and end apart: 13, of which 3 were waited for; matrix products, arithmetic and copies ran while one was open for 0% of the time, Pallas kernels for 13%

profile of v4, /device:TPU:0, one launch (start us, length us, event | category | flops | bytes accessed | tf_op | source)
XLA Modules:
  0.0 51.3 jit_solution(13877375868796116487)
XLA Ops:
  0.0 0.1 pad_add_fusion.meta_ref
  0.1 1.2 %copy-done.2 = bf16[2,512,512]{2,1,0:T(8,128)(2,1)S(1)} copy-done((bf16[2,512,512]{2,1,0:T(8,128)(2,1)S(1)}, bf16[2,512,512]{2,1,0:T(8,128)(2,1)}, u32[]{:S(2)}) %copy-start.2) | copy-done | bytes 1048600
  1.3 0.8 %cut.1 = (bf16[2,512,128]{2,1,0:T(8,128)(2,1)S(1)}, bf16[2,512,128]{2,1,0:T(8,128)(2,1)S(1)}, bf16[2,128,512]{2,1,0:T(8,128)(2,1)S(1)}, bf16[2,128,512]{2,1,0:T(...) custom-call(s32[3]{0:T(128)S(1)} %pad_add_fusion.meta_ref, ...), custom_call_target="tpu_custom_call" | custom-call | flops 4000000000 | tf_op jit(solution)/shard_map/cut/pallas_call | solution.py:298
  2.1 3.1 %collective-permute-start.7 = (bf16[2,512,128]{2,1,0:T(8,128)(2,1)S(1)}, bf16[2,512,128]{2,1,0:T(8,128)(2,1)S(1)}, u32[]{:S(2)}, u32[]{:S(2)}) collective-permute-start(bf16[2,512,128]{2,1,0:T(8,128)(2,1)S(1)} %get-tuple-element.25), channel_id=1, source_target_pairs={{0,1},{2,3},{1,0},{3,2},{4,5},{6,7},{5,4},{7,6},{8,9},{10,11},{9,8... | collective-permute-start | bytes 786440 | tf_op jit(solution)/shard_map/ppermute | solution.py:308
  5.2 0.7 %collective-permute-start.8 = (bf16[2,512,128]{2,1,0:T(8,128)(2,1)S(1)}, bf16[2,512,128]{2,1,0:T(8,128)(2,1)S(1)}, u32[]{:S(2)}, u32[]{:S(2)}) collective-permute-start(bf16[2,512,128]{2,1,0:T(8,128)(2,1)S(1)} %get-tuple-element.26), channel_id=1, source_target_pairs={{1,2},{2,1},{5,6},{6,5},{9,10},{10,9},{13,14},{14,13},{17,18},{18,... | collective-permute-start | bytes 786440 | tf_op jit(solution)/shard_map/ppermute | solution.py:308
  5.9 1.6 %collective-permute-start.1 = (bf16[1,512,128]{2,1,0:T(8,128)(2,1)S(1)}, bf16[1,512,128]{2,1,0:T(8,128)(2,1)S(1)}, u32[]{:S(2)}, u32[]{:S(2)}) collective-permute-start(bf16[1,512,128]{2,1,0:T(8,128)(2,1)S(1)} %get-tuple-element.20), channel_id=1, source_target_pairs={{0,16},{16,0},{1,17},{17,1},{2,18},{18,2},{3,19},{19,3},{4,20},{20... | collective-permute-start | bytes 393224 | tf_op jit(solution)/shard_map/ppermute | solution.py:310
  7.5 0.5 %collective-permute-start.2 = (bf16[1,512,128]{2,1,0:T(8,128)(2,1)S(1)}, bf16[1,512,128]{2,1,0:T(8,128)(2,1)S(1)}, u32[]{:S(2)}, u32[]{:S(2)}) collective-permute-start(bf16[1,512,128]{2,1,0:T(8,128)(2,1)S(1)} %get-tuple-element.21), channel_id=1, source_target_pairs={{0,16},{16,0},{1,17},{17,1},{2,18},{18,2},{3,19},{19,3},{4,20},{20... | collective-permute-start | bytes 393224 | tf_op jit(solution)/shard_map/ppermute | solution.py:311
  8.0 0.7 %collective-permute-start.10 = (bf16[2,128,512]{2,1,0:T(8,128)(2,1)S(1)}, bf16[2,128,512]{2,1,0:T(8,128)(2,1)S(1)}, u32[]{:S(2)}, u32[]{:S(2)}) collective-permute-start(bf16[2,128,512]{2,1,0:T(8,128)(2,1)S(1)} %get-tuple-element.28), channel_id=1, source_target_pairs={{4,8},{8,4},{5,9},{9,5},{6,10},{10,6},{7,11},{11,7},{20,24},{24,20... | collective-permute-start | bytes 786440 | tf_op jit(solution)/shard_map/ppermute | solution.py:309
  8.7 3.7 %collective-permute-done.1.refs_1_.first_inner_ref = bf16[1,512,128]{2,1,0:T(8,128)(2,1)S(1)} collective-permute-done((bf16[1,512,128]{2,1,0:T(8,128)(2,1)S(1)}, bf16[1,512,128]{2,1,0:T(8,128)(2,1)S(1)}, u32[]{:S(2)}, u32[]{:S(2)}) %collective-permute-start.1) | collective-permute-done | bytes 131104 | tf_op jit(solution)/shard_map/ppermute | solution.py:310
  12.3 0.0 collective-permute-start.9
  12.3 1.4 %collective-permute-done.2.refs_2_.first_outer_ref = bf16[1,512,128]{2,1,0:T(8,128)(2,1)S(1)} collective-permute-done((bf16[1,512,128]{2,1,0:T(8,128)(2,1)S(1)}, bf16[1,512,128]{2,1,0:T(8,128)(2,1)S(1)}, u32[]{:S(2)}, u32[]{:S(2)}) %collective-permute-start.2) | collective-permute-done | bytes 131104 | tf_op jit(solution)/shard_map/ppermute | solution.py:311
  13.7 1.5 %collective-permute-start = (bf16[1,512,256]{2,1,0:T(8,128)(2,1)S(1)}, bf16[1,512,256]{2,1,0:T(8,128)(2,1)S(1)}, u32[]{:S(2)}, u32[]{:S(2)}) collective-permute-start(bf16[1,512,256]{2,1,0:T(8,128)(2,1)S(1)} %get-tuple-element.19), channel_id=1, source_target_pairs={{0,16},{16,0},{1,17},{17,1},{2,18},{18,2},{3,19},{19,3},{4,20},{20... | collective-permute-start | bytes 786440 | tf_op jit(solution)/shard_map/ppermute | solution.py:312
  15.2 0.0 collective-permute-done.7.refs_0_.col_inner_ref
  15.2 4.1 %collective-permute-start.3 = (bf16[1,512,128]{2,1,0:T(8,128)(2,1)S(1)}, bf16[1,512,128]{2,1,0:T(8,128)(2,1)S(1)}, u32[]{:S(2)}, u32[]{:S(2)}) collective-permute-start(bf16[1,512,128]{2,1,0:T(8,128)(2,1)S(1)} %collective-permute-done.1.refs_1_.first_inner_ref), channel_id=1, source_target_pairs={{0,1},{2,3},{1,0},{3,2},{4,5},{6,7},{5,4},{7,6},{8,9},{10,11},{9,8... | collective-permute-start | bytes 393224 | tf_op jit(solution)/shard_map/ppermute | solution.py:313
  19.3 0.7 %collective-permute-start.4 = (bf16[1,512,128]{2,1,0:T(8,128)(2,1)S(1)}, bf16[1,512,128]{2,1,0:T(8,128)(2,1)S(1)}, u32[]{:S(2)}, u32[]{:S(2)}) collective-permute-start(bf16[1,512,128]{2,1,0:T(8,128)(2,1)S(1)} %collective-permute-done.2.refs_2_.first_outer_ref), channel_id=1, source_target_pairs={{1,2},{2,1},{5,6},{6,5},{9,10},{10,9},{13,14},{14,13},{17,18},{18,... | collective-permute-start | bytes 393224 | tf_op jit(solution)/shard_map/ppermute | solution.py:313
  20.0 0.6 %shard_map.65 = (bf16[2,128,256]{2,1,0:T(8,128)(2,1)S(1)}, bf16[2,128,256]{2,1,0:T(8,128)(2,1)S(1)}) custom-call(s32[3]{0:T(128)S(1)} %pad_add_fusion.meta_ref, bf16[2,512,128]{2,1,0:T(8,128)(2,1)S(1)} %collective-permute-done.7.refs_0_.col_inner_ref, bf16[2,512,128]{2,1,0:T(8,128)(2,1)S(1)} %collective-permute-done.8.refs_1_.col_outer_ref), custom_call_target="tpu_custom_call" | custom-call | flops 4000000000 | tf_op jit(solution)/shard_map/pallas_call | solution.py:324
  20.6 1.7 %collective-permute-done.3.refs_3_.col_inner_ref = bf16[1,512,128]{2,1,0:T(8,128)(2,1)S(1)} collective-permute-done((bf16[1,512,128]{2,1,0:T(8,128)(2,1)S(1)}, bf16[1,512,128]{2,1,0:T(8,128)(2,1)S(1)}, u32[]{:S(2)}, u32[]{:S(2)}) %collective-permute-start.3) | collective-permute-done | bytes 131104 | tf_op jit(solution)/shard_map/ppermute | solution.py:313
  22.3 0.0 copy-start.1
  22.3 0.8 %collective-permute-start.12 = (bf16[2,128,256]{2,1,0:T(8,128)(2,1)S(1)}, bf16[2,128,256]{2,1,0:T(8,128)(2,1)S(1)}, u32[]{:S(2)}, u32[]{:S(2)}) collective-permute-start(bf16[2,128,256]{2,1,0:T(8,128)(2,1)S(1)} %get-tuple-element.30), channel_id=1, source_target_pairs={{4,8},{8,4},{5,9},{9,5},{6,10},{10,6},{7,11},{11,7},{20,24},{24,20... | collective-permute-start | bytes 393224 | tf_op jit(solution)/shard_map/ppermute | solution.py:325
  23.1 0.0 collective-permute-done.refs_0_.middle_ref
  23.1 0.6 %shard_map.64 = (bf16[1,128,768]{2,1,0:T(8,128)(2,1)S(1)}, bf16[1,128,768]{2,1,0:T(8,128)(2,1)S(1)}) custom-call(s32[3]{0:T(128)S(1)} %pad_add_fusion.meta_ref, bf16[1,512,256]{2,1,0:T(8,128)(2,1)S(1)} %collective-permute-done.refs_0_.middle_ref, bf16[1,512,128]{2,1,0:T(8,128)(2,1)S(1)} %collective-permute-done.1.refs_1_.first_inner_ref, ...), custom_call_target="tpu_custom_call" | custom-call | flops 4000000000 | tf_op jit(solution)/shard_map/pallas_call | solution.py:324
  23.8 0.0 copy-start.3
  23.8 0.0 copy-start.4
  23.8 0.0 copy-start.5
  23.8 2.9 %collective-permute-start.5 = (bf16[1,128,768]{2,1,0:T(8,128)(2,1)S(1)}, bf16[1,128,768]{2,1,0:T(8,128)(2,1)S(1)}, u32[]{:S(2)}, u32[]{:S(2)}) collective-permute-start(bf16[1,128,768]{2,1,0:T(8,128)(2,1)S(1)} %get-tuple-element.22), channel_id=1, source_target_pairs={{0,4},{8,12},{4,0},{12,8},{1,5},{9,13},{5,1},{13,9},{2,6},{10,14},... | collective-permute-start | bytes 589832 | tf_op jit(solution)/shard_map/ppermute | solution.py:325
  26.8 0.7 %collective-permute-start.6 = (bf16[1,128,768]{2,1,0:T(8,128)(2,1)S(1)}, bf16[1,128,768]{2,1,0:T(8,128)(2,1)S(1)}, u32[]{:S(2)}, u32[]{:S(2)}) collective-permute-start(bf16[1,128,768]{2,1,0:T(8,128)(2,1)S(1)} %get-tuple-element.23), channel_id=1, source_target_pairs={{4,8},{8,4},{5,9},{9,5},{6,10},{10,6},{7,11},{11,7},{20,24},{24,20... | collective-permute-start | bytes 589832 | tf_op jit(solution)/shard_map/ppermute | solution.py:325
  27.5 1.9 %first.1.before_ref = f32[4,512,512]{2,1,0:T(8,128)S(1)} custom-call(s32[3]{0:T(128)S(1)} %pad_add_fusion.meta_ref, bf16[512,256]{1,0:T(8,128)(2,1)S(1)} %copy-done, bf16[256,512]{1,0:T(8,128)(2,1)S(1)} %copy-done.1, bf16[2,512,512]{2,1,0:T(8,128)(2,1)S(1)} %get-tuple-element.24.own_ref, ...), custom_call_target="tpu_custom_call" | custom-call | flops 1879048192 | bytes 4194304 | tf_op jit(solution)/shard_map/first/pallas_call | solution.py:360
  29.4 3.7 %next.1 = (f32[4,512,512]{2,1,0:T(8,128)S(1)}, f32[4,128]{1,0:T(4,128)S(1)}) custom-call(s32[3]{0:T(128)S(1)} %pad_add_fusion.meta_ref, s32[2,2,2,2]{3,2,1,0:T(2,128)S(1)} %copy-done.3, s32[8]{0:T(128)S(1)} %copy-done.4, bf16[512,256]{1,0:T(8,128)(2,1)S(1)} %copy-done, bf16[256,512]{1,0:T(8,128)(2,1)S(1)} %copy-done.1, ...), custom_call_target="tpu_custom_call" | custom-call | flops 2214592512 | bytes 4194304 | tf_op jit(solution)/shard_map/next/pallas_call | solution.py:372
  33.2 3.7 %last.1 = f32[32,128]{1,0:T(8,128)S(1)} custom-call(s32[3]{0:T(128)S(1)} %pad_add_fusion.meta_ref, s32[2,2,2,2]{3,2,1,0:T(2,128)S(1)} %copy-done.3, s32[8]{0:T(128)S(1)} %copy-done.4, bf16[512,256]{1,0:T(8,128)(2,1)S(1)} %copy-done, bf16[256,512]{1,0:T(8,128)(2,1)S(1)} %copy-done.1, f32[4,256,128]{2,1,0:T(8,128)S(1)} %copy-done.5, ...), custom_call_target="tpu_custom_call" | custom-call | flops 2214592512 | bytes 4194304 | tf_op jit(solution)/shard_map/last/pallas_call | solution.py:373
  36.8 13.7 %all_to_all.9 = f32[32,1,128]{2,1,0:T(1,128)S(1)} all-to-all(f32[32,1,128]{2,1,0:T(1,128)S(1)} %bitcast.6), channel_id=1, replica_groups=mesh['gz'=2,'row'=4,'col'=4] {'gz','row','col'}, dimensions={0} | all-to-all | bytes 32768 | tf_op jit(solution)/shard_map/all_to_all | solution.py:383
  50.6 0.1 reduce_sum.9
  50.6 0.6 %reshape.5 = f32[2,64]{1,0:T(2,128)} reshape(f32[128]{0:T(128)S(1)} %reduce_sum.9) | data formatting | bytes 1024 | tf_op jit(solution)/shard_map/reshape | solution.py:384
  (17 shorter events, 0.0 us)
Async XLA Ops:
  0.1 1.2 %copy-start.2 = (bf16[2,512,512]{2,1,0:T(8,128)(2,1)S(1)}, bf16[2,512,512]{2,1,0:T(8,128)(2,1)}, u32[]{:S(2)}) copy-start(bf16[2,512,512]{2,1,0:T(8,128)(2,1)} %far_ref.1) | copy-start | bytes 3145732
  2.1 13.1 %collective-permute-start.7 = (bf16[2,512,128]{2,1,0:T(8,128)(2,1)S(1)}, bf16[2,512,128]{2,1,0:T(8,128)(2,1)S(1)}, u32[]{:S(2)}, u32[]{:S(2)}) collective-permute-start(bf16[2,512,128]{2,1,0:T(8,128)(2,1)S(1)} %get-tuple-element.25), channel_id=1, source_target_pairs={{0,1},{2,3},{1,0},{3,2},{4,5},{6,7},{5,4},{7,6},{8,9},{10,11},{9,8... | collective-permute-start | bytes 786440 | tf_op jit(solution)/shard_map/ppermute | solution.py:308
  5.2 14.1 %collective-permute-start.8 = (bf16[2,512,128]{2,1,0:T(8,128)(2,1)S(1)}, bf16[2,512,128]{2,1,0:T(8,128)(2,1)S(1)}, u32[]{:S(2)}, u32[]{:S(2)}) collective-permute-start(bf16[2,512,128]{2,1,0:T(8,128)(2,1)S(1)} %get-tuple-element.26), channel_id=1, source_target_pairs={{1,2},{2,1},{5,6},{6,5},{9,10},{10,9},{13,14},{14,13},{17,18},{18,... | collective-permute-start | bytes 786440 | tf_op jit(solution)/shard_map/ppermute | solution.py:308
  5.9 6.4 %collective-permute-start.1 = (bf16[1,512,128]{2,1,0:T(8,128)(2,1)S(1)}, bf16[1,512,128]{2,1,0:T(8,128)(2,1)S(1)}, u32[]{:S(2)}, u32[]{:S(2)}) collective-permute-start(bf16[1,512,128]{2,1,0:T(8,128)(2,1)S(1)} %get-tuple-element.20), channel_id=1, source_target_pairs={{0,16},{16,0},{1,17},{17,1},{2,18},{18,2},{3,19},{19,3},{4,20},{20... | collective-permute-start | bytes 393224 | tf_op jit(solution)/shard_map/ppermute | solution.py:310
  7.5 6.3 %collective-permute-start.2 = (bf16[1,512,128]{2,1,0:T(8,128)(2,1)S(1)}, bf16[1,512,128]{2,1,0:T(8,128)(2,1)S(1)}, u32[]{:S(2)}, u32[]{:S(2)}) collective-permute-start(bf16[1,512,128]{2,1,0:T(8,128)(2,1)S(1)} %get-tuple-element.21), channel_id=1, source_target_pairs={{0,16},{16,0},{1,17},{17,1},{2,18},{18,2},{3,19},{19,3},{4,20},{20... | collective-permute-start | bytes 393224 | tf_op jit(solution)/shard_map/ppermute | solution.py:311
  8.0 18.7 %collective-permute-start.10 = (bf16[2,128,512]{2,1,0:T(8,128)(2,1)S(1)}, bf16[2,128,512]{2,1,0:T(8,128)(2,1)S(1)}, u32[]{:S(2)}, u32[]{:S(2)}) collective-permute-start(bf16[2,128,512]{2,1,0:T(8,128)(2,1)S(1)} %get-tuple-element.28), channel_id=1, source_target_pairs={{4,8},{8,4},{5,9},{9,5},{6,10},{10,6},{7,11},{11,7},{20,24},{24,20... | collective-permute-start | bytes 786440 | tf_op jit(solution)/shard_map/ppermute | solution.py:309
  12.3 15.1 %collective-permute-start.9 = (bf16[2,128,512]{2,1,0:T(8,128)(2,1)S(1)}, bf16[2,128,512]{2,1,0:T(8,128)(2,1)S(1)}, u32[]{:S(2)}, u32[]{:S(2)}) collective-permute-start(bf16[2,128,512]{2,1,0:T(8,128)(2,1)S(1)} %get-tuple-element.27), channel_id=1, source_target_pairs={{0,4},{8,12},{4,0},{12,8},{1,5},{9,13},{5,1},{13,9},{2,6},{10,14},... | collective-permute-start | bytes 786440 | tf_op jit(solution)/shard_map/ppermute | solution.py:309
  13.7 9.4 %collective-permute-start = (bf16[1,512,256]{2,1,0:T(8,128)(2,1)S(1)}, bf16[1,512,256]{2,1,0:T(8,128)(2,1)S(1)}, u32[]{:S(2)}, u32[]{:S(2)}) collective-permute-start(bf16[1,512,256]{2,1,0:T(8,128)(2,1)S(1)} %get-tuple-element.19), channel_id=1, source_target_pairs={{0,16},{16,0},{1,17},{17,1},{2,18},{18,2},{3,19},{19,3},{4,20},{20... | collective-permute-start | bytes 786440 | tf_op jit(solution)/shard_map/ppermute | solution.py:312
  15.2 7.0 %collective-permute-start.3 = (bf16[1,512,128]{2,1,0:T(8,128)(2,1)S(1)}, bf16[1,512,128]{2,1,0:T(8,128)(2,1)S(1)}, u32[]{:S(2)}, u32[]{:S(2)}) collective-permute-start(bf16[1,512,128]{2,1,0:T(8,128)(2,1)S(1)} %collective-permute-done.1.refs_1_.first_inner_ref), channel_id=1, source_target_pairs={{0,1},{2,3},{1,0},{3,2},{4,5},{6,7},{5,4},{7,6},{8,9},{10,11},{9,8... | collective-permute-start | bytes 393224 | tf_op jit(solution)/shard_map/ppermute | solution.py:313
  19.3 2.9 %collective-permute-start.4 = (bf16[1,512,128]{2,1,0:T(8,128)(2,1)S(1)}, bf16[1,512,128]{2,1,0:T(8,128)(2,1)S(1)}, u32[]{:S(2)}, u32[]{:S(2)}) collective-permute-start(bf16[1,512,128]{2,1,0:T(8,128)(2,1)S(1)} %collective-permute-done.2.refs_2_.first_outer_ref), channel_id=1, source_target_pairs={{1,2},{2,1},{5,6},{6,5},{9,10},{10,9},{13,14},{14,13},{17,18},{18,... | collective-permute-start | bytes 393224 | tf_op jit(solution)/shard_map/ppermute | solution.py:313
  22.3 5.1 %collective-permute-start.11 = (bf16[2,128,256]{2,1,0:T(8,128)(2,1)S(1)}, bf16[2,128,256]{2,1,0:T(8,128)(2,1)S(1)}, u32[]{:S(2)}, u32[]{:S(2)}) collective-permute-start(bf16[2,128,256]{2,1,0:T(8,128)(2,1)S(1)} %get-tuple-element.29), channel_id=1, source_target_pairs={{0,4},{8,12},{4,0},{12,8},{1,5},{9,13},{5,1},{13,9},{2,6},{10,14},... | collective-permute-start | bytes 393224 | tf_op jit(solution)/shard_map/ppermute | solution.py:325
  22.3 5.2 %copy-start = (bf16[512,256]{1,0:T(8,128)(2,1)S(1)}, bf16[512,256]{1,0:T(8,128)(2,1)}, u32[]{:S(2)}) copy-start(bf16[512,256]{1,0:T(8,128)(2,1)} %constant.26.table_ref) | copy-start | bytes 786436
  22.3 5.2 %copy-start.1 = (bf16[256,512]{1,0:T(8,128)(2,1)S(1)}, bf16[256,512]{1,0:T(8,128)(2,1)}, u32[]{:S(2)}) copy-start(bf16[256,512]{1,0:T(8,128)(2,1)} %constant.27.turned_ref) | copy-start | bytes 786436
  22.3 5.1 %collective-permute-start.12 = (bf16[2,128,256]{2,1,0:T(8,128)(2,1)S(1)}, bf16[2,128,256]{2,1,0:T(8,128)(2,1)S(1)}, u32[]{:S(2)}, u32[]{:S(2)}) collective-permute-start(bf16[2,128,256]{2,1,0:T(8,128)(2,1)S(1)} %get-tuple-element.30), channel_id=1, source_target_pairs={{4,8},{8,4},{5,9},{9,5},{6,10},{10,6},{7,11},{11,7},{20,24},{24,20... | collective-permute-start | bytes 393224 | tf_op jit(solution)/shard_map/ppermute | solution.py:325
  23.8 5.6 %copy-start.3 = (s32[2,2,2,2]{3,2,1,0:T(2,128)S(1)}, s32[2,2,2,2]{3,2,1,0:T(2,128)}, u32[]{:S(2)}) copy-start(s32[2,2,2,2]{3,2,1,0:T(2,128)} %prior_ref.3) | copy-start | bytes 196
  23.8 5.6 %copy-start.4 = (s32[8]{0:T(128)S(1)}, s32[8]{0:T(128)}, u32[]{:S(2)}) copy-start(s32[8]{0:T(128)} %order_ref.3) | copy-start | bytes 100
  23.8 5.6 %copy-start.5 = (f32[4,256,128]{2,1,0:T(8,128)S(1)}, f32[4,256,128]{2,1,0:T(8,128)}, u32[]{:S(2)}) copy-start(f32[4,256,128]{2,1,0:T(8,128)} %constant.29.lag_ref) | copy-start | bytes 1572868
  23.8 9.3 %collective-permute-start.5 = (bf16[1,128,768]{2,1,0:T(8,128)(2,1)S(1)}, bf16[1,128,768]{2,1,0:T(8,128)(2,1)S(1)}, u32[]{:S(2)}, u32[]{:S(2)}) collective-permute-start(bf16[1,128,768]{2,1,0:T(8,128)(2,1)S(1)} %get-tuple-element.22), channel_id=1, source_target_pairs={{0,4},{8,12},{4,0},{12,8},{1,5},{9,13},{5,1},{13,9},{2,6},{10,14},... | collective-permute-start | bytes 589832 | tf_op jit(solution)/shard_map/ppermute | solution.py:325
  26.8 6.4 %collective-permute-start.6 = (bf16[1,128,768]{2,1,0:T(8,128)(2,1)S(1)}, bf16[1,128,768]{2,1,0:T(8,128)(2,1)S(1)}, u32[]{:S(2)}, u32[]{:S(2)}) collective-permute-start(bf16[1,128,768]{2,1,0:T(8,128)(2,1)S(1)} %get-tuple-element.23), channel_id=1, source_target_pairs={{4,8},{8,4},{5,9},{9,5},{6,10},{10,6},{7,11},{11,7},{20,24},{24,20... | collective-permute-start | bytes 589832 | tf_op jit(solution)/shard_map/ppermute | solution.py:325

commit v5 on v4

--- a/solution.py
+++ b/solution.py
@@ -19,6 +19,7 @@
 MARGIN = HALO // 2
 AXES = ("gz", "row", "col")
 VMEM_LIMIT = 16 * 1024 * 1024
+CHUNK = 16
 GLUE_FLOPS = 4 * 10**9
 
 
@@ -40,11 +41,8 @@
     for k_odd in range(2):
         for l_odd in range(2):
             cols = slice(l_odd * HALF, l_odd * HALF + quarter)
-            if k_odd == 0:
-                yield slice(0, 16), cols
-                yield slice(16, quarter), cols
-            else:
-                yield slice(HALF, HALF + quarter), cols
+            for start in range(0, quarter, CHUNK):
+                yield slice(k_odd * HALF + start, k_odd * HALF + start + CHUNK), cols
 
 
 def sines(part):
@@ -97,10 +95,14 @@
     return jnp.concatenate(pieces, axis=1).astype(jnp.bfloat16)
 
 
-def fill_parts(table_ref, turned_ref, meta_ref, pieces, s, out_ref, ext_ref, rows_ref, spec_ref):
+def is_even(axis):
+    return lax.axis_index(axis) % 2 == 0
+
+
+def fill_parts(table_ref, turned_ref, pieces, s, out_ref, ext_ref, rows_ref, spec_ref):
     center_refs, col_refs, row_refs = pieces
     top = ext_ref.shape[0] - MARGIN
-    row_even, col_even = meta_ref[1] % 2 == 0, meta_ref[2] % 2 == 0
+    row_even, col_even = is_even("row"), is_even("col")
     if len(row_refs) == 2:
         spans = ((row_refs, slice(None), slice(None)),)
     else:
@@ -147,11 +149,11 @@
 
 
 def cut_kernel(
-    meta_ref, far_ref, inner_ref, outer_ref, row_inner_ref, row_outer_ref, first_inner_ref, first_outer_ref, middle_ref, own_ref,
+    far_ref, inner_ref, outer_ref, row_inner_ref, row_outer_ref, first_inner_ref, first_outer_ref, middle_ref, own_ref,
 ):
     own_ref[...] = far_ref[...]
     side = own_ref.shape[2]
-    row_even, col_even = meta_ref[1] % 2 == 0, meta_ref[2] % 2 == 0
+    row_even, col_even = is_even("row"), is_even("col")
     for s in range(own_ref.shape[0]):
         low, high = own_ref[s, :, 0:MARGIN], own_ref[s, :, side - MARGIN :]
         inner_ref[s] = lax.select(col_even, high, low)
@@ -165,10 +167,10 @@
     middle_ref[0] = own_ref[0, :, MARGIN : side - MARGIN]
 
 
-def edge_kernel(meta_ref, *refs):
+def edge_kernel(*refs):
     *center_refs, col_inner_ref, col_outer_ref, inner_ref, outer_ref = refs
     side, wide = col_inner_ref.shape[1], inner_ref.shape[2]
-    row_even, col_even = meta_ref[1] % 2 == 0, meta_ref[2] % 2 == 0
+    row_even, col_even = is_even("row"), is_even("col")
     low, high = slice(0, MARGIN), slice(side - MARGIN, side)
     for s in range(inner_ref.shape[0]):
         for ref, even_rows, odd_rows in ((inner_ref, high, low), (outer_ref, low, high)):
@@ -186,7 +188,7 @@
                 ref[s, :, side : side + MARGIN] = lax.select(col_even, inner, outer)
 
 
-def placed_flows(meta_ref, prior_ref, order_ref, lag_ref, cross_ref, first_ref, second_ref, s, shape, sizes):
+def placed_flows(prior_ref, order_ref, lag_ref, cross_ref, first_ref, second_ref, s, shape, sizes):
     size_gz, size_row, size_col, sec_count, per_side = sizes
     place_count = per_side * per_side
     lanes_each = 2 * size_gz * sec_count * size_col * per_side
@@ -199,7 +201,7 @@
         here = jnp.logical_and(holder == m // rows_each, lane // lanes_each == m % rows_each)
         slot = jnp.where(here, order_ref[m], slot)
     lane = lane % lanes_each
-    my_gz, my_row, my_col = meta_ref[0], meta_ref[1], meta_ref[2]
+    my_gz, my_row, my_col = (lax.axis_index(a) for a in AXES)
     total_out = jnp.zeros(shape, jnp.float32)
     scale = 2.0 / float(PATCH) ** 3
     down = (lax.broadcasted_iota(jnp.int32, (LAGS, LAGS), 0) - LAGS // 2).astype(jnp.float32)
@@ -230,34 +232,52 @@
 
 
 def first_kernel(
-    meta_ref, table_ref, turned_ref, own_ref, col_inner_ref, col_outer_ref, row_inner_ref, row_outer_ref,
+    table_ref, turned_ref, own_ref, col_inner_ref, col_outer_ref, row_inner_ref, row_outer_ref,
     corner_inner_ref, corner_outer_ref, part_ref, ext_ref, rows_ref, spec_ref, *, section,
 ):
     pieces = ((own_ref,), (col_inner_ref, col_outer_ref), (row_inner_ref, row_outer_ref, corner_inner_ref, corner_outer_ref))
-    fill_parts(table_ref, turned_ref, meta_ref, pieces, section, part_ref, ext_ref, rows_ref, spec_ref)
+    fill_parts(table_ref, turned_ref, pieces, section, part_ref, ext_ref, rows_ref, spec_ref)
 
 
 def next_kernel(
-    meta_ref, prior_ref, order_ref, table_ref, turned_ref, own_ref, col_inner_ref, col_outer_ref, row_inner_ref, row_outer_ref,
-    corner_inner_ref, corner_outer_ref, lag_ref, flow_in_ref, before_ref, part_ref, flow_ref, ext_ref, rows_ref, spec_ref, cross_ref, *, section, sizes,
+    far_prior_ref, far_order_ref, table_ref, turned_ref, own_ref, col_inner_ref, col_outer_ref, row_inner_ref, row_outer_ref,
+    corner_inner_ref, corner_outer_ref, lag_ref, flow_in_ref, before_ref, part_ref, flow_ref, ext_ref, rows_ref, spec_ref, cross_ref, prior_ref, order_ref, sems,
+    *, section, sizes,
 ):
     pieces = ((own_ref,), (col_inner_ref, col_outer_ref), (row_inner_ref, row_outer_ref, corner_inner_ref, corner_outer_ref))
-    fill_parts(table_ref, turned_ref, meta_ref, pieces, section, part_ref, ext_ref, rows_ref, spec_ref)
+    copies = (
+        pltpu.make_async_copy(far_prior_ref, prior_ref, sems.at[0]),
+        pltpu.make_async_copy(far_order_ref, order_ref, sems.at[1]),
+    )
+    for copy in copies:
+        copy.start()
+    fill_parts(table_ref, turned_ref, pieces, section, part_ref, ext_ref, rows_ref, spec_ref)
+    for copy in copies:
+        copy.wait()
     flow_ref[...] = flow_in_ref[...] + placed_flows(
-        meta_ref, prior_ref, order_ref, lag_ref, cross_ref, before_ref, part_ref, section - 1, flow_ref.shape, sizes
+        prior_ref, order_ref, lag_ref, cross_ref, before_ref, part_ref, section - 1, flow_ref.shape, sizes
     )
 
 
 def last_kernel(
-    meta_ref, prior_ref, order_ref, table_ref, turned_ref, lag_ref, middle_ref, first_inner_ref, first_outer_ref, col_inner_ref, col_outer_ref,
-    row_inner_ref, row_outer_ref, flow_ref, first_ref, out_ref, ext_ref, rows_ref, spec_ref, part_ref, cross_ref, *, sizes,
+    far_prior_ref, far_order_ref, table_ref, turned_ref, lag_ref, middle_ref, first_inner_ref, first_outer_ref, col_inner_ref, col_outer_ref,
+    row_inner_ref, row_outer_ref, flow_ref, first_ref, out_ref, ext_ref, rows_ref, spec_ref, part_ref, cross_ref, prior_ref, order_ref, sems,
+    *, sizes,
 ):
     size_gz, size_row, size_col, sec_count, _ = sizes
     center = (middle_ref, first_inner_ref, first_outer_ref)
     pieces = (center, (col_inner_ref, col_outer_ref), (row_inner_ref, row_outer_ref))
-    fill_parts(table_ref, turned_ref, meta_ref, pieces, 0, part_ref, ext_ref, rows_ref, spec_ref)
+    copies = (
+        pltpu.make_async_copy(far_prior_ref, prior_ref, sems.at[0]),
+        pltpu.make_async_copy(far_order_ref, order_ref, sems.at[1]),
+    )
+    for copy in copies:
+        copy.start()
+    fill_parts(table_ref, turned_ref, pieces, 0, part_ref, ext_ref, rows_ref, spec_ref)
+    for copy in copies:
+        copy.wait()
     flow = flow_ref[...] + placed_flows(
-        meta_ref, prior_ref, order_ref, lag_ref, cross_ref, first_ref, part_ref, sec_count - 1, flow_ref.shape, sizes
+        prior_ref, order_ref, lag_ref, cross_ref, first_ref, part_ref, sec_count - 1, flow_ref.shape, sizes
     )
     for g in range(size_gz):
         for r in range(size_row):
@@ -281,10 +301,9 @@
     turned = jnp.asarray(table.T).astype(jnp.bfloat16)
     table = jnp.asarray(table).astype(jnp.bfloat16)
     lag_table = jnp.asarray(np.stack(np.split(lag_table, PATCH // 128, axis=1))).astype(jnp.bfloat16).astype(jnp.float32)
-    meta = jnp.stack([lax.axis_index(a) for a in AXES]).astype(jnp.int32)
     wide = side + HALO
     vmem = pl.BlockSpec(memory_space=pltpu.VMEM)
-    smem = pl.BlockSpec(memory_space=pltpu.SMEM)
+    far = pl.BlockSpec(memory_space=pl.ANY)
     params = pltpu.CompilerParams(vmem_limit_bytes=VMEM_LIMIT)
     small = pltpu.CompilerParams(vmem_limit_bytes=VMEM_LIMIT // 4)
 
@@ -298,12 +317,12 @@
     cuts = pl.pallas_call(
         cut_kernel,
         out_shape=[pixels(sec_count, side, MARGIN)] * 2 + [pixels(sec_count, MARGIN, side)] * 2 + [pixels(1, side, MARGIN)] * 2 + [pixels(1, side, side - HALO), pixels(*sections.shape)],
-        in_specs=[smem, vmem],
+        in_specs=[vmem],
         out_specs=[vmem] * 8,
         compiler_params=small,
         cost_estimate=glue_cost,
         name="cut",
-    )(meta, sections)
+    )(sections)
     own = cuts[7]
     own_cols = (lax.ppermute(cuts[0], "col", col_inner), lax.ppermute(cuts[1], "col", col_outer))
     own_rows = (lax.ppermute(cuts[2], "row", row_inner), lax.ppermute(cuts[3], "row", row_outer))
@@ -316,12 +335,12 @@
         call = pl.pallas_call(
             edge_kernel,
             out_shape=[pixels(count, MARGIN, width)] * 2,
-            in_specs=[smem] + [vmem] * (len(center) + 2),
+            in_specs=[vmem] * (len(center) + 2),
             out_specs=[vmem] * 2,
             compiler_params=small,
             cost_estimate=glue_cost,
         )
-        inner, outer = call(meta, *center, *cols)
+        inner, outer = call(*center, *cols)
         return lax.ppermute(inner, "row", row_inner), lax.ppermute(outer, "row", row_outer)
 
     last_center = (middle, first_inner, first_outer)
@@ -338,6 +357,11 @@
     rows_scratch = pltpu.VMEM((per_side, wide, PATCH), jnp.bfloat16)
     spec_scratch = pltpu.VMEM((2, PATCH, PATCH), jnp.float32)
     part_scratch = pltpu.VMEM(parts, jnp.float32)
+    scalars = [
+        pltpu.SMEM(priors.shape, priors.dtype),
+        pltpu.SMEM(row_order.shape, row_order.dtype),
+        pltpu.SemaphoreType.DMA((2,)),
+    ]
     cross_scratch = pltpu.VMEM((place_count, PATCH, PATCH), jnp.bfloat16)
     spectra_cost = 2 * per_side * wide * PATCH * PATCH + 2 * place_count * PATCH**3
     pair_cost = 2 * place_count * PATCH * LAGS * (PATCH + LAGS)
@@ -350,36 +374,36 @@
     first_call = pl.pallas_call(
         functools.partial(first_kernel, section=0),
         out_shape=part_shape,
-        in_specs=[smem] + [vmem] * 9,
+        in_specs=[vmem] * 9,
         out_specs=vmem,
         scratch_shapes=[ext_scratch, rows_scratch, spec_scratch],
         compiler_params=params,
         cost_estimate=cost(spectra_cost),
         name="first",
     )
-    part = first_call(meta, table, turned, *pieces)
+    part = first_call(table, turned, *pieces)
     for section in range(1, sec_count):
         next_call = pl.pallas_call(
             functools.partial(next_kernel, section=section, sizes=sizes),
             out_shape=(part_shape, flow_shape),
-            in_specs=[smem] * 3 + [vmem] * 12,
+            in_specs=[far] * 2 + [vmem] * 12,
             out_specs=(vmem, vmem),
-            scratch_shapes=[ext_scratch, rows_scratch, spec_scratch, cross_scratch],
+            scratch_shapes=[ext_scratch, rows_scratch, spec_scratch, cross_scratch, *scalars],
             compiler_params=params,
             cost_estimate=cost(spectra_cost + pair_cost),
             name="next",
         )
-        part, flow = next_call(meta, priors, row_order, table, turned, *pieces, lag_table, flow, part)
+        part, flow = next_call(priors, row_order, table, turned, *pieces, lag_table, flow, part)
     sent = pl.pallas_call(
         functools.partial(last_kernel, sizes=sizes),
         out_shape=jax.ShapeDtypeStruct((devices, lanes), jnp.float32),
-        in_specs=[smem] * 3 + [vmem] * 12,
+        in_specs=[far] * 2 + [vmem] * 12,
         out_specs=vmem,
-        scratch_shapes=[ext_scratch, rows_scratch, spec_scratch, part_scratch, cross_scratch],
+        scratch_shapes=[ext_scratch, rows_scratch, spec_scratch, part_scratch, cross_scratch, *scalars],
         compiler_params=params,
         cost_estimate=cost(spectra_cost + pair_cost),
         name="last",
-    )(meta, priors, row_order, table, turned, lag_table, *last_center, *last_cols, *last_rows, flow, part)
+    )(priors, row_order, table, turned, lag_table, *last_center, *last_cols, *last_rows, flow, part)
     received = lax.all_to_all(sent, AXES, 0, 0, tiled=True)
     return jnp.sum(received, axis=0).reshape(row_order.shape[0] // size_row, -1)
 

time: 51.5 us -> 48.5 us (0.942)
  Pallas kernels: 11.3 us -> 7.55 us
  waiting for transfers between devices: 6.75 us -> 7.28 us
    pallas_call x4, Pallas kernels: 6.85 us -> 4.36 us  [the longest x1 2.86 us: match(): next_call(priors, row_order, table, turned, *pieces, lag_table, flow, part)]
    pallas_call x1, Pallas kernels: 3.66 us -> 2.91 us  [match(): pl.pallas_call(functools.partial(last_kernel, sizes=sizes), out_shape=jax...]
    pallas_call x1, Pallas kernels: 0.81 us -> 0.27 us  [match(): pl.pallas_call(cut_kernel, out_shape=[pixels(sec_count, side, MARGIN)] *...]
    ppermute x1, waiting for transfers between devices: 1.66 us -> 2.2 us  [match(): lax.ppermute(first_inner, 'col', col_inner)]
  transfers between devices with their start and end apart: 13 -> 13, of which waited for: 3 -> 3; matrix products, arithmetic and copies ran while one was open for 0% -> 0% of each run, Pallas kernels for 13% -> 9%
where the time goes in v5:
time: 48.5 us; the launch traced here: 48.2 us
  starting transfers between devices  17.2 us (35%)
  blocking collectives  14 us (29%)
  Pallas kernels  7.55 us (16%)
  waiting for transfers between devices  7.28 us (15%)
  local copies, waits for them, and re-layouts  1.9 us (4%)
    all_to_all x1, blocking collectives, match(): received = lax.all_to_all(sent, AXES, 0, 0, tiled=True)  14 us
    ppermute x1, starting transfers between devices, match(): lax.ppermute(first_inner, 'col', col_inner)  4.1 us
    ppermute x1, waiting for transfers between devices, match(): first_inner = lax.ppermute(cuts[4], 'gz', gz_pairs)  3.66 us
    ppermute x1, starting transfers between devices, match(): lax.ppermute(cuts[0], 'col', col_inner)  3.12 us
    ppermute x2, starting transfers between devices, edges(): lax.ppermute(inner, 'row', row_inner)  2.94 us
    pallas_call x1, Pallas kernels, match(): pl.pallas_call(functools.partial(last_kernel, sizes=sizes), out_shape=jax...  2.91 us
    pallas_call x1, Pallas kernels, match(): next_call(priors, row_order, table, turned, *pieces, lag_table, flow, part)  2.86 us
    ppermute x1, waiting for transfers between devices, match(): lax.ppermute(first_inner, 'col', col_inner)  2.2 us
  transfers between devices with their start and end apart: 13, of which 3 were waited for; matrix products, arithmetic and copies ran while one was open for 0% of the time, Pallas kernels for 9%

profile of v5, /device:TPU:0, one launch (start us, length us, event | category | flops | bytes accessed | tf_op | source)
XLA Modules:
  0.0 48.2 jit_solution(2369084738550863701)
XLA Ops:
  0.0 1.2 %copy-done.2 = bf16[2,512,512]{2,1,0:T(8,128)(2,1)S(1)} copy-done((bf16[2,512,512]{2,1,0:T(8,128)(2,1)S(1)}, bf16[2,512,512]{2,1,0:T(8,128)(2,1)}, u32[]{:S(2)}) %copy-start.2) | copy-done | bytes 1048600
  1.2 0.3 cut.1
  1.5 3.1 %collective-permute-start.7 = (bf16[2,512,128]{2,1,0:T(8,128)(2,1)S(1)}, bf16[2,512,128]{2,1,0:T(8,128)(2,1)S(1)}, u32[]{:S(2)}, u32[]{:S(2)}) collective-permute-start(bf16[2,512,128]{2,1,0:T(8,128)(2,1)S(1)} %get-tuple-element.25), channel_id=1, source_target_pairs={{0,1},{2,3},{1,0},{3,2},{4,5},{6,7},{5,4},{7,6},{8,9},{10,11},{9,8... | collective-permute-start | bytes 786440 | tf_op jit(solution)/shard_map/ppermute | solution.py:327
  4.6 0.7 %collective-permute-start.8 = (bf16[2,512,128]{2,1,0:T(8,128)(2,1)S(1)}, bf16[2,512,128]{2,1,0:T(8,128)(2,1)S(1)}, u32[]{:S(2)}, u32[]{:S(2)}) collective-permute-start(bf16[2,512,128]{2,1,0:T(8,128)(2,1)S(1)} %get-tuple-element.26), channel_id=1, source_target_pairs={{1,2},{2,1},{5,6},{6,5},{9,10},{10,9},{13,14},{14,13},{17,18},{18,... | collective-permute-start | bytes 786440 | tf_op jit(solution)/shard_map/ppermute | solution.py:327
  5.3 1.6 %collective-permute-start.1 = (bf16[1,512,128]{2,1,0:T(8,128)(2,1)S(1)}, bf16[1,512,128]{2,1,0:T(8,128)(2,1)S(1)}, u32[]{:S(2)}, u32[]{:S(2)}) collective-permute-start(bf16[1,512,128]{2,1,0:T(8,128)(2,1)S(1)} %get-tuple-element.20), channel_id=1, source_target_pairs={{0,16},{16,0},{1,17},{17,1},{2,18},{18,2},{3,19},{19,3},{4,20},{20... | collective-permute-start | bytes 393224 | tf_op jit(solution)/shard_map/ppermute | solution.py:329
  6.8 0.5 %collective-permute-start.2 = (bf16[1,512,128]{2,1,0:T(8,128)(2,1)S(1)}, bf16[1,512,128]{2,1,0:T(8,128)(2,1)S(1)}, u32[]{:S(2)}, u32[]{:S(2)}) collective-permute-start(bf16[1,512,128]{2,1,0:T(8,128)(2,1)S(1)} %get-tuple-element.21), channel_id=1, source_target_pairs={{0,16},{16,0},{1,17},{17,1},{2,18},{18,2},{3,19},{19,3},{4,20},{20... | collective-permute-start | bytes 393224 | tf_op jit(solution)/shard_map/ppermute | solution.py:330
  7.4 0.7 %collective-permute-start.10 = (bf16[2,128,512]{2,1,0:T(8,128)(2,1)S(1)}, bf16[2,128,512]{2,1,0:T(8,128)(2,1)S(1)}, u32[]{:S(2)}, u32[]{:S(2)}) collective-permute-start(bf16[2,128,512]{2,1,0:T(8,128)(2,1)S(1)} %get-tuple-element.28), channel_id=1, source_target_pairs={{4,8},{8,4},{5,9},{9,5},{6,10},{10,6},{7,11},{11,7},{20,24},{24,20... | collective-permute-start | bytes 786440 | tf_op jit(solution)/shard_map/ppermute | solution.py:328
  8.1 3.7 %collective-permute-done.1.refs_1_.first_inner_ref = bf16[1,512,128]{2,1,0:T(8,128)(2,1)S(1)} collective-permute-done((bf16[1,512,128]{2,1,0:T(8,128)(2,1)S(1)}, bf16[1,512,128]{2,1,0:T(8,128)(2,1)S(1)}, u32[]{:S(2)}, u32[]{:S(2)}) %collective-permute-start.1) | collective-permute-done | bytes 131104 | tf_op jit(solution)/shard_map/ppermute | solution.py:329
  11.7 1.4 %collective-permute-done.2.refs_2_.first_outer_ref = bf16[1,512,128]{2,1,0:T(8,128)(2,1)S(1)} collective-permute-done((bf16[1,512,128]{2,1,0:T(8,128)(2,1)S(1)}, bf16[1,512,128]{2,1,0:T(8,128)(2,1)S(1)}, u32[]{:S(2)}, u32[]{:S(2)}) %collective-permute-start.2) | collective-permute-done | bytes 131104 | tf_op jit(solution)/shard_map/ppermute | solution.py:330
  13.1 1.5 %collective-permute-start = (bf16[1,512,256]{2,1,0:T(8,128)(2,1)S(1)}, bf16[1,512,256]{2,1,0:T(8,128)(2,1)S(1)}, u32[]{:S(2)}, u32[]{:S(2)}) collective-permute-start(bf16[1,512,256]{2,1,0:T(8,128)(2,1)S(1)} %get-tuple-element.19), channel_id=1, source_target_pairs={{0,16},{16,0},{1,17},{17,1},{2,18},{18,2},{3,19},{19,3},{4,20},{20... | collective-permute-start | bytes 786440 | tf_op jit(solution)/shard_map/ppermute | solution.py:331
  14.6 0.0 collective-permute-done.7.refs_0_.col_inner_ref
  14.6 4.1 %collective-permute-start.3 = (bf16[1,512,128]{2,1,0:T(8,128)(2,1)S(1)}, bf16[1,512,128]{2,1,0:T(8,128)(2,1)S(1)}, u32[]{:S(2)}, u32[]{:S(2)}) collective-permute-start(bf16[1,512,128]{2,1,0:T(8,128)(2,1)S(1)} %collective-permute-done.1.refs_1_.first_inner_ref), channel_id=1, source_target_pairs={{0,1},{2,3},{1,0},{3,2},{4,5},{6,7},{5,4},{7,6},{8,9},{10,11},{9,8... | collective-permute-start | bytes 393224 | tf_op jit(solution)/shard_map/ppermute | solution.py:332
  18.7 0.0 collective-permute-done.8.refs_1_.col_outer_ref
  18.7 0.7 %collective-permute-start.4 = (bf16[1,512,128]{2,1,0:T(8,128)(2,1)S(1)}, bf16[1,512,128]{2,1,0:T(8,128)(2,1)S(1)}, u32[]{:S(2)}, u32[]{:S(2)}) collective-permute-start(bf16[1,512,128]{2,1,0:T(8,128)(2,1)S(1)} %collective-permute-done.2.refs_2_.first_outer_ref), channel_id=1, source_target_pairs={{1,2},{2,1},{5,6},{6,5},{9,10},{10,9},{13,14},{14,13},{17,18},{18,... | collective-permute-start | bytes 393224 | tf_op jit(solution)/shard_map/ppermute | solution.py:332
  19.4 0.1 shard_map.65
  19.5 2.2 %collective-permute-done.3.refs_3_.col_inner_ref = bf16[1,512,128]{2,1,0:T(8,128)(2,1)S(1)} collective-permute-done((bf16[1,512,128]{2,1,0:T(8,128)(2,1)S(1)}, bf16[1,512,128]{2,1,0:T(8,128)(2,1)S(1)}, u32[]{:S(2)}, u32[]{:S(2)}) %collective-permute-start.3) | collective-permute-done | bytes 131104 | tf_op jit(solution)/shard_map/ppermute | solution.py:332
  21.7 0.0 collective-permute-start.11
  21.7 0.0 collective-permute-done.4.refs_4_.col_outer_ref
  21.7 0.0 copy-start.1
  21.7 0.8 %collective-permute-start.12 = (bf16[2,128,256]{2,1,0:T(8,128)(2,1)S(1)}, bf16[2,128,256]{2,1,0:T(8,128)(2,1)S(1)}, u32[]{:S(2)}, u32[]{:S(2)}) collective-permute-start(bf16[2,128,256]{2,1,0:T(8,128)(2,1)S(1)} %get-tuple-element.30), channel_id=1, source_target_pairs={{4,8},{8,4},{5,9},{9,5},{6,10},{10,6},{7,11},{11,7},{20,24},{24,20... | collective-permute-start | bytes 393224 | tf_op jit(solution)/shard_map/ppermute | solution.py:344
  22.5 0.1 shard_map.64
  22.6 0.0 copy-start.3
  22.6 0.0 copy-start.4
  22.6 0.0 copy-start.5
  22.7 2.9 %collective-permute-start.5 = (bf16[1,128,768]{2,1,0:T(8,128)(2,1)S(1)}, bf16[1,128,768]{2,1,0:T(8,128)(2,1)S(1)}, u32[]{:S(2)}, u32[]{:S(2)}) collective-permute-start(bf16[1,128,768]{2,1,0:T(8,128)(2,1)S(1)} %get-tuple-element.22), channel_id=1, source_target_pairs={{0,4},{8,12},{4,0},{12,8},{1,5},{9,13},{5,1},{13,9},{2,6},{10,14},... | collective-permute-start | bytes 589832 | tf_op jit(solution)/shard_map/ppermute | solution.py:344
  25.6 0.7 %collective-permute-start.6 = (bf16[1,128,768]{2,1,0:T(8,128)(2,1)S(1)}, bf16[1,128,768]{2,1,0:T(8,128)(2,1)S(1)}, u32[]{:S(2)}, u32[]{:S(2)}) collective-permute-start(bf16[1,128,768]{2,1,0:T(8,128)(2,1)S(1)} %get-tuple-element.23), channel_id=1, source_target_pairs={{4,8},{8,4},{5,9},{9,5},{6,10},{10,6},{7,11},{11,7},{20,24},{24,20... | collective-permute-start | bytes 589832 | tf_op jit(solution)/shard_map/ppermute | solution.py:344
  26.3 1.3 %first.1.before_ref = f32[4,512,512]{2,1,0:T(8,128)S(1)} custom-call(bf16[512,256]{1,0:T(8,128)(2,1)S(1)} %copy-done, bf16[256,512]{1,0:T(8,128)(2,1)S(1)} %copy-done.1, bf16[2,512,512]{2,1,0:T(8,128)(2,1)S(1)} %get-tuple-element.24.own_ref, bf16[2,512,128]{2,1,0:T(8,128)(2,1)S(1)} %collective-permute-done.7.refs_0_.col_inner_ref, ...), custom_call_target="tpu_custom_call" | custom-call | flops 1879048192 | bytes 4194304 | tf_op jit(solution)/shard_map/first/pallas_call | solution.py:384
  27.7 2.9 %next.1 = (f32[4,512,512]{2,1,0:T(8,128)S(1)}, f32[4,128]{1,0:T(4,128)S(1)}) custom-call(s32[2,2,2,2]{3,2,1,0:T(2,128)S(1)} %copy-done.3, s32[8]{0:T(128)S(1)} %copy-done.4, bf16[512,256]{1,0:T(8,128)(2,1)S(1)} %copy-done, bf16[256,512]{1,0:T(8,128)(2,1)S(1)} %copy-done.1, bf16[2,512,512]{2,1,0:T(8,128)(2,1)S(1)} %get-tuple-element.24.own_ref, ...), custom_call_target="tpu_custom_call" | custom-call | flops 2214592512 | bytes 4194304 | tf_op jit(solution)/shard_map/next/pallas_call | solution.py:396
  30.6 2.9 %last.1 = f32[32,128]{1,0:T(8,128)S(1)} custom-call(s32[2,2,2,2]{3,2,1,0:T(2,128)S(1)} %copy-done.3, s32[8]{0:T(128)S(1)} %copy-done.4, bf16[512,256]{1,0:T(8,128)(2,1)S(1)} %copy-done, bf16[256,512]{1,0:T(8,128)(2,1)S(1)} %copy-done.1, f32[4,256,128]{2,1,0:T(8,128)S(1)} %copy-done.5, bf16[1,512,256]{2,1,0:T(8,128)(2,1)S(1)} %collective-permute-done.refs_0_.middle_ref, ...), custom_call_target="tpu_custom_call" | custom-call | flops 2214592512 | bytes 4194304 | tf_op jit(solution)/shard_map/last/pallas_call | solution.py:397
  33.5 14.0 %all_to_all.9 = f32[32,1,128]{2,1,0:T(1,128)S(1)} all-to-all(f32[32,1,128]{2,1,0:T(1,128)S(1)} %bitcast.3), channel_id=1, replica_groups=mesh['gz'=2,'row'=4,'col'=4] {'gz','row','col'}, dimensions={0} | all-to-all | bytes 32768 | tf_op jit(solution)/shard_map/all_to_all | solution.py:407
  47.5 0.1 reduce_sum.9
  47.6 0.6 %reshape.5 = f32[2,64]{1,0:T(2,128)} reshape(f32[128]{0:T(128)S(1)} %reduce_sum.9) | data formatting | bytes 1024 | tf_op jit(solution)/shard_map/reshape | solution.py:408
  (16 shorter events, 0.0 us)
Async XLA Ops:
  0.0 1.2 %copy-start.2 = (bf16[2,512,512]{2,1,0:T(8,128)(2,1)S(1)}, bf16[2,512,512]{2,1,0:T(8,128)(2,1)}, u32[]{:S(2)}) copy-start(bf16[2,512,512]{2,1,0:T(8,128)(2,1)} %far_ref.1) | copy-start | bytes 3145732
  1.5 13.1 %collective-permute-start.7 = (bf16[2,512,128]{2,1,0:T(8,128)(2,1)S(1)}, bf16[2,512,128]{2,1,0:T(8,128)(2,1)S(1)}, u32[]{:S(2)}, u32[]{:S(2)}) collective-permute-start(bf16[2,512,128]{2,1,0:T(8,128)(2,1)S(1)} %get-tuple-element.25), channel_id=1, source_target_pairs={{0,1},{2,3},{1,0},{3,2},{4,5},{6,7},{5,4},{7,6},{8,9},{10,11},{9,8... | collective-permute-start | bytes 786440 | tf_op jit(solution)/shard_map/ppermute | solution.py:327
  4.6 14.1 %collective-permute-start.8 = (bf16[2,512,128]{2,1,0:T(8,128)(2,1)S(1)}, bf16[2,512,128]{2,1,0:T(8,128)(2,1)S(1)}, u32[]{:S(2)}, u32[]{:S(2)}) collective-permute-start(bf16[2,512,128]{2,1,0:T(8,128)(2,1)S(1)} %get-tuple-element.26), channel_id=1, source_target_pairs={{1,2},{2,1},{5,6},{6,5},{9,10},{10,9},{13,14},{14,13},{17,18},{18,... | collective-permute-start | bytes 786440 | tf_op jit(solution)/shard_map/ppermute | solution.py:327
  5.3 6.4 %collective-permute-start.1 = (bf16[1,512,128]{2,1,0:T(8,128)(2,1)S(1)}, bf16[1,512,128]{2,1,0:T(8,128)(2,1)S(1)}, u32[]{:S(2)}, u32[]{:S(2)}) collective-permute-start(bf16[1,512,128]{2,1,0:T(8,128)(2,1)S(1)} %get-tuple-element.20), channel_id=1, source_target_pairs={{0,16},{16,0},{1,17},{17,1},{2,18},{18,2},{3,19},{19,3},{4,20},{20... | collective-permute-start | bytes 393224 | tf_op jit(solution)/shard_map/ppermute | solution.py:329
  6.8 6.3 %collective-permute-start.2 = (bf16[1,512,128]{2,1,0:T(8,128)(2,1)S(1)}, bf16[1,512,128]{2,1,0:T(8,128)(2,1)S(1)}, u32[]{:S(2)}, u32[]{:S(2)}) collective-permute-start(bf16[1,512,128]{2,1,0:T(8,128)(2,1)S(1)} %get-tuple-element.21), channel_id=1, source_target_pairs={{0,16},{16,0},{1,17},{17,1},{2,18},{18,2},{3,19},{19,3},{4,20},{20... | collective-permute-start | bytes 393224 | tf_op jit(solution)/shard_map/ppermute | solution.py:330
  7.4 18.2 %collective-permute-start.10 = (bf16[2,128,512]{2,1,0:T(8,128)(2,1)S(1)}, bf16[2,128,512]{2,1,0:T(8,128)(2,1)S(1)}, u32[]{:S(2)}, u32[]{:S(2)}) collective-permute-start(bf16[2,128,512]{2,1,0:T(8,128)(2,1)S(1)} %get-tuple-element.28), channel_id=1, source_target_pairs={{4,8},{8,4},{5,9},{9,5},{6,10},{10,6},{7,11},{11,7},{20,24},{24,20... | collective-permute-start | bytes 786440 | tf_op jit(solution)/shard_map/ppermute | solution.py:328
  11.7 14.5 %collective-permute-start.9 = (bf16[2,128,512]{2,1,0:T(8,128)(2,1)S(1)}, bf16[2,128,512]{2,1,0:T(8,128)(2,1)S(1)}, u32[]{:S(2)}, u32[]{:S(2)}) collective-permute-start(bf16[2,128,512]{2,1,0:T(8,128)(2,1)S(1)} %get-tuple-element.27), channel_id=1, source_target_pairs={{0,4},{8,12},{4,0},{12,8},{1,5},{9,13},{5,1},{13,9},{2,6},{10,14},... | collective-permute-start | bytes 786440 | tf_op jit(solution)/shard_map/ppermute | solution.py:328
  13.1 9.4 %collective-permute-start = (bf16[1,512,256]{2,1,0:T(8,128)(2,1)S(1)}, bf16[1,512,256]{2,1,0:T(8,128)(2,1)S(1)}, u32[]{:S(2)}, u32[]{:S(2)}) collective-permute-start(bf16[1,512,256]{2,1,0:T(8,128)(2,1)S(1)} %get-tuple-element.19), channel_id=1, source_target_pairs={{0,16},{16,0},{1,17},{17,1},{2,18},{18,2},{3,19},{19,3},{4,20},{20... | collective-permute-start | bytes 786440 | tf_op jit(solution)/shard_map/ppermute | solution.py:331
  14.6 7.0 %collective-permute-start.3 = (bf16[1,512,128]{2,1,0:T(8,128)(2,1)S(1)}, bf16[1,512,128]{2,1,0:T(8,128)(2,1)S(1)}, u32[]{:S(2)}, u32[]{:S(2)}) collective-permute-start(bf16[1,512,128]{2,1,0:T(8,128)(2,1)S(1)} %collective-permute-done.1.refs_1_.first_inner_ref), channel_id=1, source_target_pairs={{0,1},{2,3},{1,0},{3,2},{4,5},{6,7},{5,4},{7,6},{8,9},{10,11},{9,8... | collective-permute-start | bytes 393224 | tf_op jit(solution)/shard_map/ppermute | solution.py:332
  18.7 2.9 %collective-permute-start.4 = (bf16[1,512,128]{2,1,0:T(8,128)(2,1)S(1)}, bf16[1,512,128]{2,1,0:T(8,128)(2,1)S(1)}, u32[]{:S(2)}, u32[]{:S(2)}) collective-permute-start(bf16[1,512,128]{2,1,0:T(8,128)(2,1)S(1)} %collective-permute-done.2.refs_2_.first_outer_ref), channel_id=1, source_target_pairs={{1,2},{2,1},{5,6},{6,5},{9,10},{10,9},{13,14},{14,13},{17,18},{18,... | collective-permute-start | bytes 393224 | tf_op jit(solution)/shard_map/ppermute | solution.py:332
  21.7 4.6 %collective-permute-start.11 = (bf16[2,128,256]{2,1,0:T(8,128)(2,1)S(1)}, bf16[2,128,256]{2,1,0:T(8,128)(2,1)S(1)}, u32[]{:S(2)}, u32[]{:S(2)}) collective-permute-start(bf16[2,128,256]{2,1,0:T(8,128)(2,1)S(1)} %get-tuple-element.29), channel_id=1, source_target_pairs={{0,4},{8,12},{4,0},{12,8},{1,5},{9,13},{5,1},{13,9},{2,6},{10,14},... | collective-permute-start | bytes 393224 | tf_op jit(solution)/shard_map/ppermute | solution.py:344
  21.7 4.6 %copy-start = (bf16[512,256]{1,0:T(8,128)(2,1)S(1)}, bf16[512,256]{1,0:T(8,128)(2,1)}, u32[]{:S(2)}) copy-start(bf16[512,256]{1,0:T(8,128)(2,1)} %constant.13.table_ref) | copy-start | bytes 786436
  21.7 4.6 %copy-start.1 = (bf16[256,512]{1,0:T(8,128)(2,1)S(1)}, bf16[256,512]{1,0:T(8,128)(2,1)}, u32[]{:S(2)}) copy-start(bf16[256,512]{1,0:T(8,128)(2,1)} %constant.14.turned_ref) | copy-start | bytes 786436
  21.7 4.6 %collective-permute-start.12 = (bf16[2,128,256]{2,1,0:T(8,128)(2,1)S(1)}, bf16[2,128,256]{2,1,0:T(8,128)(2,1)S(1)}, u32[]{:S(2)}, u32[]{:S(2)}) collective-permute-start(bf16[2,128,256]{2,1,0:T(8,128)(2,1)S(1)} %get-tuple-element.30), channel_id=1, source_target_pairs={{4,8},{8,4},{5,9},{9,5},{6,10},{10,6},{7,11},{11,7},{20,24},{24,20... | collective-permute-start | bytes 393224 | tf_op jit(solution)/shard_map/ppermute | solution.py:344
  22.6 5.1 %copy-start.3 = (s32[2,2,2,2]{3,2,1,0:T(2,128)S(1)}, s32[2,2,2,2]{3,2,1,0:T(2,128)}, u32[]{:S(2)}) copy-start(s32[2,2,2,2]{3,2,1,0:T(2,128)} %far_prior_ref.3) | copy-start | bytes 196
  22.6 5.1 %copy-start.4 = (s32[8]{0:T(128)S(1)}, s32[8]{0:T(128)}, u32[]{:S(2)}) copy-start(s32[8]{0:T(128)} %far_order_ref.3) | copy-start | bytes 100
  22.6 5.1 %copy-start.5 = (f32[4,256,128]{2,1,0:T(8,128)S(1)}, f32[4,256,128]{2,1,0:T(8,128)}, u32[]{:S(2)}) copy-start(f32[4,256,128]{2,1,0:T(8,128)} %constant.16.lag_ref) | copy-start | bytes 1572868
  22.7 7.9 %collective-permute-start.5 = (bf16[1,128,768]{2,1,0:T(8,128)(2,1)S(1)}, bf16[1,128,768]{2,1,0:T(8,128)(2,1)S(1)}, u32[]{:S(2)}, u32[]{:S(2)}) collective-permute-start(bf16[1,128,768]{2,1,0:T(8,128)(2,1)S(1)} %get-tuple-element.22), channel_id=1, source_target_pairs={{0,4},{8,12},{4,0},{12,8},{1,5},{9,13},{5,1},{13,9},{2,6},{10,14},... | collective-permute-start | bytes 589832 | tf_op jit(solution)/shard_map/ppermute | solution.py:344
  25.6 5.0 %collective-permute-start.6 = (bf16[1,128,768]{2,1,0:T(8,128)(2,1)S(1)}, bf16[1,128,768]{2,1,0:T(8,128)(2,1)S(1)}, u32[]{:S(2)}, u32[]{:S(2)}) collective-permute-start(bf16[1,128,768]{2,1,0:T(8,128)(2,1)S(1)} %get-tuple-element.23), channel_id=1, source_target_pairs={{4,8},{8,4},{5,9},{9,5},{6,10},{10,6},{7,11},{11,7},{20,24},{24,20... | collective-permute-start | bytes 589832 | tf_op jit(solution)/shard_map/ppermute | solution.py:344

commit v6 on v5

--- a/solution.py
+++ b/solution.py
@@ -99,10 +99,18 @@
     return lax.axis_index(axis) % 2 == 0
 
 
-def fill_parts(table_ref, turned_ref, pieces, s, out_ref, ext_ref, rows_ref, spec_ref):
-    center_refs, col_refs, row_refs = pieces
-    top = ext_ref.shape[0] - MARGIN
-    row_even, col_even = is_even("row"), is_even("col")
+def fill_center(ext_ref, center_refs, col_refs, s):
+    top = ext_ref.shape[1] - MARGIN
+    col_even = is_even("col")
+    inner, outer = col_refs[0][s], col_refs[1][s]
+    ext_ref[:, 0:MARGIN] = lax.select(col_even, outer, inner)
+    ext_ref[:, top:] = lax.select(col_even, inner, outer)
+    center_rows(ext_ref.at[:, MARGIN:top], col_even, center_refs, s, slice(0, top - MARGIN))
+
+
+def fill_edge(ext_ref, row_refs, s):
+    top = ext_ref.shape[1] - MARGIN
+    row_even = is_even("row")
     if len(row_refs) == 2:
         spans = ((row_refs, slice(None), slice(None)),)
     else:
@@ -115,23 +123,43 @@
     for refs, source, target in spans:
         inner, outer = refs[0][s, :, source], refs[1][s, :, source]
         ext_ref[0:MARGIN, target] = lax.select(row_even, outer, inner)
-        ext_ref[top:, target] = lax.select(row_even, inner, outer)
-    inner, outer = col_refs[0][s], col_refs[1][s]
-    ext_ref[MARGIN:top, 0:MARGIN] = lax.select(col_even, outer, inner)
-    ext_ref[MARGIN:top, top:] = lax.select(col_even, inner, outer)
-    center_rows(ext_ref.at[MARGIN:top, MARGIN:top], col_even, center_refs, s, slice(0, top - MARGIN))
-    per_side = (top - MARGIN) // STRIDE
-    parities = (slice(0, HALF), slice(HALF, PATCH))
-    for pj in range(per_side):
+        ext_ref[MARGIN:, target] = lax.select(row_even, inner, outer)
+
+
+PARITIES = (slice(0, HALF), slice(HALF, PATCH))
+
+
+def row_pass(ext_ref, turned_ref, out_ref):
+    for pj in range(out_ref.shape[0]):
         near = ext_ref[:, pj * STRIDE : pj * STRIDE + HALF]
         away = ext_ref[:, pj * STRIDE + HALF : pj * STRIDE + PATCH]
-        for part, folded in zip(parities, (near + away, near - away)):
-            rows_ref[pj, :, part] = jnp.dot(folded, turned_ref[:, part], preferred_element_type=jnp.float32).astype(jnp.bfloat16)
+        for part, folded in zip(PARITIES, (near + away, near - away)):
+            found = jnp.dot(folded, turned_ref[:, part], preferred_element_type=jnp.float32)
+            out_ref[pj, :, part] = found.astype(jnp.bfloat16)
+
+
+def column_pass(table_ref, middle_ref, edge_ref, spec_ref, out_ref):
+    per_side, side = middle_ref.shape[:2]
+    bounds = (0, MARGIN, side + MARGIN, side + HALO)
+
+    def rows(pj, start, stop):
+        found = []
+        for ref, shift, low, high in (
+            (edge_ref, 0, bounds[0], bounds[1]),
+            (middle_ref, MARGIN, bounds[1], bounds[2]),
+            (edge_ref, side, bounds[2], bounds[3]),
+        ):
+            low, high = max(low, start), min(high, stop)
+            if low < high:
+                found.append(ref[pj, low - shift : high - shift, :])
+        return found[0] if len(found) == 1 else jnp.concatenate(found, axis=0)
+
+    for pj in range(per_side):
         for pi in range(per_side):
             n = pi * per_side + pj
-            near = rows_ref[pj, pi * STRIDE : pi * STRIDE + HALF, :]
-            away = rows_ref[pj, pi * STRIDE + HALF : pi * STRIDE + PATCH, :]
-            for part, folded in zip(parities, (near + away, near - away)):
+            near = rows(pj, pi * STRIDE, pi * STRIDE + HALF)
+            away = rows(pj, pi * STRIDE + HALF, pi * STRIDE + PATCH)
+            for part, folded in zip(PARITIES, (near + away, near - away)):
                 spec_ref[n % 2, part] = jnp.dot(table_ref[part], folded, preferred_element_type=jnp.float32)
             split_parts(spec_ref.at[n % 2], out_ref.at[n])
 
@@ -231,27 +259,46 @@
     return total_out
 
 
+def rows_kernel(turned_ref, own_ref, col_inner_ref, col_outer_ref, rows_ref, ext_ref):
+    for s in range(own_ref.shape[0]):
+        fill_center(ext_ref.at[s], (own_ref,), (col_inner_ref, col_outer_ref), s)
+        row_pass(ext_ref.at[s], turned_ref, rows_ref.at[s])
+
+
+def last_rows_kernel(
+    turned_ref, middle_ref, first_inner_ref, first_outer_ref, col_inner_ref, col_outer_ref, rows_ref, ext_ref,
+):
+    fill_center(ext_ref, (middle_ref, first_inner_ref, first_outer_ref), (col_inner_ref, col_outer_ref), 0)
+    row_pass(ext_ref, turned_ref, rows_ref)
+
+
+def own_parts(table_ref, turned_ref, middle_ref, row_refs, section, part_ref, ext_ref, rows_ref, spec_ref):
+    fill_edge(ext_ref, row_refs, section)
+    row_pass(ext_ref, turned_ref, rows_ref)
+    column_pass(table_ref, middle_ref.at[section], rows_ref, spec_ref, part_ref)
+
+
 def first_kernel(
-    table_ref, turned_ref, own_ref, col_inner_ref, col_outer_ref, row_inner_ref, row_outer_ref,
-    corner_inner_ref, corner_outer_ref, part_ref, ext_ref, rows_ref, spec_ref, *, section,
+    table_ref, turned_ref, middle_ref, row_inner_ref, row_outer_ref, corner_inner_ref, corner_outer_ref,
+    part_ref, ext_ref, rows_ref, spec_ref, *, section,
 ):
-    pieces = ((own_ref,), (col_inner_ref, col_outer_ref), (row_inner_ref, row_outer_ref, corner_inner_ref, corner_outer_ref))
-    fill_parts(table_ref, turned_ref, pieces, section, part_ref, ext_ref, rows_ref, spec_ref)
+    row_refs = (row_inner_ref, row_outer_ref, corner_inner_ref, corner_outer_ref)
+    own_parts(table_ref, turned_ref, middle_ref, row_refs, section, part_ref, ext_ref, rows_ref, spec_ref)
 
 
 def next_kernel(
-    far_prior_ref, far_order_ref, table_ref, turned_ref, own_ref, col_inner_ref, col_outer_ref, row_inner_ref, row_outer_ref,
-    corner_inner_ref, corner_outer_ref, lag_ref, flow_in_ref, before_ref, part_ref, flow_ref, ext_ref, rows_ref, spec_ref, cross_ref, prior_ref, order_ref, sems,
-    *, section, sizes,
+    far_prior_ref, far_order_ref, table_ref, turned_ref, middle_ref, row_inner_ref, row_outer_ref,
+    corner_inner_ref, corner_outer_ref, lag_ref, flow_in_ref, before_ref, part_ref, flow_ref,
+    ext_ref, rows_ref, spec_ref, cross_ref, prior_ref, order_ref, sems, *, section, sizes,
 ):
-    pieces = ((own_ref,), (col_inner_ref, col_outer_ref), (row_inner_ref, row_outer_ref, corner_inner_ref, corner_outer_ref))
+    row_refs = (row_inner_ref, row_outer_ref, corner_inner_ref, corner_outer_ref)
     copies = (
         pltpu.make_async_copy(far_prior_ref, prior_ref, sems.at[0]),
         pltpu.make_async_copy(far_order_ref, order_ref, sems.at[1]),
     )
     for copy in copies:
         copy.start()
-    fill_parts(table_ref, turned_ref, pieces, section, part_ref, ext_ref, rows_ref, spec_ref)
+    own_parts(table_ref, turned_ref, middle_ref, row_refs, section, part_ref, ext_ref, rows_ref, spec_ref)
     for copy in copies:
         copy.wait()
     flow_ref[...] = flow_in_ref[...] + placed_flows(
@@ -260,20 +307,19 @@
 
 
 def last_kernel(
-    far_prior_ref, far_order_ref, table_ref, turned_ref, lag_ref, middle_ref, first_inner_ref, first_outer_ref, col_inner_ref, col_outer_ref,
-    row_inner_ref, row_outer_ref, flow_ref, first_ref, out_ref, ext_ref, rows_ref, spec_ref, part_ref, cross_ref, prior_ref, order_ref, sems,
-    *, sizes,
+    far_prior_ref, far_order_ref, table_ref, turned_ref, lag_ref, middle_ref, row_inner_ref, row_outer_ref,
+    flow_ref, first_ref, out_ref, ext_ref, rows_ref, spec_ref, part_ref, cross_ref, prior_ref, order_ref, sems, *, sizes,
 ):
     size_gz, size_row, size_col, sec_count, _ = sizes
-    center = (middle_ref, first_inner_ref, first_outer_ref)
-    pieces = (center, (col_inner_ref, col_outer_ref), (row_inner_ref, row_outer_ref))
     copies = (
         pltpu.make_async_copy(far_prior_ref, prior_ref, sems.at[0]),
         pltpu.make_async_copy(far_order_ref, order_ref, sems.at[1]),
     )
     for copy in copies:
         copy.start()
-    fill_parts(table_ref, turned_ref, pieces, 0, part_ref, ext_ref, rows_ref, spec_ref)
+    fill_edge(ext_ref, (row_inner_ref, row_outer_ref), 0)
+    row_pass(ext_ref, turned_ref, rows_ref)
+    column_pass(table_ref, middle_ref, rows_ref, spec_ref, part_ref)
     for copy in copies:
         copy.wait()
     flow = flow_ref[...] + placed_flows(
@@ -353,8 +399,8 @@
 
     part_shape = jax.ShapeDtypeStruct(parts, jnp.float32)
     flow_shape = jax.ShapeDtypeStruct((size_row, lanes), jnp.float32)
-    ext_scratch = pltpu.VMEM((wide, wide), jnp.bfloat16)
-    rows_scratch = pltpu.VMEM((per_side, wide, PATCH), jnp.bfloat16)
+    edge_ext_scratch = pltpu.VMEM((HALO, wide), jnp.bfloat16)
+    edge_rows_scratch = pltpu.VMEM((per_side, HALO, PATCH), jnp.bfloat16)
     spec_scratch = pltpu.VMEM((2, PATCH, PATCH), jnp.float32)
     part_scratch = pltpu.VMEM(parts, jnp.float32)
     scalars = [
@@ -370,13 +416,24 @@
         return pl.CostEstimate(flops=flops, bytes_accessed=place_count * PATCH * PATCH * 4, transcendentals=0)
 
     flow = jnp.zeros((size_row, lanes), jnp.float32)
-    pieces = (own, *own_cols, *own_rows, *own_corners)
+    rows_call = pl.pallas_call(
+        rows_kernel,
+        out_shape=pixels(sec_count, per_side, side, PATCH),
+        in_specs=[vmem] * 4,
+        out_specs=vmem,
+        scratch_shapes=[pltpu.VMEM((sec_count, side, wide), jnp.bfloat16)],
+        compiler_params=params,
+        cost_estimate=cost(2 * sec_count * per_side * side * HALF * PATCH),
+        name="rows",
+    )
+    own_middle = rows_call(turned, own, *own_cols)
+    pieces = (own_middle, *own_rows, *own_corners)
     first_call = pl.pallas_call(
         functools.partial(first_kernel, section=0),
         out_shape=part_shape,
-        in_specs=[vmem] * 9,
+        in_specs=[vmem] * 7,
         out_specs=vmem,
-        scratch_shapes=[ext_scratch, rows_scratch, spec_scratch],
+        scratch_shapes=[edge_ext_scratch, edge_rows_scratch, spec_scratch],
         compiler_params=params,
         cost_estimate=cost(spectra_cost),
         name="first",
@@ -386,24 +443,35 @@
         next_call = pl.pallas_call(
             functools.partial(next_kernel, section=section, sizes=sizes),
             out_shape=(part_shape, flow_shape),
-            in_specs=[far] * 2 + [vmem] * 12,
+            in_specs=[far] * 2 + [vmem] * 10,
             out_specs=(vmem, vmem),
-            scratch_shapes=[ext_scratch, rows_scratch, spec_scratch, cross_scratch, *scalars],
+            scratch_shapes=[edge_ext_scratch, edge_rows_scratch, spec_scratch, cross_scratch, *scalars],
             compiler_params=params,
             cost_estimate=cost(spectra_cost + pair_cost),
             name="next",
         )
         part, flow = next_call(priors, row_order, table, turned, *pieces, lag_table, flow, part)
+    last_rows_call = pl.pallas_call(
+        last_rows_kernel,
+        out_shape=pixels(per_side, side, PATCH),
+        in_specs=[vmem] * 6,
+        out_specs=vmem,
+        scratch_shapes=[pltpu.VMEM((side, wide), jnp.bfloat16)],
+        compiler_params=params,
+        cost_estimate=cost(2 * per_side * side * HALF * PATCH),
+        name="last_middle",
+    )
+    last_middle = last_rows_call(turned, *last_center, *last_cols)
     sent = pl.pallas_call(
         functools.partial(last_kernel, sizes=sizes),
         out_shape=jax.ShapeDtypeStruct((devices, lanes), jnp.float32),
-        in_specs=[far] * 2 + [vmem] * 12,
+        in_specs=[far] * 2 + [vmem] * 8,
         out_specs=vmem,
-        scratch_shapes=[ext_scratch, rows_scratch, spec_scratch, part_scratch, cross_scratch, *scalars],
+        scratch_shapes=[edge_ext_scratch, edge_rows_scratch, spec_scratch, part_scratch, cross_scratch, *scalars],
         compiler_params=params,
         cost_estimate=cost(spectra_cost + pair_cost),
         name="last",
-    )(priors, row_order, table, turned, lag_table, *last_center, *last_cols, *last_rows, flow, part)
+    )(priors, row_order, table, turned, lag_table, last_middle, *last_rows, flow, part)
     received = lax.all_to_all(sent, AXES, 0, 0, tiled=True)
     return jnp.sum(received, axis=0).reshape(row_order.shape[0] // size_row, -1)
 

time: 48.5 us -> 48.3 us (level)
    pallas_call x0 -> x2, Pallas kernels: none -> 1.19 us  [the longest x1 0.73 us: match(): own_middle = rows_call(turned, own, *own_cols)]
  transfers between devices with their start and end apart: 13 -> 13, of which waited for: 3 -> 3; matrix products, arithmetic and copies ran while one was open for 0% -> 0% of each run, Pallas kernels for 9% -> 10%
where the time goes in v6:
time: 48.3 us; the launch traced here: 48.1 us
  starting transfers between devices  17.3 us (36%)
  blocking collectives  13.6 us (28%)
  Pallas kernels  7.67 us (16%)
  waiting for transfers between devices  7.28 us (15%)
  local copies, waits for them, and re-layouts  1.9 us (4%)
    all_to_all x1, blocking collectives, match(): received = lax.all_to_all(sent, AXES, 0, 0, tiled=True)  13.6 us
    ppermute x1, starting transfers between devices, match(): lax.ppermute(first_inner, 'col', col_inner)  4.1 us
    ppermute x1, waiting for transfers between devices, match(): first_inner = lax.ppermute(cuts[4], 'gz', gz_pairs)  3.66 us
    ppermute x1, starting transfers between devices, match(): lax.ppermute(cuts[0], 'col', col_inner)  3.12 us
    ppermute x2, starting transfers between devices, edges(): lax.ppermute(inner, 'row', row_inner)  2.94 us
    pallas_call x1, Pallas kernels, match(): pl.pallas_call(functools.partial(last_kernel, sizes=sizes), out_shape=jax...  2.53 us
    pallas_call x1, Pallas kernels, match(): next_call(priors, row_order, table, turned, *pieces, lag_table, flow, part)  2.52 us
    ppermute x1, waiting for transfers between devices, match(): lax.ppermute(first_inner, 'col', col_inner)  2.2 us
  transfers between devices with their start and end apart: 13, of which 3 were waited for; matrix products, arithmetic and copies ran while one was open for 0% of the time, Pallas kernels for 10%

profile of v6, /device:TPU:0, one launch (start us, length us, event | category | flops | bytes accessed | tf_op | source)
XLA Modules:
  0.0 48.1 jit_solution(15334476528258720068)
XLA Ops:
  0.0 1.2 %copy-done.2 = bf16[2,512,512]{2,1,0:T(8,128)(2,1)S(1)} copy-done((bf16[2,512,512]{2,1,0:T(8,128)(2,1)S(1)}, bf16[2,512,512]{2,1,0:T(8,128)(2,1)}, u32[]{:S(2)}) %copy-start.2) | copy-done | bytes 1048600
  1.2 0.3 cut.1
  1.5 3.1 %collective-permute-start.7 = (bf16[2,512,128]{2,1,0:T(8,128)(2,1)S(1)}, bf16[2,512,128]{2,1,0:T(8,128)(2,1)S(1)}, u32[]{:S(2)}, u32[]{:S(2)}) collective-permute-start(bf16[2,512,128]{2,1,0:T(8,128)(2,1)S(1)} %get-tuple-element.25), channel_id=1, source_target_pairs={{0,1},{2,3},{1,0},{3,2},{4,5},{6,7},{5,4},{7,6},{8,9},{10,11},{9,8... | collective-permute-start | bytes 786440 | tf_op jit(solution)/shard_map/ppermute | solution.py:373
  4.6 0.7 %collective-permute-start.8 = (bf16[2,512,128]{2,1,0:T(8,128)(2,1)S(1)}, bf16[2,512,128]{2,1,0:T(8,128)(2,1)S(1)}, u32[]{:S(2)}, u32[]{:S(2)}) collective-permute-start(bf16[2,512,128]{2,1,0:T(8,128)(2,1)S(1)} %get-tuple-element.26), channel_id=1, source_target_pairs={{1,2},{2,1},{5,6},{6,5},{9,10},{10,9},{13,14},{14,13},{17,18},{18,... | collective-permute-start | bytes 786440 | tf_op jit(solution)/shard_map/ppermute | solution.py:373
  5.3 1.6 %collective-permute-start.1 = (bf16[1,512,128]{2,1,0:T(8,128)(2,1)S(1)}, bf16[1,512,128]{2,1,0:T(8,128)(2,1)S(1)}, u32[]{:S(2)}, u32[]{:S(2)}) collective-permute-start(bf16[1,512,128]{2,1,0:T(8,128)(2,1)S(1)} %get-tuple-element.20), channel_id=1, source_target_pairs={{0,16},{16,0},{1,17},{17,1},{2,18},{18,2},{3,19},{19,3},{4,20},{20... | collective-permute-start | bytes 393224 | tf_op jit(solution)/shard_map/ppermute | solution.py:375
  6.8 0.5 %collective-permute-start.2 = (bf16[1,512,128]{2,1,0:T(8,128)(2,1)S(1)}, bf16[1,512,128]{2,1,0:T(8,128)(2,1)S(1)}, u32[]{:S(2)}, u32[]{:S(2)}) collective-permute-start(bf16[1,512,128]{2,1,0:T(8,128)(2,1)S(1)} %get-tuple-element.21), channel_id=1, source_target_pairs={{0,16},{16,0},{1,17},{17,1},{2,18},{18,2},{3,19},{19,3},{4,20},{20... | collective-permute-start | bytes 393224 | tf_op jit(solution)/shard_map/ppermute | solution.py:376
  7.4 0.7 %collective-permute-start.10 = (bf16[2,128,512]{2,1,0:T(8,128)(2,1)S(1)}, bf16[2,128,512]{2,1,0:T(8,128)(2,1)S(1)}, u32[]{:S(2)}, u32[]{:S(2)}) collective-permute-start(bf16[2,128,512]{2,1,0:T(8,128)(2,1)S(1)} %get-tuple-element.28), channel_id=1, source_target_pairs={{4,8},{8,4},{5,9},{9,5},{6,10},{10,6},{7,11},{11,7},{20,24},{24,20... | collective-permute-start | bytes 786440 | tf_op jit(solution)/shard_map/ppermute | solution.py:374
  8.1 3.7 %collective-permute-done.1.first_inner_ref.refs_1_ = bf16[1,512,128]{2,1,0:T(8,128)(2,1)S(1)} collective-permute-done((bf16[1,512,128]{2,1,0:T(8,128)(2,1)S(1)}, bf16[1,512,128]{2,1,0:T(8,128)(2,1)S(1)}, u32[]{:S(2)}, u32[]{:S(2)}) %collective-permute-start.1) | collective-permute-done | bytes 131104 | tf_op jit(solution)/shard_map/ppermute | solution.py:375
  11.7 1.4 %collective-permute-done.2.first_outer_ref.refs_2_ = bf16[1,512,128]{2,1,0:T(8,128)(2,1)S(1)} collective-permute-done((bf16[1,512,128]{2,1,0:T(8,128)(2,1)S(1)}, bf16[1,512,128]{2,1,0:T(8,128)(2,1)S(1)}, u32[]{:S(2)}, u32[]{:S(2)}) %collective-permute-start.2) | collective-permute-done | bytes 131104 | tf_op jit(solution)/shard_map/ppermute | solution.py:376
  13.1 1.5 %collective-permute-start = (bf16[1,512,256]{2,1,0:T(8,128)(2,1)S(1)}, bf16[1,512,256]{2,1,0:T(8,128)(2,1)S(1)}, u32[]{:S(2)}, u32[]{:S(2)}) collective-permute-start(bf16[1,512,256]{2,1,0:T(8,128)(2,1)S(1)} %get-tuple-element.19), channel_id=1, source_target_pairs={{0,16},{16,0},{1,17},{17,1},{2,18},{18,2},{3,19},{19,3},{4,20},{20... | collective-permute-start | bytes 786440 | tf_op jit(solution)/shard_map/ppermute | solution.py:377
  14.6 0.0 collective-permute-done.7.col_inner_ref.refs_0_
  14.6 4.1 %collective-permute-start.3 = (bf16[1,512,128]{2,1,0:T(8,128)(2,1)S(1)}, bf16[1,512,128]{2,1,0:T(8,128)(2,1)S(1)}, u32[]{:S(2)}, u32[]{:S(2)}) collective-permute-start(bf16[1,512,128]{2,1,0:T(8,128)(2,1)S(1)} %collective-permute-done.1.first_inner_ref.refs_1_), channel_id=1, source_target_pairs={{0,1},{2,3},{1,0},{3,2},{4,5},{6,7},{5,4},{7,6},{8,9},{10,11},{9,8... | collective-permute-start | bytes 393224 | tf_op jit(solution)/shard_map/ppermute | solution.py:378
  18.7 0.0 collective-permute-done.8.col_outer_ref.refs_1_
  18.7 0.7 %collective-permute-start.4 = (bf16[1,512,128]{2,1,0:T(8,128)(2,1)S(1)}, bf16[1,512,128]{2,1,0:T(8,128)(2,1)S(1)}, u32[]{:S(2)}, u32[]{:S(2)}) collective-permute-start(bf16[1,512,128]{2,1,0:T(8,128)(2,1)S(1)} %collective-permute-done.2.first_outer_ref.refs_2_), channel_id=1, source_target_pairs={{1,2},{2,1},{5,6},{6,5},{9,10},{10,9},{13,14},{14,13},{17,18},{18,... | collective-permute-start | bytes 393224 | tf_op jit(solution)/shard_map/ppermute | solution.py:378
  19.4 0.1 shard_map.65
  19.5 2.2 %collective-permute-done.3.col_inner_ref.refs_3_ = bf16[1,512,128]{2,1,0:T(8,128)(2,1)S(1)} collective-permute-done((bf16[1,512,128]{2,1,0:T(8,128)(2,1)S(1)}, bf16[1,512,128]{2,1,0:T(8,128)(2,1)S(1)}, u32[]{:S(2)}, u32[]{:S(2)}) %collective-permute-start.3) | collective-permute-done | bytes 131104 | tf_op jit(solution)/shard_map/ppermute | solution.py:378
  21.7 0.8 %collective-permute-start.12 = (bf16[2,128,256]{2,1,0:T(8,128)(2,1)S(1)}, bf16[2,128,256]{2,1,0:T(8,128)(2,1)S(1)}, u32[]{:S(2)}, u32[]{:S(2)}) collective-permute-start(bf16[2,128,256]{2,1,0:T(8,128)(2,1)S(1)} %get-tuple-element.30), channel_id=1, source_target_pairs={{4,8},{8,4},{5,9},{9,5},{6,10},{10,6},{7,11},{11,7},{20,24},{24,20... | collective-permute-start | bytes 393224 | tf_op jit(solution)/shard_map/ppermute | solution.py:390
  22.5 0.1 shard_map.64
  22.6 0.0 copy-start.1
  22.6 2.9 %collective-permute-start.5 = (bf16[1,128,768]{2,1,0:T(8,128)(2,1)S(1)}, bf16[1,128,768]{2,1,0:T(8,128)(2,1)S(1)}, u32[]{:S(2)}, u32[]{:S(2)}) collective-permute-start(bf16[1,128,768]{2,1,0:T(8,128)(2,1)S(1)} %get-tuple-element.22), channel_id=1, source_target_pairs={{0,4},{8,12},{4,0},{12,8},{1,5},{9,13},{5,1},{13,9},{2,6},{10,14},... | collective-permute-start | bytes 589832 | tf_op jit(solution)/shard_map/ppermute | solution.py:390
  25.6 0.5 last_middle.1.middle_ref
  26.0 0.7 %rows.1.middle_ref = bf16[2,2,512,512]{3,2,1,0:T(8,128)(2,1)S(1)} custom-call(bf16[256,512]{1,0:T(8,128)(2,1)S(1)} %copy-done, bf16[2,512,512]{2,1,0:T(8,128)(2,1)S(1)} %get-tuple-element.24.own_ref, bf16[2,512,128]{2,1,0:T(8,128)(2,1)S(1)} %collective-permute-done.7.col_inner_ref.refs_0_, bf16[2,512,128]{2,1,0:T(8,128)(2,1)S(1)} %collective-permute-done.8.col_outer_ref.refs_1_), custom_call_target="tpu_custom_call" | custom-call | flops 536870912 | bytes 4194304 | tf_op jit(solution)/shard_map/rows/pallas_call | solution.py:429
  26.8 0.0 copy-start.3
  26.8 0.0 copy-start.4
  26.8 0.0 copy-start.5
  26.8 0.8 %collective-permute-start.6 = (bf16[1,128,768]{2,1,0:T(8,128)(2,1)S(1)}, bf16[1,128,768]{2,1,0:T(8,128)(2,1)S(1)}, u32[]{:S(2)}, u32[]{:S(2)}) collective-permute-start(bf16[1,128,768]{2,1,0:T(8,128)(2,1)S(1)} %get-tuple-element.23), channel_id=1, source_target_pairs={{4,8},{8,4},{5,9},{9,5},{6,10},{10,6},{7,11},{11,7},{20,24},{24,20... | collective-permute-start | bytes 589832 | tf_op jit(solution)/shard_map/ppermute | solution.py:390
  27.7 1.0 %first.1.before_ref = f32[4,512,512]{2,1,0:T(8,128)S(1)} custom-call(bf16[512,256]{1,0:T(8,128)(2,1)S(1)} %copy-done.1, bf16[256,512]{1,0:T(8,128)(2,1)S(1)} %copy-done, bf16[2,2,512,512]{3,2,1,0:T(8,128)(2,1)S(1)} %rows.1.middle_ref, bf16[2,128,512]{2,1,0:T(8,128)(2,1)S(1)} %collective-permute-done.9.row_inner_ref, ...), custom_call_target="tpu_custom_call" | custom-call | flops 1879048192 | bytes 4194304 | tf_op jit(solution)/shard_map/first/pallas_call | solution.py:441
  28.7 2.5 %next.1 = (f32[4,512,512]{2,1,0:T(8,128)S(1)}, f32[4,128]{1,0:T(4,128)S(1)}) custom-call(s32[2,2,2,2]{3,2,1,0:T(2,128)S(1)} %copy-done.3, s32[8]{0:T(128)S(1)} %copy-done.4, bf16[512,256]{1,0:T(8,128)(2,1)S(1)} %copy-done.1, bf16[256,512]{1,0:T(8,128)(2,1)S(1)} %copy-done, bf16[2,2,512,512]{3,2,1,0:T(8,128)(2,1)S(1)} %rows.1.middle_ref, ...), custom_call_target="tpu_custom_call" | custom-call | flops 2214592512 | bytes 4194304 | tf_op jit(solution)/shard_map/next/pallas_call | solution.py:453
  31.2 2.5 %last.1 = f32[32,128]{1,0:T(8,128)S(1)} custom-call(s32[2,2,2,2]{3,2,1,0:T(2,128)S(1)} %copy-done.3, s32[8]{0:T(128)S(1)} %copy-done.4, bf16[512,256]{1,0:T(8,128)(2,1)S(1)} %copy-done.1, bf16[256,512]{1,0:T(8,128)(2,1)S(1)} %copy-done, f32[4,256,128]{2,1,0:T(8,128)S(1)} %copy-done.5, bf16[2,512,512]{2,1,0:T(8,128)(2,1)S(1)} %last_middle.1.middle_ref, ...), custom_call_target="tpu_custom_call" | custom-call | flops 2214592512 | bytes 4194304 | tf_op jit(solution)/shard_map/last/pallas_call | solution.py:465
  33.8 13.6 %all_to_all.9 = f32[32,1,128]{2,1,0:T(1,128)S(1)} all-to-all(f32[32,1,128]{2,1,0:T(1,128)S(1)} %bitcast.3), channel_id=1, replica_groups=mesh['gz'=2,'row'=4,'col'=4] {'gz','row','col'}, dimensions={0} | all-to-all | bytes 32768 | tf_op jit(solution)/shard_map/all_to_all | solution.py:475
  47.4 0.1 reduce_sum.9
  47.4 0.6 %reshape.5 = f32[2,64]{1,0:T(2,128)} reshape(f32[128]{0:T(128)S(1)} %reduce_sum.9) | data formatting | bytes 1024 | tf_op jit(solution)/shard_map/reshape | solution.py:476
  (18 shorter events, 0.0 us)
Async XLA Ops:
  0.0 1.2 %copy-start.2 = (bf16[2,512,512]{2,1,0:T(8,128)(2,1)S(1)}, bf16[2,512,512]{2,1,0:T(8,128)(2,1)}, u32[]{:S(2)}) copy-start(bf16[2,512,512]{2,1,0:T(8,128)(2,1)} %far_ref.1) | copy-start | bytes 3145732
  1.5 13.1 %collective-permute-start.7 = (bf16[2,512,128]{2,1,0:T(8,128)(2,1)S(1)}, bf16[2,512,128]{2,1,0:T(8,128)(2,1)S(1)}, u32[]{:S(2)}, u32[]{:S(2)}) collective-permute-start(bf16[2,512,128]{2,1,0:T(8,128)(2,1)S(1)} %get-tuple-element.25), channel_id=1, source_target_pairs={{0,1},{2,3},{1,0},{3,2},{4,5},{6,7},{5,4},{7,6},{8,9},{10,11},{9,8... | collective-permute-start | bytes 786440 | tf_op jit(solution)/shard_map/ppermute | solution.py:373
  4.6 14.1 %collective-permute-start.8 = (bf16[2,512,128]{2,1,0:T(8,128)(2,1)S(1)}, bf16[2,512,128]{2,1,0:T(8,128)(2,1)S(1)}, u32[]{:S(2)}, u32[]{:S(2)}) collective-permute-start(bf16[2,512,128]{2,1,0:T(8,128)(2,1)S(1)} %get-tuple-element.26), channel_id=1, source_target_pairs={{1,2},{2,1},{5,6},{6,5},{9,10},{10,9},{13,14},{14,13},{17,18},{18,... | collective-permute-start | bytes 786440 | tf_op jit(solution)/shard_map/ppermute | solution.py:373
  5.3 6.4 %collective-permute-start.1 = (bf16[1,512,128]{2,1,0:T(8,128)(2,1)S(1)}, bf16[1,512,128]{2,1,0:T(8,128)(2,1)S(1)}, u32[]{:S(2)}, u32[]{:S(2)}) collective-permute-start(bf16[1,512,128]{2,1,0:T(8,128)(2,1)S(1)} %get-tuple-element.20), channel_id=1, source_target_pairs={{0,16},{16,0},{1,17},{17,1},{2,18},{18,2},{3,19},{19,3},{4,20},{20... | collective-permute-start | bytes 393224 | tf_op jit(solution)/shard_map/ppermute | solution.py:375
  6.8 6.3 %collective-permute-start.2 = (bf16[1,512,128]{2,1,0:T(8,128)(2,1)S(1)}, bf16[1,512,128]{2,1,0:T(8,128)(2,1)S(1)}, u32[]{:S(2)}, u32[]{:S(2)}) collective-permute-start(bf16[1,512,128]{2,1,0:T(8,128)(2,1)S(1)} %get-tuple-element.21), channel_id=1, source_target_pairs={{0,16},{16,0},{1,17},{17,1},{2,18},{18,2},{3,19},{19,3},{4,20},{20... | collective-permute-start | bytes 393224 | tf_op jit(solution)/shard_map/ppermute | solution.py:376
  7.4 19.4 %collective-permute-start.10 = (bf16[2,128,512]{2,1,0:T(8,128)(2,1)S(1)}, bf16[2,128,512]{2,1,0:T(8,128)(2,1)S(1)}, u32[]{:S(2)}, u32[]{:S(2)}) collective-permute-start(bf16[2,128,512]{2,1,0:T(8,128)(2,1)S(1)} %get-tuple-element.28), channel_id=1, source_target_pairs={{4,8},{8,4},{5,9},{9,5},{6,10},{10,6},{7,11},{11,7},{20,24},{24,20... | collective-permute-start | bytes 786440 | tf_op jit(solution)/shard_map/ppermute | solution.py:374
  11.7 15.9 %collective-permute-start.9 = (bf16[2,128,512]{2,1,0:T(8,128)(2,1)S(1)}, bf16[2,128,512]{2,1,0:T(8,128)(2,1)S(1)}, u32[]{:S(2)}, u32[]{:S(2)}) collective-permute-start(bf16[2,128,512]{2,1,0:T(8,128)(2,1)S(1)} %get-tuple-element.27), channel_id=1, source_target_pairs={{0,4},{8,12},{4,0},{12,8},{1,5},{9,13},{5,1},{13,9},{2,6},{10,14},... | collective-permute-start | bytes 786440 | tf_op jit(solution)/shard_map/ppermute | solution.py:374
  13.1 9.4 %collective-permute-start = (bf16[1,512,256]{2,1,0:T(8,128)(2,1)S(1)}, bf16[1,512,256]{2,1,0:T(8,128)(2,1)S(1)}, u32[]{:S(2)}, u32[]{:S(2)}) collective-permute-start(bf16[1,512,256]{2,1,0:T(8,128)(2,1)S(1)} %get-tuple-element.19), channel_id=1, source_target_pairs={{0,16},{16,0},{1,17},{17,1},{2,18},{18,2},{3,19},{19,3},{4,20},{20... | collective-permute-start | bytes 786440 | tf_op jit(solution)/shard_map/ppermute | solution.py:377
  14.6 7.0 %collective-permute-start.3 = (bf16[1,512,128]{2,1,0:T(8,128)(2,1)S(1)}, bf16[1,512,128]{2,1,0:T(8,128)(2,1)S(1)}, u32[]{:S(2)}, u32[]{:S(2)}) collective-permute-start(bf16[1,512,128]{2,1,0:T(8,128)(2,1)S(1)} %collective-permute-done.1.first_inner_ref.refs_1_), channel_id=1, source_target_pairs={{0,1},{2,3},{1,0},{3,2},{4,5},{6,7},{5,4},{7,6},{8,9},{10,11},{9,8... | collective-permute-start | bytes 393224 | tf_op jit(solution)/shard_map/ppermute | solution.py:378
  18.7 2.9 %collective-permute-start.4 = (bf16[1,512,128]{2,1,0:T(8,128)(2,1)S(1)}, bf16[1,512,128]{2,1,0:T(8,128)(2,1)S(1)}, u32[]{:S(2)}, u32[]{:S(2)}) collective-permute-start(bf16[1,512,128]{2,1,0:T(8,128)(2,1)S(1)} %collective-permute-done.2.first_outer_ref.refs_2_), channel_id=1, source_target_pairs={{1,2},{2,1},{5,6},{6,5},{9,10},{10,9},{13,14},{14,13},{17,18},{18,... | collective-permute-start | bytes 393224 | tf_op jit(solution)/shard_map/ppermute | solution.py:378
  21.7 6.0 %collective-permute-start.11 = (bf16[2,128,256]{2,1,0:T(8,128)(2,1)S(1)}, bf16[2,128,256]{2,1,0:T(8,128)(2,1)S(1)}, u32[]{:S(2)}, u32[]{:S(2)}) collective-permute-start(bf16[2,128,256]{2,1,0:T(8,128)(2,1)S(1)} %get-tuple-element.29), channel_id=1, source_target_pairs={{0,4},{8,12},{4,0},{12,8},{1,5},{9,13},{5,1},{13,9},{2,6},{10,14},... | collective-permute-start | bytes 393224 | tf_op jit(solution)/shard_map/ppermute | solution.py:390
  21.7 3.9 %copy-start = (bf16[256,512]{1,0:T(8,128)(2,1)S(1)}, bf16[256,512]{1,0:T(8,128)(2,1)}, u32[]{:S(2)}) copy-start(bf16[256,512]{1,0:T(8,128)(2,1)} %constant.14.turned_ref) | copy-start | bytes 786436
  21.7 6.0 %collective-permute-start.12 = (bf16[2,128,256]{2,1,0:T(8,128)(2,1)S(1)}, bf16[2,128,256]{2,1,0:T(8,128)(2,1)S(1)}, u32[]{:S(2)}, u32[]{:S(2)}) collective-permute-start(bf16[2,128,256]{2,1,0:T(8,128)(2,1)S(1)} %get-tuple-element.30), channel_id=1, source_target_pairs={{4,8},{8,4},{5,9},{9,5},{6,10},{10,6},{7,11},{11,7},{20,24},{24,20... | collective-permute-start | bytes 393224 | tf_op jit(solution)/shard_map/ppermute | solution.py:390
  22.6 5.1 %copy-start.1 = (bf16[512,256]{1,0:T(8,128)(2,1)S(1)}, bf16[512,256]{1,0:T(8,128)(2,1)}, u32[]{:S(2)}) copy-start(bf16[512,256]{1,0:T(8,128)(2,1)} %constant.13.table_ref) | copy-start | bytes 786436
  22.6 8.6 %collective-permute-start.5 = (bf16[1,128,768]{2,1,0:T(8,128)(2,1)S(1)}, bf16[1,128,768]{2,1,0:T(8,128)(2,1)S(1)}, u32[]{:S(2)}, u32[]{:S(2)}) collective-permute-start(bf16[1,128,768]{2,1,0:T(8,128)(2,1)S(1)} %get-tuple-element.22), channel_id=1, source_target_pairs={{0,4},{8,12},{4,0},{12,8},{1,5},{9,13},{5,1},{13,9},{2,6},{10,14},... | collective-permute-start | bytes 589832 | tf_op jit(solution)/shard_map/ppermute | solution.py:390
  26.8 1.9 %copy-start.3 = (s32[2,2,2,2]{3,2,1,0:T(2,128)S(1)}, s32[2,2,2,2]{3,2,1,0:T(2,128)}, u32[]{:S(2)}) copy-start(s32[2,2,2,2]{3,2,1,0:T(2,128)} %far_prior_ref.3) | copy-start | bytes 196
  26.8 1.9 %copy-start.4 = (s32[8]{0:T(128)S(1)}, s32[8]{0:T(128)}, u32[]{:S(2)}) copy-start(s32[8]{0:T(128)} %far_order_ref.3) | copy-start | bytes 100
  26.8 1.9 %copy-start.5 = (f32[4,256,128]{2,1,0:T(8,128)S(1)}, f32[4,256,128]{2,1,0:T(8,128)}, u32[]{:S(2)}) copy-start(f32[4,256,128]{2,1,0:T(8,128)} %constant.16.lag_ref) | copy-start | bytes 1572868
  26.8 4.4 %collective-permute-start.6 = (bf16[1,128,768]{2,1,0:T(8,128)(2,1)S(1)}, bf16[1,128,768]{2,1,0:T(8,128)(2,1)S(1)}, u32[]{:S(2)}, u32[]{:S(2)}) collective-permute-start(bf16[1,128,768]{2,1,0:T(8,128)(2,1)S(1)} %get-tuple-element.23), channel_id=1, source_target_pairs={{4,8},{8,4},{5,9},{9,5},{6,10},{10,6},{7,11},{11,7},{20,24},{24,20... | collective-permute-start | bytes 589832 | tf_op jit(solution)/shard_map/ppermute | solution.py:390

commit v7 on v6

--- a/solution.py
+++ b/solution.py
@@ -278,18 +278,10 @@
     column_pass(table_ref, middle_ref.at[section], rows_ref, spec_ref, part_ref)
 
 
-def first_kernel(
-    table_ref, turned_ref, middle_ref, row_inner_ref, row_outer_ref, corner_inner_ref, corner_outer_ref,
-    part_ref, ext_ref, rows_ref, spec_ref, *, section,
-):
-    row_refs = (row_inner_ref, row_outer_ref, corner_inner_ref, corner_outer_ref)
-    own_parts(table_ref, turned_ref, middle_ref, row_refs, section, part_ref, ext_ref, rows_ref, spec_ref)
-
-
-def next_kernel(
+def own_kernel(
     far_prior_ref, far_order_ref, table_ref, turned_ref, middle_ref, row_inner_ref, row_outer_ref,
-    corner_inner_ref, corner_outer_ref, lag_ref, flow_in_ref, before_ref, part_ref, flow_ref,
-    ext_ref, rows_ref, spec_ref, cross_ref, prior_ref, order_ref, sems, *, section, sizes,
+    corner_inner_ref, corner_outer_ref, lag_ref, part_ref, flow_ref,
+    ext_ref, rows_ref, spec_ref, before_ref, cross_ref, prior_ref, order_ref, sems, *, sizes,
 ):
     row_refs = (row_inner_ref, row_outer_ref, corner_inner_ref, corner_outer_ref)
     copies = (
@@ -298,12 +290,21 @@
     )
     for copy in copies:
         copy.start()
-    own_parts(table_ref, turned_ref, middle_ref, row_refs, section, part_ref, ext_ref, rows_ref, spec_ref)
-    for copy in copies:
-        copy.wait()
-    flow_ref[...] = flow_in_ref[...] + placed_flows(
-        prior_ref, order_ref, lag_ref, cross_ref, before_ref, part_ref, section - 1, flow_ref.shape, sizes
-    )
+    sec_count = middle_ref.shape[0]
+    flow = jnp.zeros(flow_ref.shape, jnp.float32)
+    for section in range(sec_count):
+        here = part_ref if section == sec_count - 1 else before_ref.at[section]
+        own_parts(
+            table_ref, turned_ref, middle_ref, row_refs, section, here, ext_ref.at[section], rows_ref.at[section], spec_ref,
+        )
+        if section == min(1, sec_count - 1):
+            for copy in copies:
+                copy.wait()
+        if section > 0:
+            flow += placed_flows(
+                prior_ref, order_ref, lag_ref, cross_ref, before_ref.at[section - 1], here, section - 1, flow.shape, sizes
+            )
+    flow_ref[...] = flow
 
 
 def last_kernel(
@@ -415,7 +416,6 @@
     def cost(flops):
         return pl.CostEstimate(flops=flops, bytes_accessed=place_count * PATCH * PATCH * 4, transcendentals=0)
 
-    flow = jnp.zeros((size_row, lanes), jnp.float32)
     rows_call = pl.pallas_call(
         rows_kernel,
         out_shape=pixels(sec_count, per_side, side, PATCH),
@@ -428,29 +428,24 @@
     )
     own_middle = rows_call(turned, own, *own_cols)
     pieces = (own_middle, *own_rows, *own_corners)
-    first_call = pl.pallas_call(
-        functools.partial(first_kernel, section=0),
-        out_shape=part_shape,
-        in_specs=[vmem] * 7,
-        out_specs=vmem,
-        scratch_shapes=[edge_ext_scratch, edge_rows_scratch, spec_scratch],
+    own_call = pl.pallas_call(
+        functools.partial(own_kernel, sizes=sizes),
+        out_shape=(part_shape, flow_shape),
+        in_specs=[far] * 2 + [vmem] * 8,
+        out_specs=(vmem, vmem),
+        scratch_shapes=[
+            pltpu.VMEM((sec_count, HALO, wide), jnp.bfloat16),
+            pltpu.VMEM((sec_count, per_side, HALO, PATCH), jnp.bfloat16),
+            spec_scratch,
+            pltpu.VMEM((max(1, sec_count - 1),) + parts, jnp.float32),
+            cross_scratch,
+            *scalars,
+        ],
         compiler_params=params,
-        cost_estimate=cost(spectra_cost),
-        name="first",
-    )
-    part = first_call(table, turned, *pieces)
-    for section in range(1, sec_count):
-        next_call = pl.pallas_call(
-            functools.partial(next_kernel, section=section, sizes=sizes),
-            out_shape=(part_shape, flow_shape),
-            in_specs=[far] * 2 + [vmem] * 10,
-            out_specs=(vmem, vmem),
-            scratch_shapes=[edge_ext_scratch, edge_rows_scratch, spec_scratch, cross_scratch, *scalars],
-            compiler_params=params,
-            cost_estimate=cost(spectra_cost + pair_cost),
-            name="next",
-        )
-        part, flow = next_call(priors, row_order, table, turned, *pieces, lag_table, flow, part)
+        cost_estimate=cost(sec_count * (spectra_cost + pair_cost)),
+        name="own",
+    )
+    part, flow = own_call(priors, row_order, table, turned, *pieces, lag_table)
     last_rows_call = pl.pallas_call(
         last_rows_kernel,
         out_shape=pixels(per_side, side, PATCH),

time: 48.3 us -> 48.2 us (level)
    pallas_call x2 -> x1, Pallas kernels: 3.5 us -> 3.39 us  [match(): part, flow = own_call(priors, row_order, table, turned, *pieces, lag_table)]
where the time goes in v7:
time: 48.2 us; the launch traced here: 47.9 us
  starting transfers between devices  17.2 us (36%)
  blocking collectives  13.8 us (29%)
  Pallas kernels  7.52 us (16%)
  waiting for transfers between devices  7.28 us (15%)
  local copies, waits for them, and re-layouts  1.9 us (4%)
    all_to_all x1, blocking collectives, match(): received = lax.all_to_all(sent, AXES, 0, 0, tiled=True)  13.8 us
    ppermute x1, starting transfers between devices, match(): lax.ppermute(first_inner, 'col', col_inner)  4.1 us
    ppermute x1, waiting for transfers between devices, match(): first_inner = lax.ppermute(cuts[4], 'gz', gz_pairs)  3.66 us
    pallas_call x1, Pallas kernels, match(): part, flow = own_call(priors, row_order, table, turned, *pieces, lag_table)  3.39 us
    ppermute x1, starting transfers between devices, match(): lax.ppermute(cuts[0], 'col', col_inner)  3.12 us
    ppermute x2, starting transfers between devices, edges(): lax.ppermute(inner, 'row', row_inner)  2.94 us
    pallas_call x1, Pallas kernels, match(): pl.pallas_call(functools.partial(last_kernel, sizes=sizes), out_shape=jax...  2.45 us
    ppermute x1, waiting for transfers between devices, match(): lax.ppermute(first_inner, 'col', col_inner)  2.2 us
  transfers between devices with their start and end apart: 13, of which 3 were waited for; matrix products, arithmetic and copies ran while one was open for 0% of the time, Pallas kernels for 10%

profile of v7, /device:TPU:0, one launch (start us, length us, event | category | flops | bytes accessed | tf_op | source)
XLA Modules:
  0.0 47.9 jit_solution(3375833655508296878)
XLA Ops:
  0.0 1.2 %copy-done.1 = bf16[2,512,512]{2,1,0:T(8,128)(2,1)S(1)} copy-done((bf16[2,512,512]{2,1,0:T(8,128)(2,1)S(1)}, bf16[2,512,512]{2,1,0:T(8,128)(2,1)}, u32[]{:S(2)}) %copy-start.1) | copy-done | bytes 1048600
  1.2 0.3 cut.1
  1.5 3.1 %collective-permute-start.7 = (bf16[2,512,128]{2,1,0:T(8,128)(2,1)S(1)}, bf16[2,512,128]{2,1,0:T(8,128)(2,1)S(1)}, u32[]{:S(2)}, u32[]{:S(2)}) collective-permute-start(bf16[2,512,128]{2,1,0:T(8,128)(2,1)S(1)} %get-tuple-element.25), channel_id=1, source_target_pairs={{0,1},{2,3},{1,0},{3,2},{4,5},{6,7},{5,4},{7,6},{8,9},{10,11},{9,8... | collective-permute-start | bytes 786440 | tf_op jit(solution)/shard_map/ppermute | solution.py:374
  4.6 0.7 %collective-permute-start.8 = (bf16[2,512,128]{2,1,0:T(8,128)(2,1)S(1)}, bf16[2,512,128]{2,1,0:T(8,128)(2,1)S(1)}, u32[]{:S(2)}, u32[]{:S(2)}) collective-permute-start(bf16[2,512,128]{2,1,0:T(8,128)(2,1)S(1)} %get-tuple-element.26), channel_id=1, source_target_pairs={{1,2},{2,1},{5,6},{6,5},{9,10},{10,9},{13,14},{14,13},{17,18},{18,... | collective-permute-start | bytes 786440 | tf_op jit(solution)/shard_map/ppermute | solution.py:374
  5.3 1.6 %collective-permute-start.1 = (bf16[1,512,128]{2,1,0:T(8,128)(2,1)S(1)}, bf16[1,512,128]{2,1,0:T(8,128)(2,1)S(1)}, u32[]{:S(2)}, u32[]{:S(2)}) collective-permute-start(bf16[1,512,128]{2,1,0:T(8,128)(2,1)S(1)} %get-tuple-element.20), channel_id=1, source_target_pairs={{0,16},{16,0},{1,17},{17,1},{2,18},{18,2},{3,19},{19,3},{4,20},{20... | collective-permute-start | bytes 393224 | tf_op jit(solution)/shard_map/ppermute | solution.py:376
  6.8 0.5 %collective-permute-start.2 = (bf16[1,512,128]{2,1,0:T(8,128)(2,1)S(1)}, bf16[1,512,128]{2,1,0:T(8,128)(2,1)S(1)}, u32[]{:S(2)}, u32[]{:S(2)}) collective-permute-start(bf16[1,512,128]{2,1,0:T(8,128)(2,1)S(1)} %get-tuple-element.21), channel_id=1, source_target_pairs={{0,16},{16,0},{1,17},{17,1},{2,18},{18,2},{3,19},{19,3},{4,20},{20... | collective-permute-start | bytes 393224 | tf_op jit(solution)/shard_map/ppermute | solution.py:377
  7.4 0.7 %collective-permute-start.10 = (bf16[2,128,512]{2,1,0:T(8,128)(2,1)S(1)}, bf16[2,128,512]{2,1,0:T(8,128)(2,1)S(1)}, u32[]{:S(2)}, u32[]{:S(2)}) collective-permute-start(bf16[2,128,512]{2,1,0:T(8,128)(2,1)S(1)} %get-tuple-element.28), channel_id=1, source_target_pairs={{4,8},{8,4},{5,9},{9,5},{6,10},{10,6},{7,11},{11,7},{20,24},{24,20... | collective-permute-start | bytes 786440 | tf_op jit(solution)/shard_map/ppermute | solution.py:375
  8.1 3.7 %collective-permute-done.1.first_inner_ref.refs_1_ = bf16[1,512,128]{2,1,0:T(8,128)(2,1)S(1)} collective-permute-done((bf16[1,512,128]{2,1,0:T(8,128)(2,1)S(1)}, bf16[1,512,128]{2,1,0:T(8,128)(2,1)S(1)}, u32[]{:S(2)}, u32[]{:S(2)}) %collective-permute-start.1) | collective-permute-done | bytes 131104 | tf_op jit(solution)/shard_map/ppermute | solution.py:376
  11.7 1.4 %collective-permute-done.2.first_outer_ref.refs_2_ = bf16[1,512,128]{2,1,0:T(8,128)(2,1)S(1)} collective-permute-done((bf16[1,512,128]{2,1,0:T(8,128)(2,1)S(1)}, bf16[1,512,128]{2,1,0:T(8,128)(2,1)S(1)}, u32[]{:S(2)}, u32[]{:S(2)}) %collective-permute-start.2) | collective-permute-done | bytes 131104 | tf_op jit(solution)/shard_map/ppermute | solution.py:377
  13.1 1.5 %collective-permute-start = (bf16[1,512,256]{2,1,0:T(8,128)(2,1)S(1)}, bf16[1,512,256]{2,1,0:T(8,128)(2,1)S(1)}, u32[]{:S(2)}, u32[]{:S(2)}) collective-permute-start(bf16[1,512,256]{2,1,0:T(8,128)(2,1)S(1)} %get-tuple-element.19), channel_id=1, source_target_pairs={{0,16},{16,0},{1,17},{17,1},{2,18},{18,2},{3,19},{19,3},{4,20},{20... | collective-permute-start | bytes 786440 | tf_op jit(solution)/shard_map/ppermute | solution.py:378
  14.6 0.0 collective-permute-done.7.col_inner_ref.refs_0_
  14.6 4.1 %collective-permute-start.3 = (bf16[1,512,128]{2,1,0:T(8,128)(2,1)S(1)}, bf16[1,512,128]{2,1,0:T(8,128)(2,1)S(1)}, u32[]{:S(2)}, u32[]{:S(2)}) collective-permute-start(bf16[1,512,128]{2,1,0:T(8,128)(2,1)S(1)} %collective-permute-done.1.first_inner_ref.refs_1_), channel_id=1, source_target_pairs={{0,1},{2,3},{1,0},{3,2},{4,5},{6,7},{5,4},{7,6},{8,9},{10,11},{9,8... | collective-permute-start | bytes 393224 | tf_op jit(solution)/shard_map/ppermute | solution.py:379
  18.7 0.0 collective-permute-done.8.col_outer_ref.refs_1_
  18.7 0.7 %collective-permute-start.4 = (bf16[1,512,128]{2,1,0:T(8,128)(2,1)S(1)}, bf16[1,512,128]{2,1,0:T(8,128)(2,1)S(1)}, u32[]{:S(2)}, u32[]{:S(2)}) collective-permute-start(bf16[1,512,128]{2,1,0:T(8,128)(2,1)S(1)} %collective-permute-done.2.first_outer_ref.refs_2_), channel_id=1, source_target_pairs={{1,2},{2,1},{5,6},{6,5},{9,10},{10,9},{13,14},{14,13},{17,18},{18,... | collective-permute-start | bytes 393224 | tf_op jit(solution)/shard_map/ppermute | solution.py:379
  19.4 0.1 shard_map.65
  19.5 2.2 %collective-permute-done.3.col_inner_ref.refs_3_ = bf16[1,512,128]{2,1,0:T(8,128)(2,1)S(1)} collective-permute-done((bf16[1,512,128]{2,1,0:T(8,128)(2,1)S(1)}, bf16[1,512,128]{2,1,0:T(8,128)(2,1)S(1)}, u32[]{:S(2)}, u32[]{:S(2)}) %collective-permute-start.3) | collective-permute-done | bytes 131104 | tf_op jit(solution)/shard_map/ppermute | solution.py:379
  21.7 0.0 collective-permute-start.11
  21.7 0.8 %collective-permute-start.12 = (bf16[2,128,256]{2,1,0:T(8,128)(2,1)S(1)}, bf16[2,128,256]{2,1,0:T(8,128)(2,1)S(1)}, u32[]{:S(2)}, u32[]{:S(2)}) collective-permute-start(bf16[2,128,256]{2,1,0:T(8,128)(2,1)S(1)} %get-tuple-element.30), channel_id=1, source_target_pairs={{4,8},{8,4},{5,9},{9,5},{6,10},{10,6},{7,11},{11,7},{20,24},{24,20... | collective-permute-start | bytes 393224 | tf_op jit(solution)/shard_map/ppermute | solution.py:391
  22.5 0.1 shard_map.64
  22.6 0.0 copy-start.2
  22.6 0.0 copy-start.3
  22.6 0.0 copy-start.4
  22.6 0.0 copy-start.5
  22.7 2.9 %collective-permute-start.5 = (bf16[1,128,768]{2,1,0:T(8,128)(2,1)S(1)}, bf16[1,128,768]{2,1,0:T(8,128)(2,1)S(1)}, u32[]{:S(2)}, u32[]{:S(2)}) collective-permute-start(bf16[1,128,768]{2,1,0:T(8,128)(2,1)S(1)} %get-tuple-element.22), channel_id=1, source_target_pairs={{0,4},{8,12},{4,0},{12,8},{1,5},{9,13},{5,1},{13,9},{2,6},{10,14},... | collective-permute-start | bytes 589832 | tf_op jit(solution)/shard_map/ppermute | solution.py:391
  25.6 0.5 last_middle.1.middle_ref
  26.1 0.8 %rows.1.middle_ref = bf16[2,2,512,512]{3,2,1,0:T(8,128)(2,1)S(1)} custom-call(bf16[256,512]{1,0:T(8,128)(2,1)S(1)} %copy-done, bf16[2,512,512]{2,1,0:T(8,128)(2,1)S(1)} %get-tuple-element.24.own_ref, bf16[2,512,128]{2,1,0:T(8,128)(2,1)S(1)} %collective-permute-done.7.col_inner_ref.refs_0_, bf16[2,512,128]{2,1,0:T(8,128)(2,1)S(1)} %collective-permute-done.8.col_outer_ref.refs_1_), custom_call_target="tpu_custom_call" | custom-call | flops 536870912 | bytes 4194304 | tf_op jit(solution)/shard_map/rows/pallas_call | solution.py:429
  26.9 0.7 %collective-permute-start.6 = (bf16[1,128,768]{2,1,0:T(8,128)(2,1)S(1)}, bf16[1,128,768]{2,1,0:T(8,128)(2,1)S(1)}, u32[]{:S(2)}, u32[]{:S(2)}) collective-permute-start(bf16[1,128,768]{2,1,0:T(8,128)(2,1)S(1)} %get-tuple-element.23), channel_id=1, source_target_pairs={{4,8},{8,4},{5,9},{9,5},{6,10},{10,6},{7,11},{11,7},{20,24},{24,20... | collective-permute-start | bytes 589832 | tf_op jit(solution)/shard_map/ppermute | solution.py:391
  27.6 3.4 %own.1 = (f32[4,512,512]{2,1,0:T(8,128)S(1)}, f32[4,128]{1,0:T(4,128)S(1)}) custom-call(s32[2,2,2,2]{3,2,1,0:T(2,128)S(1)} %copy-done.2, s32[8]{0:T(128)S(1)} %copy-done.3, bf16[512,256]{1,0:T(8,128)(2,1)S(1)} %copy-done.5, bf16[256,512]{1,0:T(8,128)(2,1)S(1)} %copy-done, bf16[2,2,512,512]{3,2,1,0:T(8,128)(2,1)S(1)} %rows.1.middle_ref, ...), custom_call_target="tpu_custom_call" | custom-call | flops 4429185024 | bytes 4194304 | tf_op jit(solution)/shard_map/own/pallas_call | solution.py:448
  31.0 2.5 %last.1 = f32[32,128]{1,0:T(8,128)S(1)} custom-call(s32[2,2,2,2]{3,2,1,0:T(2,128)S(1)} %copy-done.2, s32[8]{0:T(128)S(1)} %copy-done.3, bf16[512,256]{1,0:T(8,128)(2,1)S(1)} %copy-done.5, bf16[256,512]{1,0:T(8,128)(2,1)S(1)} %copy-done, f32[4,256,128]{2,1,0:T(8,128)S(1)} %copy-done.4, bf16[2,512,512]{2,1,0:T(8,128)(2,1)S(1)} %last_middle.1.middle_ref, ...), custom_call_target="tpu_custom_call" | custom-call | flops 2214592512 | bytes 4194304 | tf_op jit(solution)/shard_map/last/pallas_call | solution.py:460
  33.5 13.8 %all_to_all.9 = f32[32,1,128]{2,1,0:T(1,128)S(1)} all-to-all(f32[32,1,128]{2,1,0:T(1,128)S(1)} %bitcast.3), channel_id=1, replica_groups=mesh['gz'=2,'row'=4,'col'=4] {'gz','row','col'}, dimensions={0} | all-to-all | bytes 32768 | tf_op jit(solution)/shard_map/all_to_all | solution.py:470
  47.2 0.1 reduce_sum.9
  47.3 0.6 %reshape.5 = f32[2,64]{1,0:T(2,128)} reshape(f32[128]{0:T(128)S(1)} %reduce_sum.9) | data formatting | bytes 1024 | tf_op jit(solution)/shard_map/reshape | solution.py:471
  (16 shorter events, 0.0 us)
Async XLA Ops:
  0.0 1.2 %copy-start.1 = (bf16[2,512,512]{2,1,0:T(8,128)(2,1)S(1)}, bf16[2,512,512]{2,1,0:T(8,128)(2,1)}, u32[]{:S(2)}) copy-start(bf16[2,512,512]{2,1,0:T(8,128)(2,1)} %far_ref.1) | copy-start | bytes 3145732
  1.5 13.1 %collective-permute-start.7 = (bf16[2,512,128]{2,1,0:T(8,128)(2,1)S(1)}, bf16[2,512,128]{2,1,0:T(8,128)(2,1)S(1)}, u32[]{:S(2)}, u32[]{:S(2)}) collective-permute-start(bf16[2,512,128]{2,1,0:T(8,128)(2,1)S(1)} %get-tuple-element.25), channel_id=1, source_target_pairs={{0,1},{2,3},{1,0},{3,2},{4,5},{6,7},{5,4},{7,6},{8,9},{10,11},{9,8... | collective-permute-start | bytes 786440 | tf_op jit(solution)/shard_map/ppermute | solution.py:374
  4.6 14.1 %collective-permute-start.8 = (bf16[2,512,128]{2,1,0:T(8,128)(2,1)S(1)}, bf16[2,512,128]{2,1,0:T(8,128)(2,1)S(1)}, u32[]{:S(2)}, u32[]{:S(2)}) collective-permute-start(bf16[2,512,128]{2,1,0:T(8,128)(2,1)S(1)} %get-tuple-element.26), channel_id=1, source_target_pairs={{1,2},{2,1},{5,6},{6,5},{9,10},{10,9},{13,14},{14,13},{17,18},{18,... | collective-permute-start | bytes 786440 | tf_op jit(solution)/shard_map/ppermute | solution.py:374
  5.3 6.4 %collective-permute-start.1 = (bf16[1,512,128]{2,1,0:T(8,128)(2,1)S(1)}, bf16[1,512,128]{2,1,0:T(8,128)(2,1)S(1)}, u32[]{:S(2)}, u32[]{:S(2)}) collective-permute-start(bf16[1,512,128]{2,1,0:T(8,128)(2,1)S(1)} %get-tuple-element.20), channel_id=1, source_target_pairs={{0,16},{16,0},{1,17},{17,1},{2,18},{18,2},{3,19},{19,3},{4,20},{20... | collective-permute-start | bytes 393224 | tf_op jit(solution)/shard_map/ppermute | solution.py:376
  6.8 6.3 %collective-permute-start.2 = (bf16[1,512,128]{2,1,0:T(8,128)(2,1)S(1)}, bf16[1,512,128]{2,1,0:T(8,128)(2,1)S(1)}, u32[]{:S(2)}, u32[]{:S(2)}) collective-permute-start(bf16[1,512,128]{2,1,0:T(8,128)(2,1)S(1)} %get-tuple-element.21), channel_id=1, source_target_pairs={{0,16},{16,0},{1,17},{17,1},{2,18},{18,2},{3,19},{19,3},{4,20},{20... | collective-permute-start | bytes 393224 | tf_op jit(solution)/shard_map/ppermute | solution.py:377
  7.4 19.5 %collective-permute-start.10 = (bf16[2,128,512]{2,1,0:T(8,128)(2,1)S(1)}, bf16[2,128,512]{2,1,0:T(8,128)(2,1)S(1)}, u32[]{:S(2)}, u32[]{:S(2)}) collective-permute-start(bf16[2,128,512]{2,1,0:T(8,128)(2,1)S(1)} %get-tuple-element.28), channel_id=1, source_target_pairs={{4,8},{8,4},{5,9},{9,5},{6,10},{10,6},{7,11},{11,7},{20,24},{24,20... | collective-permute-start | bytes 786440 | tf_op jit(solution)/shard_map/ppermute | solution.py:375
  11.7 15.8 %collective-permute-start.9 = (bf16[2,128,512]{2,1,0:T(8,128)(2,1)S(1)}, bf16[2,128,512]{2,1,0:T(8,128)(2,1)S(1)}, u32[]{:S(2)}, u32[]{:S(2)}) collective-permute-start(bf16[2,128,512]{2,1,0:T(8,128)(2,1)S(1)} %get-tuple-element.27), channel_id=1, source_target_pairs={{0,4},{8,12},{4,0},{12,8},{1,5},{9,13},{5,1},{13,9},{2,6},{10,14},... | collective-permute-start | bytes 786440 | tf_op jit(solution)/shard_map/ppermute | solution.py:375
  13.1 9.4 %collective-permute-start = (bf16[1,512,256]{2,1,0:T(8,128)(2,1)S(1)}, bf16[1,512,256]{2,1,0:T(8,128)(2,1)S(1)}, u32[]{:S(2)}, u32[]{:S(2)}) collective-permute-start(bf16[1,512,256]{2,1,0:T(8,128)(2,1)S(1)} %get-tuple-element.19), channel_id=1, source_target_pairs={{0,16},{16,0},{1,17},{17,1},{2,18},{18,2},{3,19},{19,3},{4,20},{20... | collective-permute-start | bytes 786440 | tf_op jit(solution)/shard_map/ppermute | solution.py:378
  14.6 7.0 %collective-permute-start.3 = (bf16[1,512,128]{2,1,0:T(8,128)(2,1)S(1)}, bf16[1,512,128]{2,1,0:T(8,128)(2,1)S(1)}, u32[]{:S(2)}, u32[]{:S(2)}) collective-permute-start(bf16[1,512,128]{2,1,0:T(8,128)(2,1)S(1)} %collective-permute-done.1.first_inner_ref.refs_1_), channel_id=1, source_target_pairs={{0,1},{2,3},{1,0},{3,2},{4,5},{6,7},{5,4},{7,6},{8,9},{10,11},{9,8... | collective-permute-start | bytes 393224 | tf_op jit(solution)/shard_map/ppermute | solution.py:379
  18.7 2.9 %collective-permute-start.4 = (bf16[1,512,128]{2,1,0:T(8,128)(2,1)S(1)}, bf16[1,512,128]{2,1,0:T(8,128)(2,1)S(1)}, u32[]{:S(2)}, u32[]{:S(2)}) collective-permute-start(bf16[1,512,128]{2,1,0:T(8,128)(2,1)S(1)} %collective-permute-done.2.first_outer_ref.refs_2_), channel_id=1, source_target_pairs={{1,2},{2,1},{5,6},{6,5},{9,10},{10,9},{13,14},{14,13},{17,18},{18,... | collective-permute-start | bytes 393224 | tf_op jit(solution)/shard_map/ppermute | solution.py:379
  21.7 5.9 %collective-permute-start.11 = (bf16[2,128,256]{2,1,0:T(8,128)(2,1)S(1)}, bf16[2,128,256]{2,1,0:T(8,128)(2,1)S(1)}, u32[]{:S(2)}, u32[]{:S(2)}) collective-permute-start(bf16[2,128,256]{2,1,0:T(8,128)(2,1)S(1)} %get-tuple-element.29), channel_id=1, source_target_pairs={{0,4},{8,12},{4,0},{12,8},{1,5},{9,13},{5,1},{13,9},{2,6},{10,14},... | collective-permute-start | bytes 393224 | tf_op jit(solution)/shard_map/ppermute | solution.py:391
  21.7 3.9 %copy-start = (bf16[256,512]{1,0:T(8,128)(2,1)S(1)}, bf16[256,512]{1,0:T(8,128)(2,1)}, u32[]{:S(2)}) copy-start(bf16[256,512]{1,0:T(8,128)(2,1)} %constant.13.turned_ref) | copy-start | bytes 786436
  21.7 5.9 %collective-permute-start.12 = (bf16[2,128,256]{2,1,0:T(8,128)(2,1)S(1)}, bf16[2,128,256]{2,1,0:T(8,128)(2,1)S(1)}, u32[]{:S(2)}, u32[]{:S(2)}) collective-permute-start(bf16[2,128,256]{2,1,0:T(8,128)(2,1)S(1)} %get-tuple-element.30), channel_id=1, source_target_pairs={{4,8},{8,4},{5,9},{9,5},{6,10},{10,6},{7,11},{11,7},{20,24},{24,20... | collective-permute-start | bytes 393224 | tf_op jit(solution)/shard_map/ppermute | solution.py:391
  22.6 5.0 %copy-start.2 = (s32[2,2,2,2]{3,2,1,0:T(2,128)S(1)}, s32[2,2,2,2]{3,2,1,0:T(2,128)}, u32[]{:S(2)}) copy-start(s32[2,2,2,2]{3,2,1,0:T(2,128)} %far_prior_ref.3) | copy-start | bytes 196
  22.6 5.0 %copy-start.3 = (s32[8]{0:T(128)S(1)}, s32[8]{0:T(128)}, u32[]{:S(2)}) copy-start(s32[8]{0:T(128)} %far_order_ref.3) | copy-start | bytes 100
  22.6 5.0 %copy-start.4 = (f32[4,256,128]{2,1,0:T(8,128)S(1)}, f32[4,256,128]{2,1,0:T(8,128)}, u32[]{:S(2)}) copy-start(f32[4,256,128]{2,1,0:T(8,128)} %constant.15.lag_ref) | copy-start | bytes 1572868
  22.6 5.0 %copy-start.5 = (bf16[512,256]{1,0:T(8,128)(2,1)S(1)}, bf16[512,256]{1,0:T(8,128)(2,1)}, u32[]{:S(2)}) copy-start(bf16[512,256]{1,0:T(8,128)(2,1)} %constant.12.table_ref) | copy-start | bytes 786436
  22.7 8.4 %collective-permute-start.5 = (bf16[1,128,768]{2,1,0:T(8,128)(2,1)S(1)}, bf16[1,128,768]{2,1,0:T(8,128)(2,1)S(1)}, u32[]{:S(2)}, u32[]{:S(2)}) collective-permute-start(bf16[1,128,768]{2,1,0:T(8,128)(2,1)S(1)} %get-tuple-element.22), channel_id=1, source_target_pairs={{0,4},{8,12},{4,0},{12,8},{1,5},{9,13},{5,1},{13,9},{2,6},{10,14},... | collective-permute-start | bytes 589832 | tf_op jit(solution)/shard_map/ppermute | solution.py:391
  26.9 4.2 %collective-permute-start.6 = (bf16[1,128,768]{2,1,0:T(8,128)(2,1)S(1)}, bf16[1,128,768]{2,1,0:T(8,128)(2,1)S(1)}, u32[]{:S(2)}, u32[]{:S(2)}) collective-permute-start(bf16[1,128,768]{2,1,0:T(8,128)(2,1)S(1)} %get-tuple-element.23), channel_id=1, source_target_pairs={{4,8},{8,4},{5,9},{9,5},{6,10},{10,6},{7,11},{11,7},{20,24},{24,20... | collective-permute-start | bytes 589832 | tf_op jit(solution)/shard_map/ppermute | solution.py:391
